TPU v7x, 128 devices: a whole 4x4x4 slice. The times are simulated.
128 devices in a mesh: ep: 8 (over x, core), tp: 16 (over z, y).
Axes of the slice: x: 4, y: 4, z: 4, core: 2. Of those that a mesh axis runs over, the one named last changes fastest.
Arguments:
- layer_input: bfloat16 [2048, 4096], P('ep', 'tp'), may hold values from -6 to 6
- out_grad: bfloat16 [2048, 4096], P('ep', 'tp'), may hold values from -6 to 6
- route: int32 [2048, 2], P('ep'), may hold values from 0 to 7, all different within a row; in each aligned block of 256 rows (0 to 255, 256 to 511, ...) at most 96 rows name the same one
- gate_share: float32 [2048, 2], P('ep'), may hold values from 0.2 to 1
- gate_weight: bfloat16 [8, 4096, 14336], P('ep', None, 'tp'), may hold values from -0.125 to 0.125
- up_weight: bfloat16 [8, 4096, 14336], P('ep', None, 'tp'), may hold values from -0.125 to 0.125
- down_weight: bfloat16 [8, 14336, 4096], P('ep', 'tp'), may hold values from -0.046875 to 0.046875
Outputs:
- input_grad: bfloat16 [2048, 4096], P('ep', 'tp')
Inputs may be any that keep to these rules, and one draw needn't show every extreme that they name: `route`: each row names 2 different experts. In each aligned block of 256 rows (the rows of one index of ep) no expert is named by more than 96 rows, a bound that some block reaches.
All inputs are finite; a program needn't handle non-finite values.
Results may differ from a plain program's by a relative error of at most 0.0057.
Values may be sent and summed in bfloat16 or wider, within the bound.
No kernel may reach another device: no remote copies, remote signals or barrier semaphores. Data moves between devices by JAX's collectives and lax.ppermute only.
A program may use at most 320 MiB of HBM per device.

v0:
```python
import functools

import jax
import jax.numpy as jnp
from jax import lax
from jax.experimental import pallas as pl
from jax.experimental.pallas import tpu as pltpu
from jax.sharding import PartitionSpec as P


BF = jnp.bfloat16
F32 = jnp.float32
SIDE = 4
TP = SIDE * SIDE
COLS_BY_COLS = (((0,), (0,)), ((), ()))


def flat_slots(routes, experts, capacity):
    tokens = routes.shape[1]
    first, second = routes[0:1, :], routes[1:2, :]
    expert = lax.broadcasted_iota(jnp.int32, (experts, tokens), 0)
    in_first, in_second = expert == first, expert == second
    named = jnp.where(in_first | in_second, 1.0, 0.0).astype(BF)
    earlier = lax.broadcasted_iota(jnp.int32, (tokens, tokens), 0)
    later = lax.broadcasted_iota(jnp.int32, (tokens, tokens), 1)
    before = jnp.dot(named, jnp.where(earlier < later, 1.0, 0.0).astype(BF), preferred_element_type=F32)
    place_first = jnp.sum(jnp.where(in_first, before, 0.0), axis=0, keepdims=True)
    place_second = jnp.sum(jnp.where(in_second, before, 0.0), axis=0, keepdims=True)
    return (
        first * capacity + place_first.astype(jnp.int32),
        second * capacity + place_second.astype(jnp.int32),
    )


def dispatch_body(routes, inputs, grads, out):
    experts, both, _ = out.shape
    capacity = both // 2
    tokens = inputs.shape[0]
    first, second = flat_slots(routes[...], experts, capacity)
    slot = lax.broadcasted_iota(jnp.int32, (experts * capacity, tokens), 0)
    pick = jnp.where((slot == first) | (slot == second), 1.0, 0.0).astype(BF)
    for at, source in ((0, inputs), (capacity, grads)):
        rows = jnp.dot(pick, source[...], preferred_element_type=F32).astype(BF)
        for e in range(experts):
            out[e, at : at + capacity] = rows[e * capacity : (e + 1) * capacity]


def combine_body(routes, shares, *refs):
    backs, out = refs[:-1], refs[-1]
    experts, part, _ = backs[0].shape
    capacity = part * len(backs)
    tokens = out.shape[0]
    first, second = flat_slots(routes[...], experts, capacity)
    slot = lax.broadcasted_iota(jnp.int32, (experts * capacity, tokens), 0)
    share = jnp.concatenate([shares[...], jnp.zeros((6, tokens), F32)], axis=0).T
    back = jnp.concatenate([ref[e] for e in range(experts) for ref in backs], axis=0)
    one = lax.dot_general(
        jnp.where(slot == first, 1.0, 0.0).astype(BF), back, COLS_BY_COLS, preferred_element_type=F32
    )
    two = lax.dot_general(
        jnp.where(slot == second, 1.0, 0.0).astype(BF), back, COLS_BY_COLS, preferred_element_type=F32
    )
    out[...] = (one * share[:, 0:1] + two * share[:, 1:2]).astype(out.dtype)


def turn_body(gate, up, down, wide, tall):
    units = gate.shape[1]
    wide[0, :units] = gate[...].T
    wide[0, units:] = up[...].T
    tall[0] = down[...].T


def acts_body(order, *refs, first, count):
    gate_out, up_out, rows_by_features = refs[-3:]
    before = refs[-5:-3] if first > 0 else ()
    ins = refs[: -3 - len(before)]
    pieces, (gate, up) = ins[:-2], ins[-2:]
    per_half = len(pieces) // 2
    width = pieces[0].shape[-1]
    unit = gate.shape[-1]

    @pl.when(pl.program_id(0) == 0)
    def _():
        for half in range(2):
            blocks = [p[i] for p in pieces[half * per_half : (half + 1) * per_half] for i in range(p.shape[0])]
            for s in range(count):
                for f in range(SIDE):
                    rows_by_features[half * count + s, :, f * width : (f + 1) * width] = blocks[s * SIDE + f]

    for half in range(2):
        total = None
        for s in range(count):
            named = [order[(half * SIDE + first + s) * SIDE + f] for f in range(SIDE)]
            right = jnp.concatenate([jnp.concatenate([gate[t], up[t]], axis=1) for t in named], axis=0)
            part = jnp.dot(rows_by_features[half * count + s], right, preferred_element_type=F32)
            total = part if total is None else total + part
        blocks = gate_out.shape[0] // 2
        here = slice(half * blocks, (half + 1) * blocks)
        shape = (blocks, gate_out.shape[1], unit)
        gate_sum, up_sum = total[:, :unit].reshape(shape), total[:, unit:].reshape(shape)
        if before:
            gate_sum = gate_sum + before[0][here]
            up_sum = up_sum + before[1][here]
        gate_out[here] = gate_sum
        up_out[here] = up_sum


def expert_body(order, g, tall, gate_act, up_act, *refs):
    members = len(refs) - SIDE - 5
    wide, outs = refs[:members], refs[members:-5]
    left, total, for_gate, for_up, grads = refs[-5:]
    pieces, blocks, part_rows, width = g.shape
    units = total.shape[1]
    step = pl.program_id(0)
    deep = TP // pieces

    @pl.when(step < deep)
    def _():
        for i in range(pieces):
            for b in range(blocks):
                left[b * part_rows : (b + 1) * part_rows, i * width : (i + 1) * width] = g[i, b]
        part = jnp.dot(left[...], tall[...].reshape(pieces * width, units), preferred_element_type=F32)

        @pl.when(step == 0)
        def _():
            total[...] = part

        @pl.when(step != 0)
        def _():
            total[...] += part

        count = gate_act.shape[0] * part_rows
        gate = gate_act[...].reshape(count, units)
        sigma = jax.nn.sigmoid(gate)
        here = pl.ds(pl.multiple_of(step * count, count), count)
        for_gate[here] = up_act[...].reshape(count, units) * (sigma * (1.0 + gate * (1.0 - sigma)))
        for_up[here] = gate * sigma

    @pl.when(step == deep)
    def _():
        grads[:, :units] = (total[...] * for_gate[...]).astype(BF)
        grads[:, units:] = (total[...] * for_up[...]).astype(BF)

    @pl.when(step >= deep)
    def _():
        right = jnp.concatenate([w[0] for w in wide], axis=1)
        part = jnp.dot(grads[...], right, preferred_element_type=F32).astype(BF)
        per_out = SIDE // members
        for at, out in enumerate(outs):

            @pl.when((step - deep) // per_out == at)
            def _():
                for i in range(members):
                    out[i] = part[:, i * width : (i + 1) * width]


def vmem(mebibytes):
    return pltpu.CompilerParams(vmem_limit_bytes=mebibytes << 20)


def in_hbm(*arrays):
    return [pltpu.with_memory_space_constraint(a, pltpu.HBM) for a in arrays]


def z_shift(by):
    return [(z * SIDE + y, (z + by) % SIDE * SIDE + y) for z in range(SIDE) for y in range(SIDE)]


def y_shift(by):
    return [(z * SIDE + y, z * SIDE + (y + by) % SIDE) for z in range(SIDE) for y in range(SIDE)]


def shifted(x, shift, by):
    return lax.ppermute(x, "tp", shift(by))


def ring_gather(x, shift):
    half = x.shape[0] // 2
    below = shifted(x, shift, 1)
    above = shifted(x, shift, 3)
    far_low = shifted(below[:half], shift, 1)
    far_high = shifted(above[half:], shift, 3)
    return [x, below, above, far_low, far_high]


def plane_gather(x, first, second):
    rows, width = x.shape
    line = jnp.concatenate(ring_gather(x, first), axis=0)
    return [piece.reshape(-1, rows, width) for piece in ring_gather(line, second)]


def ring_sum(far, ahead, behind, own, shift):
    total = own.astype(F32)
    for by, part in ((2, far), (1, ahead), (3, behind)):
        total = total + shifted(part.astype(BF), shift, by).astype(F32)
    return total


def body(layer_input, out_grad, route, gate_share, gate_weight, up_weight, down_weight):
    experts = lax.axis_size("ep")
    tokens, width = layer_input.shape
    choose = route.shape[1]
    capacity = tokens * choose * 3 // (2 * experts)
    slots = experts * capacity
    parts = (2 * capacity // 3, capacity // 3)
    gate_matrix, up_matrix, down_matrix = gate_weight[0], up_weight[0], down_weight[0]
    _, units = gate_matrix.shape
    routes, shares = route.T, gate_share.T

    me = lax.axis_index("tp")
    z, y = me // SIDE, me % SIDE
    away = jnp.array([0, SIDE - 1, 1, 2], jnp.int32)
    steps = jnp.arange(SIDE, dtype=jnp.int32)

    def plane(in_z, in_y):
        return ((z + in_z) % SIDE * SIDE + (y + in_y) % SIDE).astype(jnp.int32)

    gathered_order = jnp.stack(
        [plane(away[None, :], away[:, None]), plane(away[:, None], away[None, :])]
    ).reshape(-1)
    summed_order = [plane(steps[:, None], steps[None, :]), plane(steps[None, :], steps[:, None])]

    sent = pl.pallas_call(
        dispatch_body,
        out_shape=jax.ShapeDtypeStruct((experts, 2 * capacity, width), BF),
        name="dispatch",
        compiler_params=vmem(16),
    )(routes, layer_input, out_grad)
    got = lax.all_to_all(sent, "ep", split_axis=0, concat_axis=0, tiled=True)
    all_g = lax.all_gather(got[:, capacity:].reshape(slots, width), "tp", axis=0, tiled=False)
    all_g = all_g.reshape(TP, experts, capacity, width)
    low = got[: experts // 2, :capacity].reshape(slots // 2, width)
    high = got[experts // 2 :, :capacity].reshape(slots // 2, width)
    pieces = plane_gather(low, z_shift, y_shift) + plane_gather(high, y_shift, z_shift)

    wide, tall = pl.pallas_call(
        turn_body,
        grid=(TP,),
        in_specs=[
            pl.BlockSpec((width, units), lambda k: (k, 0)),
            pl.BlockSpec((width, units), lambda k: (k, 0)),
            pl.BlockSpec((units, width), lambda k: (0, k)),
        ],
        out_specs=[
            pl.BlockSpec((1, 2 * units, width), lambda k: (k, 0, 0)),
            pl.BlockSpec((1, width, units), lambda k: (k, 0, 0)),
        ],
        out_shape=[
            jax.ShapeDtypeStruct((TP, 2 * units, width), BF),
            jax.ShapeDtypeStruct((TP, width, units), BF),
        ],
        name="turn",
        compiler_params=vmem(16),
    )(*in_hbm(gate_matrix, up_matrix, down_matrix))

    strip = 128
    acts = []
    per_half = len(pieces) // 2
    for first, count in ((0, SIDE - 1), (SIDE - 1, 1)):
        which = slice(0, 3) if first == 0 else slice(3, 5)
        used = pieces[:per_half][which] + pieces[per_half:][which]
        column = pl.BlockSpec((experts, capacity, strip), lambda n, order: (0, 0, n))
        acts = pl.pallas_call(
            functools.partial(acts_body, first=first, count=count),
            grid_spec=pltpu.PrefetchScalarGridSpec(
                num_scalar_prefetch=1,
                grid=(units // strip,),
                in_specs=[pl.BlockSpec(p.shape, lambda n, order: (0, 0, 0)) for p in used]
                + [pl.BlockSpec((TP, width, strip), lambda n, order: (0, 0, n))] * 2
                + [column] * len(acts),
                out_specs=[column] * 2,
                scratch_shapes=[pltpu.VMEM((2 * count, slots // 2, SIDE * width), BF)],
            ),
            out_shape=[jax.ShapeDtypeStruct((experts, capacity, units), F32)] * 2,
            name="acts",
            compiler_params=vmem(40),
        )(
            gathered_order,
            *in_hbm(*used, gate_matrix.reshape(TP, width, units), up_matrix.reshape(TP, width, units)),
            *acts,
        )

    span = 4
    at_once = 2
    deep, per_out = TP // span, SIDE // at_once
    summed = []
    for h, part in enumerate(parts):
        start = sum(parts[:h]) // part
        rows = experts * part

        def wide_block(i):
            return lambda k, order: (order[jnp.maximum(k - deep, 0) * at_once + i], 0, 0)

        def out_block(at):
            return lambda k, order: (jnp.clip(k - deep - at * per_out, 0, per_out - 1), 0, 0)

        deep_step = lambda k: jnp.minimum(k, deep - 1)
        acts_block = pl.BlockSpec(
            (experts // deep, part, units), lambda k, order, start=start: (deep_step(k), start, 0)
        )
        outs = pl.pallas_call(
            expert_body,
            grid_spec=pltpu.PrefetchScalarGridSpec(
                num_scalar_prefetch=1,
                grid=(deep + SIDE * per_out,),
                in_specs=[
                    pl.BlockSpec(
                        (span, experts, part, width),
                        lambda k, order, start=start: (deep_step(k), 0, start, 0),
                    ),
                    pl.BlockSpec((span, width, units), lambda k, order: (deep_step(k), 0, 0)),
                    acts_block,
                    acts_block,
                ]
                + [pl.BlockSpec((1, 2 * units, width), wide_block(i)) for i in range(at_once)],
                out_specs=[pl.BlockSpec((at_once, rows, width), out_block(at)) for at in range(SIDE)],
                scratch_shapes=[pltpu.VMEM((rows, span * width), BF)]
                + [pltpu.VMEM((rows, units), F32)] * 3
                + [pltpu.VMEM((rows, 2 * units), BF)],
            ),
            out_shape=[jax.ShapeDtypeStruct((SIDE, rows, width), BF)] * SIDE,
            name="expert",
            compiler_params=vmem(40),
        )(
            summed_order[h][jnp.array([2, 1, 3, 0])].reshape(-1),
            *in_hbm(all_g, tall, *acts, *[wide] * at_once),
        )
        first, second = (z_shift, y_shift) if h == 0 else (y_shift, z_shift)
        line = ring_sum(*outs, first)
        mine = ring_sum(line[2], line[1], line[3], line[0], second)
        summed.append(mine.astype(BF).reshape(experts, part, width))
    backs = [
        lax.all_to_all(jnp.concatenate(summed, axis=1), "ep", split_axis=0, concat_axis=0, tiled=True)
    ]

    return pl.pallas_call(
        combine_body,
        out_shape=jax.ShapeDtypeStruct((tokens, width), BF),
        name="combine",
        compiler_params=vmem(16),
    )(routes, shares, *backs)


def solution(mesh):
    return jax.shard_map(
        body,
        mesh=mesh,
        in_specs=(
            P("ep", "tp"),
            P("ep", "tp"),
            P("ep", None),
            P("ep", None),
            P("ep", None, "tp"),
            P("ep", None, "tp"),
            P("ep", "tp", None),
        ),
        out_specs=P("ep", "tp"),
        check_vma=False,
    )
```

profile of v0, /device:TPU:1, one launch (start us, length us, event | category | flops | bytes accessed | tf_op | source)
XLA Modules:
  0.0 260.3 jit_solution(16834272252534983195)
XLA Ops:
  9.6 17.7 %all_to_all.10 = bf16[8,192,256]{2,1,0:T(8,128)(2,1)S(1)} all-to-all(bf16[8,192,256]{2,1,0:T(8,128)(2,1)S(1)} %dispatch.1), channel_id=1, replica_groups=mesh['ep'=8,'tp'=16] {'ep'}, dimensions={0} | all-to-all | bytes 1572864 | tf_op jit(solution)/shard_map/all_to_all | solution.py:229
  28.1 3.8 %collective-permute-start.1 = (bf16[384,256]{1,0:T(8,128)(2,1)S(1)}, bf16[384,256]{1,0:T(8,128)(2,1)S(1)}, u32[]{:S(2)}, u32[]{:S(2)}) collective-permute-start(bf16[384,256]{1,0:T(8,128)(2,1)S(1)} %bitcast.75), channel_id=1, source_target_pairs={{0,12},{1,13},{2,14},{3,15},{4,0},{5,1},{6,2},{7,3},{8,4},{9,5},{1... | collective-permute-start | bytes 589832 | tf_op jit(solution)/shard_map/ppermute | solution.py:174
  32.0 2.7 %collective-permute-start.9 = (bf16[384,256]{1,0:T(8,128)(2,1)S(1)}, bf16[384,256]{1,0:T(8,128)(2,1)S(1)}, u32[]{:S(2)}, u32[]{:S(2)}) collective-permute-start(bf16[384,256]{1,0:T(8,128)(2,1)S(1)} %bitcast.72), channel_id=1, source_target_pairs={{0,3},{1,0},{2,1},{3,2},{4,7},{5,4},{6,5},{7,6},{8,11},{9,8},{10,9... | collective-permute-start | bytes 589832 | tf_op jit(solution)/shard_map/ppermute | solution.py:174
  36.1 2.7 %collective-permute-start.3 = (bf16[192,256]{1,0:T(8,128)(2,1)S(1)}, bf16[192,256]{1,0:T(8,128)(2,1)S(1)}, u32[]{:S(2)}, u32[]{:S(2)}) collective-permute-start(bf16[192,256]{1,0:T(8,128)(2,1)S(1)} %slice.89), channel_id=1, source_target_pairs={{0,12},{1,13},{2,14},{3,15},{4,0},{5,1},{6,2},{7,3},{8,4},{9,5},{1... | collective-permute-start | bytes 294920 | tf_op jit(solution)/shard_map/ppermute | solution.py:174
  39.0 2.7 %collective-permute-start.11 = (bf16[192,256]{1,0:T(8,128)(2,1)S(1)}, bf16[192,256]{1,0:T(8,128)(2,1)S(1)}, u32[]{:S(2)}, u32[]{:S(2)}) collective-permute-start(bf16[192,256]{1,0:T(8,128)(2,1)S(1)} %slice.94), channel_id=1, source_target_pairs={{0,3},{1,0},{2,1},{3,2},{4,7},{5,4},{6,5},{7,6},{8,11},{9,8},{10,9... | collective-permute-start | bytes 294920 | tf_op jit(solution)/shard_map/ppermute | solution.py:174
  44.6 2.7 %collective-permute-done.10 = bf16[192,256]{1,0:T(8,128)(2,1)S(1)} collective-permute-done((bf16[192,256]{1,0:T(8,128)(2,1)S(1)}, bf16[192,256]{1,0:T(8,128)(2,1)S(1)}, u32[]{:S(2)}, u32[]{:S(2)}) %collective-permute-start.10) | collective-permute-done | bytes 98336 | tf_op jit(solution)/shard_map/ppermute | solution.py:174
  48.5 3.6 %collective-permute-start.14 = (bf16[1536,256]{1,0:T(8,128)(2,1)}, bf16[1536,256]{1,0:T(8,128)(2,1)S(1)}, u32[]{:S(2)}, u32[]{:S(2)}) collective-permute-start(bf16[1536,256]{1,0:T(8,128)(2,1)} %constant_dynamic-update-slice_fusion.5), channel_id=1, source_target_pairs={{0,12},{1,13},{2,14},{3,15},{4,0},{5,1},{6,2},{7,3},{8,4},{9,5},{1... | collective-permute-start | bytes 2359304 | tf_op jit(solution)/shard_map/ppermute | solution.py:174
  54.9 14.4 %collective-permute-done.14 = bf16[1536,256]{1,0:T(8,128)(2,1)S(1)} collective-permute-done((bf16[1536,256]{1,0:T(8,128)(2,1)}, bf16[1536,256]{1,0:T(8,128)(2,1)S(1)}, u32[]{:S(2)}, u32[]{:S(2)}) %collective-permute-start.14) | collective-permute-done | bytes 786464 | tf_op jit(solution)/shard_map/ppermute | solution.py:174
  69.4 3.5 %collective-permute-start.15 = (bf16[768,256]{1,0:T(8,128)(2,1)S(1)}, bf16[768,256]{1,0:T(8,128)(2,1)}, u32[]{:S(2)}, u32[]{:S(2)}) collective-permute-start(bf16[768,256]{1,0:T(8,128)(2,1)S(1)} %slice.96), channel_id=1, source_target_pairs={{0,12},{1,13},{2,14},{3,15},{4,0},{5,1},{6,2},{7,3},{8,4},{9,5},{1... | collective-permute-start | bytes 1179656 | tf_op jit(solution)/shard_map/ppermute | solution.py:174
  74.8 1.8 slice.90
  78.0 15.1 %turn.1 = (bf16[16,1792,256]{2,1,0:T(8,128)(2,1)S(1)}, bf16[16,256,896]{2,1,0:T(8,128)(2,1)S(1)}) custom-call(bf16[4096,896]{1,0:T(8,128)(2,1)} %bitcast.58, bf16[4096,896]{1,0:T(8,128)(2,1)} %bitcast.61, bf16[896,4096]{1,0:T(8,128)(2,1)} %bitcast.66), custom_call_target="tpu_custom_call" | custom-call | tf_op jit(solution)/shard_map/turn/pallas_call | solution.py:236
  93.2 5.2 %copy-done = bf16[16,1792,256]{2,1,0:T(8,128)(2,1)} copy-done((bf16[16,1792,256]{2,1,0:T(8,128)(2,1)}, bf16[16,1792,256]{2,1,0:T(8,128)(2,1)S(1)}, u32[]{:S(2)}) %copy-start) | copy-done | bytes 14680088
  98.4 2.9 %copy-done.1 = bf16[16,256,896]{2,1,0:T(8,128)(2,1)} copy-done((bf16[16,256,896]{2,1,0:T(8,128)(2,1)}, bf16[16,256,896]{2,1,0:T(8,128)(2,1)S(1)}, u32[]{:S(2)}) %copy-start.1) | copy-done | bytes 7340056
  101.3 14.6 %acts.2 = (f32[8,96,896]{2,1,0:T(8,128)S(1)}, f32[8,96,896]{2,1,0:T(8,128)S(1)}) custom-call(s32[32]{0:T(128)S(1)} %reshape.270.order, bf16[4,384,256]{2,1,0:T(8,128)(2,1)} %bitcast.15.refs_0_, bf16[4,384,256]{2,1,0:T(8,128)(2,1)} %bitcast.16.refs_1_, bf16[4,384,256]{2,1,0:T(8,128)(2,1)} %bitcast.69, bf16[4,384,256]{2,1,0:T(8,128)(2,1)} %bitcast.18.refs_3_, ...), custom_call_target="tpu_custom_call" | custom-call | tf_op jit(solution)/shard_map/acts/pallas_call | solution.py:263
  116.0 10.2 %acts.3 = (f32[8,96,896]{2,1,0:T(8,128)S(1)}, f32[8,96,896]{2,1,0:T(8,128)S(1)}) custom-call(s32[32]{0:T(128)S(1)} %reshape.270.order, bf16[2,384,256]{2,1,0:T(8,128)(2,1)} %bitcast.8.refs_0_, bf16[2,384,256]{2,1,0:T(8,128)(2,1)} %bitcast.9.refs_1_, bf16[2,384,256]{2,1,0:T(8,128)(2,1)} %bitcast.11.refs_2_, bf16[2,384,256]{2,1,0:T(8,128)(2,1)} %bitcast.12.refs_3_, ...), custom_call_target="tpu_custom_call" | custom-call | tf_op jit(solution)/shard_map/acts/pallas_call | solution.py:263
  129.2 16.5 %expert.3 = (bf16[4,256,256]{2,1,0:T(8,128)(2,1)S(1)}, bf16[4,256,256]{2,1,0:T(8,128)(2,1)S(1)}, bf16[4,256,256]{2,1,0:T(8,128)(2,1)S(1)}, bf16[4,256,256]{2,1,0:T(8,128)(2,1)S(1)}) custom-call(s32[16]{0:T(128)S(1)} %reshape.284.order, bf16[16,8,96,256]{3,2,1,0:T(8,128)(2,1)} %bitcast.64, bf16[16,256,896]{2,1,0:T(8,128)(2,1)} %copy-done.1, ...), custom_call_target="tpu_custom_call" | custom-call | tf_op jit(solution)/shard_map/expert/pallas_call | solution.py:301
  150.4 21.2 %expert.2 = (bf16[4,512,256]{2,1,0:T(8,128)(2,1)S(1)}, bf16[4,512,256]{2,1,0:T(8,128)(2,1)S(1)}, bf16[4,512,256]{2,1,0:T(8,128)(2,1)S(1)}, bf16[4,512,256]{2,1,0:T(8,128)(2,1)S(1)}) custom-call(s32[16]{0:T(128)S(1)} %reshape.268.order, bf16[16,8,96,256]{3,2,1,0:T(8,128)(2,1)} %bitcast.65, bf16[16,256,896]{2,1,0:T(8,128)(2,1)} %copy-done.1, ...), custom_call_target="tpu_custom_call" | custom-call | tf_op jit(solution)/shard_map/expert/pallas_call | solution.py:301
  172.7 2.0 collective-permute-start.17
  177.9 2.1 collective-permute-start.27
  180.0 6.9 %collective-permute-done.16 = bf16[4,512,256]{2,1,0:T(8,128)(2,1)S(1)} collective-permute-done((bf16[4,512,256]{2,1,0:T(8,128)(2,1)S(1)}, bf16[4,512,256]{2,1,0:T(8,128)(2,1)S(1)}, u32[]{:S(2)}, u32[]{:S(2)}) %collective-permute-start.16) | collective-permute-done | bytes 1048608 | tf_op jit(solution)/shard_map/ppermute | solution.py:174
  187.0 30.7 %collective-permute-done.17 = bf16[4,512,256]{2,1,0:T(8,128)(2,1)S(1)} collective-permute-done((bf16[4,512,256]{2,1,0:T(8,128)(2,1)S(1)}, bf16[4,512,256]{2,1,0:T(8,128)(2,1)S(1)}, u32[]{:S(2)}, u32[]{:S(2)}) %collective-permute-start.17) | collective-permute-done | bytes 1048608 | tf_op jit(solution)/shard_map/ppermute | solution.py:174
  220.5 4.6 %collective-permute-done.19 = bf16[512,256]{1,0:T(8,128)(2,1)S(1)} collective-permute-done((bf16[512,256]{1,0:T(8,128)(2,1)S(1)}, bf16[512,256]{1,0:T(8,128)(2,1)S(1)}, u32[]{:S(2)}, u32[]{:S(2)}) %collective-permute-start.19) | collective-permute-done | bytes 262176 | tf_op jit(solution)/shard_map/ppermute | solution.py:174
  225.2 2.7 %collective-permute-done.20 = bf16[512,256]{1,0:T(8,128)(2,1)S(1)} collective-permute-done((bf16[512,256]{1,0:T(8,128)(2,1)S(1)}, bf16[512,256]{1,0:T(8,128)(2,1)S(1)}, u32[]{:S(2)}, u32[]{:S(2)}) %collective-permute-start.20) | collective-permute-done | bytes 262176 | tf_op jit(solution)/shard_map/ppermute | solution.py:174
  228.0 24.2 %all_to_all.11.refs_0_ = bf16[8,96,256]{2,1,0:T(8,128)(2,1)S(1)} all-to-all(bf16[8,96,256]{2,1,0:T(8,128)(2,1)S(1)} %pad_maximum_fusion), channel_id=1, replica_groups=mesh['ep'=8,'tp'=16] {'ep'}, dimensions={0} | all-to-all | bytes 786432 | tf_op jit(solution)/shard_map/all_to_all | solution.py:333
  (110 shorter events, 32.0 us)
Async XLA Ops:
  6.5 122.7 %all-gather.2.cloned.1.call-start = ((), (), s32[]{:S(2)}) async-start(), calls=%async_computation.2 | async-start | bytes 6684672 | tf_op jit(solution)/shard_map/all_gather | solution.py:230
  28.1 8.0 %collective-permute-start.1 = (bf16[384,256]{1,0:T(8,128)(2,1)S(1)}, bf16[384,256]{1,0:T(8,128)(2,1)S(1)}, u32[]{:S(2)}, u32[]{:S(2)}) collective-permute-start(bf16[384,256]{1,0:T(8,128)(2,1)S(1)} %bitcast.75), channel_id=1, source_target_pairs={{0,12},{1,13},{2,14},{3,15},{4,0},{5,1},{6,2},{7,3},{8,4},{9,5},{1... | collective-permute-start | bytes 589832 | tf_op jit(solution)/shard_map/ppermute | solution.py:174
  34.7 7.0 %collective-permute-start.8 = (bf16[384,256]{1,0:T(8,128)(2,1)S(1)}, bf16[384,256]{1,0:T(8,128)(2,1)S(1)}, u32[]{:S(2)}, u32[]{:S(2)}) collective-permute-start(bf16[384,256]{1,0:T(8,128)(2,1)S(1)} %bitcast.73), channel_id=1, source_target_pairs={{0,1},{1,2},{2,3},{3,0},{4,5},{5,6},{6,7},{7,4},{8,9},{9,10},{10,1... | collective-permute-start | bytes 589832 | tf_op jit(solution)/shard_map/ppermute | solution.py:174
  36.1 16.6 %collective-permute-start.3 = (bf16[192,256]{1,0:T(8,128)(2,1)S(1)}, bf16[192,256]{1,0:T(8,128)(2,1)S(1)}, u32[]{:S(2)}, u32[]{:S(2)}) collective-permute-start(bf16[192,256]{1,0:T(8,128)(2,1)S(1)} %slice.89), channel_id=1, source_target_pairs={{0,12},{1,13},{2,14},{3,15},{4,0},{5,1},{6,2},{7,3},{8,4},{9,5},{1... | collective-permute-start | bytes 294920 | tf_op jit(solution)/shard_map/ppermute | solution.py:174
  38.9 13.2 %collective-permute-start.2 = (bf16[192,256]{1,0:T(8,128)(2,1)S(1)}, bf16[192,256]{1,0:T(8,128)(2,1)S(1)}, u32[]{:S(2)}, u32[]{:S(2)}) collective-permute-start(bf16[192,256]{1,0:T(8,128)(2,1)S(1)} %slice.88), channel_id=1, source_target_pairs={{0,4},{1,5},{2,6},{3,7},{4,8},{5,9},{6,10},{7,11},{8,12},{9,13},{1... | collective-permute-start | bytes 294920 | tf_op jit(solution)/shard_map/ppermute | solution.py:174
  39.0 8.9 %collective-permute-start.11 = (bf16[192,256]{1,0:T(8,128)(2,1)S(1)}, bf16[192,256]{1,0:T(8,128)(2,1)S(1)}, u32[]{:S(2)}, u32[]{:S(2)}) collective-permute-start(bf16[192,256]{1,0:T(8,128)(2,1)S(1)} %slice.94), channel_id=1, source_target_pairs={{0,3},{1,0},{2,1},{3,2},{4,7},{5,4},{6,5},{7,6},{8,11},{9,8},{10,9... | collective-permute-start | bytes 294920 | tf_op jit(solution)/shard_map/ppermute | solution.py:174
  48.5 20.8 %collective-permute-start.14 = (bf16[1536,256]{1,0:T(8,128)(2,1)}, bf16[1536,256]{1,0:T(8,128)(2,1)S(1)}, u32[]{:S(2)}, u32[]{:S(2)}) collective-permute-start(bf16[1536,256]{1,0:T(8,128)(2,1)} %constant_dynamic-update-slice_fusion.5), channel_id=1, source_target_pairs={{0,12},{1,13},{2,14},{3,15},{4,0},{5,1},{6,2},{7,3},{8,4},{9,5},{1... | collective-permute-start | bytes 2359304 | tf_op jit(solution)/shard_map/ppermute | solution.py:174
  52.1 20.8 %collective-permute-start.12 = (bf16[1536,256]{1,0:T(8,128)(2,1)}, bf16[1536,256]{1,0:T(8,128)(2,1)S(1)}, u32[]{:S(2)}, u32[]{:S(2)}) collective-permute-start(bf16[1536,256]{1,0:T(8,128)(2,1)} %constant_dynamic-update-slice_fusion.5), channel_id=1, source_target_pairs={{0,4},{1,5},{2,6},{3,7},{4,8},{5,9},{6,10},{7,11},{8,12},{9,13},{1... | collective-permute-start | bytes 2359304 | tf_op jit(solution)/shard_map/ppermute | solution.py:174
  53.4 19.6 %collective-permute-start.6 = (bf16[1536,256]{1,0:T(8,128)(2,1)}, bf16[1536,256]{1,0:T(8,128)(2,1)S(1)}, u32[]{:S(2)}, u32[]{:S(2)}) collective-permute-start(bf16[1536,256]{1,0:T(8,128)(2,1)} %constant_dynamic-update-slice_fusion), channel_id=1, source_target_pairs={{0,3},{1,0},{2,1},{3,2},{4,7},{5,4},{6,5},{7,6},{8,11},{9,8},{10,9... | collective-permute-start | bytes 2359304 | tf_op jit(solution)/shard_map/ppermute | solution.py:174
  53.4 21.4 %collective-permute-start.4 = (bf16[1536,256]{1,0:T(8,128)(2,1)}, bf16[1536,256]{1,0:T(8,128)(2,1)}, u32[]{:S(2)}, u32[]{:S(2)}) collective-permute-start(bf16[1536,256]{1,0:T(8,128)(2,1)} %constant_dynamic-update-slice_fusion), channel_id=1, source_target_pairs={{0,1},{1,2},{2,3},{3,0},{4,5},{5,6},{6,7},{7,4},{8,9},{9,10},{10,1... | collective-permute-start | bytes 2359304 | tf_op jit(solution)/shard_map/ppermute | solution.py:174
  69.4 46.6 %collective-permute-start.15 = (bf16[768,256]{1,0:T(8,128)(2,1)S(1)}, bf16[768,256]{1,0:T(8,128)(2,1)}, u32[]{:S(2)}, u32[]{:S(2)}) collective-permute-start(bf16[768,256]{1,0:T(8,128)(2,1)S(1)} %slice.96), channel_id=1, source_target_pairs={{0,12},{1,13},{2,14},{3,15},{4,0},{5,1},{6,2},{7,3},{8,4},{9,5},{1... | collective-permute-start | bytes 1179656 | tf_op jit(solution)/shard_map/ppermute | solution.py:174
  72.9 43.1 %collective-permute-start.13 = (bf16[768,256]{1,0:T(8,128)(2,1)S(1)}, bf16[768,256]{1,0:T(8,128)(2,1)}, u32[]{:S(2)}, u32[]{:S(2)}) collective-permute-start(bf16[768,256]{1,0:T(8,128)(2,1)S(1)} %slice.95), channel_id=1, source_target_pairs={{0,4},{1,5},{2,6},{3,7},{4,8},{5,9},{6,10},{7,11},{8,12},{9,13},{1... | collective-permute-start | bytes 1179656 | tf_op jit(solution)/shard_map/ppermute | solution.py:174
  73.9 42.1 %collective-permute-start.7 = (bf16[768,256]{1,0:T(8,128)(2,1)}, bf16[768,256]{1,0:T(8,128)(2,1)}, u32[]{:S(2)}, u32[]{:S(2)}) collective-permute-start(bf16[768,256]{1,0:T(8,128)(2,1)} %slice.91), channel_id=1, source_target_pairs={{0,3},{1,0},{2,1},{3,2},{4,7},{5,4},{6,5},{7,6},{8,11},{9,8},{10,9... | collective-permute-start | bytes 1179656 | tf_op jit(solution)/shard_map/ppermute | solution.py:174
  76.6 39.4 %collective-permute-start.5 = (bf16[768,256]{1,0:T(8,128)(2,1)}, bf16[768,256]{1,0:T(8,128)(2,1)}, u32[]{:S(2)}, u32[]{:S(2)}) collective-permute-start(bf16[768,256]{1,0:T(8,128)(2,1)} %slice.90), channel_id=1, source_target_pairs={{0,1},{1,2},{2,3},{3,0},{4,5},{5,6},{6,7},{7,4},{8,9},{9,10},{10,1... | collective-permute-start | bytes 1179656 | tf_op jit(solution)/shard_map/ppermute | solution.py:174
  145.8 28.9 %collective-permute-start.22 = (bf16[4,256,256]{2,1,0:T(8,128)(2,1)S(1)}, bf16[4,256,256]{2,1,0:T(8,128)(2,1)S(1)}, u32[]{:S(2)}, u32[]{:S(2)}) collective-permute-start(bf16[4,256,256]{2,1,0:T(8,128)(2,1)S(1)} %get-tuple-element.30), channel_id=1, source_target_pairs={{0,2},{1,3},{2,0},{3,1},{4,6},{5,7},{6,4},{7,5},{8,10},{9,11},{10,... | collective-permute-start | bytes 1572872 | tf_op jit(solution)/shard_map/ppermute | solution.py:174
  147.1 28.3 %collective-permute-start.23 = (bf16[4,256,256]{2,1,0:T(8,128)(2,1)S(1)}, bf16[4,256,256]{2,1,0:T(8,128)(2,1)S(1)}, u32[]{:S(2)}, u32[]{:S(2)}) collective-permute-start(bf16[4,256,256]{2,1,0:T(8,128)(2,1)S(1)} %get-tuple-element.31), channel_id=1, source_target_pairs={{0,1},{1,2},{2,3},{3,0},{4,5},{5,6},{6,7},{7,4},{8,9},{9,10},{10,1... | collective-permute-start | bytes 1572872 | tf_op jit(solution)/shard_map/ppermute | solution.py:174
  148.5 26.9 %collective-permute-start.24 = (bf16[4,256,256]{2,1,0:T(8,128)(2,1)S(1)}, bf16[4,256,256]{2,1,0:T(8,128)(2,1)}, u32[]{:S(2)}, u32[]{:S(2)}) collective-permute-start(bf16[4,256,256]{2,1,0:T(8,128)(2,1)S(1)} %get-tuple-element.32), channel_id=1, source_target_pairs={{0,3},{1,0},{2,1},{3,2},{4,7},{5,4},{6,5},{7,6},{8,11},{9,8},{10,9... | collective-permute-start | bytes 1572872 | tf_op jit(solution)/shard_map/ppermute | solution.py:174
  171.6 15.3 %collective-permute-start.16 = (bf16[4,512,256]{2,1,0:T(8,128)(2,1)S(1)}, bf16[4,512,256]{2,1,0:T(8,128)(2,1)S(1)}, u32[]{:S(2)}, u32[]{:S(2)}) collective-permute-start(bf16[4,512,256]{2,1,0:T(8,128)(2,1)S(1)} %get-tuple-element.26), channel_id=1, source_target_pairs={{0,8},{1,9},{2,10},{3,11},{4,12},{5,13},{6,14},{7,15},{8,0},{9,1},... | collective-permute-start | bytes 3145736 | tf_op jit(solution)/shard_map/ppermute | solution.py:174
  172.7 44.9 %collective-permute-start.17 = (bf16[4,512,256]{2,1,0:T(8,128)(2,1)S(1)}, bf16[4,512,256]{2,1,0:T(8,128)(2,1)S(1)}, u32[]{:S(2)}, u32[]{:S(2)}) collective-permute-start(bf16[4,512,256]{2,1,0:T(8,128)(2,1)S(1)} %get-tuple-element.27), channel_id=1, source_target_pairs={{0,4},{1,5},{2,6},{3,7},{4,8},{5,9},{6,10},{7,11},{8,12},{9,13},{1... | collective-permute-start | bytes 3145736 | tf_op jit(solution)/shard_map/ppermute | solution.py:174
  174.7 43.0 %collective-permute-start.18 = (bf16[4,512,256]{2,1,0:T(8,128)(2,1)S(1)}, bf16[4,512,256]{2,1,0:T(8,128)(2,1)S(1)}, u32[]{:S(2)}, u32[]{:S(2)}) collective-permute-start(bf16[4,512,256]{2,1,0:T(8,128)(2,1)S(1)} %get-tuple-element.28), channel_id=1, source_target_pairs={{0,12},{1,13},{2,14},{3,15},{4,0},{5,1},{6,2},{7,3},{8,4},{9,5},{1... | collective-permute-start | bytes 3145736 | tf_op jit(solution)/shard_map/ppermute | solution.py:174
  176.8 43.2 %collective-permute-start.25 = (bf16[256,256]{1,0:T(8,128)(2,1)S(1)}, bf16[256,256]{1,0:T(8,128)(2,1)S(1)}, u32[]{:S(2)}, u32[]{:S(2)}) collective-permute-start(bf16[256,256]{1,0:T(8,128)(2,1)S(1)} %get-tuple-element.42), channel_id=1, source_target_pairs={{0,8},{1,9},{2,10},{3,11},{4,12},{5,13},{6,14},{7,15},{8,0},{9,1},... | collective-permute-start | bytes 393224 | tf_op jit(solution)/shard_map/ppermute | solution.py:174
  177.9 42.0 %collective-permute-start.27 = (bf16[256,256]{1,0:T(8,128)(2,1)S(1)}, bf16[256,256]{1,0:T(8,128)(2,1)S(1)}, u32[]{:S(2)}, u32[]{:S(2)}) collective-permute-start(bf16[256,256]{1,0:T(8,128)(2,1)S(1)} %get-tuple-element.43), channel_id=1, source_target_pairs={{0,12},{1,13},{2,14},{3,15},{4,0},{5,1},{6,2},{7,3},{8,4},{9,5},{1... | collective-permute-start | bytes 393224 | tf_op jit(solution)/shard_map/ppermute | solution.py:174
  186.9 33.5 %collective-permute-start.26 = (bf16[256,256]{1,0:T(8,128)(2,1)S(1)}, bf16[256,256]{1,0:T(8,128)(2,1)S(1)}, u32[]{:S(2)}, u32[]{:S(2)}) collective-permute-start(bf16[256,256]{1,0:T(8,128)(2,1)S(1)} %get-tuple-element.44), channel_id=1, source_target_pairs={{0,4},{1,5},{2,6},{3,7},{4,8},{5,9},{6,10},{7,11},{8,12},{9,13},{1... | collective-permute-start | bytes 393224 | tf_op jit(solution)/shard_map/ppermute | solution.py:174
  219.9 8.0 %collective-permute-start.20 = (bf16[512,256]{1,0:T(8,128)(2,1)S(1)}, bf16[512,256]{1,0:T(8,128)(2,1)S(1)}, u32[]{:S(2)}, u32[]{:S(2)}) collective-permute-start(bf16[512,256]{1,0:T(8,128)(2,1)S(1)} %get-tuple-element.39), channel_id=1, source_target_pairs={{0,1},{1,2},{2,3},{3,0},{4,5},{5,6},{6,7},{7,4},{8,9},{9,10},{10,1... | collective-permute-start | bytes 786440 | tf_op jit(solution)/shard_map/ppermute | solution.py:174
  (19 other events, 241.4 us)
Sparse Core Ops, SparseCore 0:
  28.2 79.6 all-gather.1
where the time goes:
time: 262 us; the launch traced here: 260 us
  Pallas kernels  79.4 us (30%)
  waiting for transfers between devices  62.6 us (24%)
  blocking collectives  41.9 us (16%)
  starting transfers between devices  35.1 us (13%)
  local copies, waits for them, and re-layouts  25.4 us (10%)
  between operations  13.7 us (5%)
    ppermute x28, waiting for transfers between devices, shifted(): return lax.ppermute(x, 'tp', shift(by))  62.6 us
    pallas_call x2, Pallas kernels, body(): pl.pallas_call(expert_body, grid_spec=pltpu.PrefetchScalarGridSpec(num_sc...  37.7 us
    ppermute x28, starting transfers between devices, shifted(): return lax.ppermute(x, 'tp', shift(by))  35 us
    pallas_call x2, Pallas kernels, body(): pl.pallas_call(functools.partial(acts_body, first=first, count=count), gr...  24.8 us
    all_to_all x1, blocking collectives, body(): lax.all_to_all(jnp.concatenate(summed, axis=1), 'ep', split_axis=0, conca...  24.2 us
    unnamed x36, local copies, waits for them, and re-layouts  19.1 us
    all_to_all x1, blocking collectives, body(): got = lax.all_to_all(sent, 'ep', split_axis=0, concat_axis=0, tiled=True)  17.7 us
    pallas_call x1, Pallas kernels, body(): pl.pallas_call(turn_body, grid=(TP,), in_specs=[pl.BlockSpec((width, unit...  15.1 us
  transfers between devices with their start and end apart: 29, of which 7 were waited for; matrix products, arithmetic and copies ran while one was open for 5% of the time, Pallas kernels for 23%

commit v1 on v0

v1 whole, which is shorter than its diff:
```python
import functools

import jax
import jax.numpy as jnp
import numpy as np
from jax import lax
from jax.experimental import pallas as pl
from jax.experimental.pallas import tpu as pltpu
from jax.sharding import PartitionSpec as P


BF = jnp.bfloat16
F32 = jnp.float32
SIDE = 4
TP = SIDE * SIDE
COLS_BY_COLS = (((0,), (0,)), ((), ()))


def flat_slots(routes, experts, capacity):
    tokens = routes.shape[1]
    first, second = routes[0:1, :], routes[1:2, :]
    expert = lax.broadcasted_iota(jnp.int32, (experts, tokens), 0)
    in_first, in_second = expert == first, expert == second
    named = jnp.where(in_first | in_second, 1.0, 0.0).astype(BF)
    earlier = lax.broadcasted_iota(jnp.int32, (tokens, tokens), 0)
    later = lax.broadcasted_iota(jnp.int32, (tokens, tokens), 1)
    before = jnp.dot(named, jnp.where(earlier < later, 1.0, 0.0).astype(BF), preferred_element_type=F32)
    place_first = jnp.sum(jnp.where(in_first, before, 0.0), axis=0, keepdims=True)
    place_second = jnp.sum(jnp.where(in_second, before, 0.0), axis=0, keepdims=True)
    return (
        first * capacity + place_first.astype(jnp.int32),
        second * capacity + place_second.astype(jnp.int32),
    )


def dispatch_body(routes, inputs, grads, out):
    experts, both, _ = out.shape
    capacity = both // 2
    tokens = inputs.shape[0]
    first, second = flat_slots(routes[...], experts, capacity)
    slot = lax.broadcasted_iota(jnp.int32, (experts * capacity, tokens), 0)
    pick = jnp.where((slot == first) | (slot == second), 1.0, 0.0).astype(BF)
    for at, source in ((0, inputs), (capacity, grads)):
        rows = jnp.dot(pick, source[...], preferred_element_type=F32).astype(BF)
        for e in range(experts):
            out[e, at : at + capacity] = rows[e * capacity : (e + 1) * capacity]


def combine_body(routes, shares, *refs):
    backs, out = refs[:-1], refs[-1]
    experts, part, _ = backs[0].shape
    capacity = part * len(backs)
    tokens = out.shape[0]
    first, second = flat_slots(routes[...], experts, capacity)
    slot = lax.broadcasted_iota(jnp.int32, (experts * capacity, tokens), 0)
    share = jnp.concatenate([shares[...], jnp.zeros((6, tokens), F32)], axis=0).T
    back = jnp.concatenate([ref[e] for e in range(experts) for ref in backs], axis=0)
    one = lax.dot_general(
        jnp.where(slot == first, 1.0, 0.0).astype(BF), back, COLS_BY_COLS, preferred_element_type=F32
    )
    two = lax.dot_general(
        jnp.where(slot == second, 1.0, 0.0).astype(BF), back, COLS_BY_COLS, preferred_element_type=F32
    )
    out[...] = (one * share[:, 0:1] + two * share[:, 1:2]).astype(out.dtype)


def turn_body(gate, up, down, wide, tall):
    units = gate.shape[1]
    wide[0, :units] = gate[...].T
    wide[0, units:] = up[...].T
    tall[0] = down[...].T


def acts_body(order, *refs, first, count):
    if first > 0:
        pieces, (before, gate, up, out, weights, rows, arrived, result, leaving) = refs[:-9], refs[-9:]
    else:
        pieces, (gate, up, out, weights, rows, arrived) = refs[:-6], refs[-6:]
        result, before = out, None
    per_half = len(pieces) // 2
    units = gate.shape[-1]
    width = gate.shape[1]

    def fetch(k):
        return [
            pltpu.make_async_copy(gate.at[order[k]], weights.at[k, :, :units], arrived.at[0, k]),
            pltpu.make_async_copy(up.at[order[k]], weights.at[k, :, units:], arrived.at[1, k]),
        ]

    lows = [SIDE * s + f for s in range(first, first + count) for f in range(SIDE)]
    highs = [SIDE * f + s for s in range(first, first + count) for f in range(SIDE)]
    for k in dict.fromkeys(lows + highs):
        for copy in fetch(k):
            copy.start()
    for half in range(2):
        blocks = [p.at[i] for p in pieces[half * per_half : (half + 1) * per_half] for i in range(p.shape[0])]
        for at, block in enumerate(blocks):
            s, f = at // SIDE, at % SIDE
            rows[half * count + s, :, f * width : (f + 1) * width] = block[...]

    for half in range(2):

        def ring(i, carry, half=half):
            s = first + i
            slots = [SIDE * s + f if half == 0 else SIDE * f + s for f in range(SIDE)]
            for f in range(SIDE):
                if half == 0 or (f >= SIDE - 1 if first == 0 else f < SIDE - 1):
                    for copy in fetch(slots[f]):
                        copy.wait()
            right = jnp.concatenate([weights[k] for k in slots], axis=0)
            part = jnp.dot(rows[half * count + i], right, preferred_element_type=F32)
            if before is not None:
                result[half] = before[half] + part
            else:

                @pl.when(i == 0)
                def _():
                    result[half] = part

                @pl.when(i != 0)
                def _():
                    result[half] += part

            return carry

        lax.fori_loop(0, count, ring, 0)
        if first > 0:
            pltpu.make_async_copy(result.at[half], out.at[half], leaving.at[half]).start()
    if first > 0:
        for half in range(2):
            pltpu.make_async_copy(result.at[half], out.at[half], leaving.at[half]).wait()


def expert_body(order, acts, g, tall, wide, *refs, start):
    outs = refs[:SIDE]
    left, downs, sides, held, total, grads, g_here, tall_here, wide_here, acts_here = refs[SIDE:]
    experts, part_rows, features = left.shape
    rows = experts * part_rows
    width = features // TP
    units = total.shape[1]
    deep = 4
    span = TP // deep

    def fetch_g(t, lanes):
        return pltpu.make_async_copy(g.at[t, :, start : start + part_rows, :], left.at[:, :, lanes], g_here.at[t])

    def fetch_tall(i, here):
        return pltpu.make_async_copy(tall.at[here], downs.at[here], tall_here.at[i])

    def fetch_wide(k):
        return pltpu.make_async_copy(wide.at[order[k]], sides.at[k], wide_here.at[k])

    fetch_acts = pltpu.make_async_copy(acts.at[:, start : start + part_rows, :], held, acts_here.at[0])
    for i in range(deep):
        for t in range(i * span, (i + 1) * span):
            fetch_g(t, slice(t * width, (t + 1) * width)).start()
        fetch_tall(i, slice(i * span, (i + 1) * span)).start()
    fetch_acts.start()
    for k in range(TP):
        fetch_wide(k).start()

    def deepen(i, carry):
        for j in range(span):
            t = i * span + j
            fetch_g(t, pl.ds(pl.multiple_of(t * width, width), width)).wait()
        here = pl.ds(i * span, span)
        fetch_tall(i, here).wait()
        step = span * width
        part = jnp.dot(
            left[:, :, pl.ds(pl.multiple_of(i * step, step), step)].reshape(rows, step),
            downs[here].reshape(step, units),
            preferred_element_type=F32,
        )

        @pl.when(i == 0)
        def _():
            total[...] = part

        @pl.when(i != 0)
        def _():
            total[...] += part

        return carry

    lax.fori_loop(0, deep, deepen, 0)
    fetch_acts.wait()

    def form(b, carry):
        here = pl.ds(pl.multiple_of(b * part_rows, part_rows), part_rows)
        gate, up = held[b, :, :units], held[b, :, units:]
        hidden = total[here]
        sigma = jax.nn.sigmoid(gate)
        slope = sigma * (1.0 + gate * (1.0 - sigma))
        grads[here, :units] = (hidden * up * slope).astype(BF)
        grads[here, units:] = (hidden * gate * sigma).astype(BF)
        return carry

    lax.fori_loop(0, experts, form, 0)

    def members(j, carry):
        k = 2 * j
        fetch_wide(k).wait()
        fetch_wide(k + 1).wait()
        right = jnp.concatenate([sides[k], sides[k + 1]], axis=1)
        part = jnp.dot(grads[...], right, preferred_element_type=F32).astype(BF)
        for f in range(SIDE):

            @pl.when(k // SIDE == f)
            def _():
                outs[f][k % SIDE] = part[:, :width]
                outs[f][k % SIDE + 1] = part[:, width:]

        return carry

    lax.fori_loop(0, TP // 2, members, 0)


def vmem(mebibytes):
    return pltpu.CompilerParams(vmem_limit_bytes=mebibytes << 20)


def in_hbm(*arrays):
    return [pltpu.with_memory_space_constraint(a, pltpu.HBM) for a in arrays]


def z_shift(by):
    return [(z * SIDE + y, (z + by) % SIDE * SIDE + y) for z in range(SIDE) for y in range(SIDE)]


def y_shift(by):
    return [(z * SIDE + y, z * SIDE + (y + by) % SIDE) for z in range(SIDE) for y in range(SIDE)]


def shifted(x, shift, by):
    return lax.ppermute(x, "tp", shift(by))


def ring_gather(x, shift):
    half = x.shape[0] // 2
    below = shifted(x, shift, 1)
    above = shifted(x, shift, 3)
    far_low = shifted(below[:half], shift, 1)
    far_high = shifted(above[half:], shift, 3)
    return [x, below, above, far_low, far_high]


def plane_gather(x, first, second):
    rows, width = x.shape
    line = jnp.concatenate(ring_gather(x, first), axis=0)
    return [piece.reshape(-1, rows, width) for piece in ring_gather(line, second)]


def ring_sum(far, ahead, behind, own, shift):
    total = own.astype(F32)
    for by, part in ((2, far), (1, ahead), (3, behind)):
        total = total + shifted(part.astype(BF), shift, by).astype(F32)
    return total


def body(layer_input, out_grad, route, gate_share, gate_weight, up_weight, down_weight):
    experts = lax.axis_size("ep")
    tokens, width = layer_input.shape
    choose = route.shape[1]
    capacity = tokens * choose * 3 // (2 * experts)
    slots = experts * capacity
    parts = (2 * capacity // 3, capacity // 3)
    gate_matrix, up_matrix, down_matrix = gate_weight[0], up_weight[0], down_weight[0]
    features, units = gate_matrix.shape
    routes, shares = route.T, gate_share.T

    me = lax.axis_index("tp")
    z, y = me // SIDE, me % SIDE
    away = np.array([0, SIDE - 1, 1, 2], np.int32)
    ahead = np.array([2, 1, 3, 0], np.int32)

    def plane(outer, inner, z_outer):
        outer, inner = np.repeat(outer, SIDE), np.tile(inner, SIDE)
        in_z, in_y = (outer, inner) if z_outer else (inner, outer)
        return ((z + in_z) % SIDE * SIDE + (y + in_y) % SIDE).astype(jnp.int32)

    gathered_order = plane(away, away, False)
    summed_order = [plane(ahead, np.arange(SIDE), True), plane(ahead, np.arange(SIDE), False)]

    sent = pl.pallas_call(
        dispatch_body,
        out_shape=jax.ShapeDtypeStruct((experts, 2 * capacity, width), BF),
        name="dispatch",
        compiler_params=vmem(16),
    )(routes, layer_input, out_grad)
    got = lax.all_to_all(sent, "ep", split_axis=0, concat_axis=0, tiled=True)
    all_g = lax.all_gather(got[:, capacity:].reshape(slots, width), "tp", axis=0, tiled=False)
    all_g = all_g.reshape(TP, experts, capacity, width)
    low = got[: experts // 2, :capacity].reshape(slots // 2, width)
    high = got[experts // 2 :, :capacity].reshape(slots // 2, width)
    pieces = plane_gather(low, z_shift, y_shift) + plane_gather(high, y_shift, z_shift)

    wide, tall = pl.pallas_call(
        turn_body,
        grid=(TP,),
        in_specs=[
            pl.BlockSpec((width, units), lambda k: (k, 0)),
            pl.BlockSpec((width, units), lambda k: (k, 0)),
            pl.BlockSpec((units, width), lambda k: (0, k)),
        ],
        out_specs=[
            pl.BlockSpec((1, 2 * units, width), lambda k: (k, 0, 0)),
            pl.BlockSpec((1, width, units), lambda k: (k, 0, 0)),
        ],
        out_shape=[
            pltpu.HBM((TP, 2 * units, width), BF),
            pltpu.HBM((TP, width, units), BF),
        ],
        name="turn",
        compiler_params=vmem(10),
    )(*in_hbm(gate_matrix, up_matrix, down_matrix))

    in_vmem = pl.BlockSpec(memory_space=pltpu.VMEM)
    in_smem = pl.BlockSpec(memory_space=pltpu.SMEM)
    stays = pl.BlockSpec(memory_space=pltpu.HBM)
    dma = pltpu.SemaphoreType.DMA
    acts = []
    per_half = len(pieces) // 2
    for first, count in ((0, SIDE - 1), (SIDE - 1, 1)):
        which = slice(0, 3) if first == 0 else slice(3, 5)
        used = pieces[:per_half][which] + pieces[per_half:][which] + acts
        shape = (2, slots // 2, 2 * units)
        last = first > 0
        acts = [
            pl.pallas_call(
                functools.partial(acts_body, first=first, count=count),
                in_specs=[in_smem] + [in_vmem] * len(used) + [stays] * 2,
                out_specs=stays if last else in_vmem,
                out_shape=pltpu.HBM(shape, F32) if last else jax.ShapeDtypeStruct(shape, F32),
                scratch_shapes=[
                    pltpu.VMEM((TP, width, 2 * units), BF),
                    pltpu.VMEM((2 * count, slots // 2, SIDE * width), BF),
                    dma((2, TP)),
                ]
                + ([pltpu.VMEM(shape, F32), dma((2,))] if last else []),
                name="acts",
                compiler_params=vmem(36),
            )(
                gathered_order,
                *used,
                *in_hbm(gate_matrix.reshape(TP, width, units), up_matrix.reshape(TP, width, units)),
            )
        ]
    acts = acts[0].reshape(experts, capacity, 2 * units)

    summed = []
    for h, part in enumerate(parts):
        rows = experts * part
        outs = pl.pallas_call(
            functools.partial(expert_body, start=sum(parts[:h])),
            in_specs=[in_smem] + [stays] * 4,
            out_specs=[in_vmem] * SIDE,
            out_shape=[jax.ShapeDtypeStruct((SIDE, rows, width), BF)] * SIDE,
            scratch_shapes=[
                pltpu.VMEM((experts, part, features), BF),
                pltpu.VMEM((TP, width, units), BF),
                pltpu.VMEM((TP, 2 * units, width), BF),
                pltpu.VMEM((experts, part, 2 * units), F32),
                pltpu.VMEM((rows, units), F32),
                pltpu.VMEM((rows, 2 * units), BF),
                dma((TP,)),
                dma((4,)),
                dma((TP,)),
                dma((1,)),
            ],
            name="expert",
            compiler_params=vmem(48),
        )(summed_order[h], *in_hbm(acts, all_g, tall, wide))
        first, second = (z_shift, y_shift) if h == 0 else (y_shift, z_shift)
        line = ring_sum(*outs, first)
        mine = ring_sum(line[2], line[1], line[3], line[0], second)
        summed.append(mine.astype(BF).reshape(experts, part, width))
    backs = [
        lax.all_to_all(jnp.concatenate(summed, axis=1), "ep", split_axis=0, concat_axis=0, tiled=True)
    ]

    return pl.pallas_call(
        combine_body,
        out_shape=jax.ShapeDtypeStruct((tokens, width), BF),
        name="combine",
        compiler_params=vmem(16),
    )(routes, shares, *backs)


def solution(mesh):
    return jax.shard_map(
        body,
        mesh=mesh,
        in_specs=(
            P("ep", "tp"),
            P("ep", "tp"),
            P("ep", None),
            P("ep", None),
            P("ep", None, "tp"),
            P("ep", None, "tp"),
            P("ep", "tp", None),
        ),
        out_specs=P("ep", "tp"),
        check_vma=False,
    )
```

time: 262 us -> 231 us (0.88)
  waiting for transfers between devices: 62.6 us -> 46.9 us
  local copies, waits for them, and re-layouts: 25.4 us -> 10.3 us
    ppermute x28, waiting for transfers between devices: 62.6 us -> 46.1 us  [shifted(): return lax.ppermute(x, 'tp', shift(by))]
    unnamed x36 -> x26, local copies, waits for them, and re-layouts: 19.1 us -> 7.99 us
    pallas_call x1, Pallas kernels: 15.1 us -> 21.5 us  [body(): pl.pallas_call(turn_body, grid=(TP,), in_specs=[pl.BlockSpec((width, unit...]
    pallas_call x4, Pallas kernels: 62.5 us -> 58.7 us  [the longest x2 35.7 us: body(): pl.pallas_call(functools.partial(expert_body, start=sum(parts[:h])), in_s...]
  transfers between devices with their start and end apart: 29 -> 29, of which waited for: 7 -> 9; matrix products, arithmetic and copies ran while one was open for 5% -> 3% of each run, Pallas kernels for 23% -> 28%
where the time goes in v1:
time: 231 us; the launch traced here: 230 us
  Pallas kernels  82 us (35%)
  waiting for transfers between devices  46.9 us (20%)
  blocking collectives  41.2 us (18%)
  starting transfers between devices  35.1 us (15%)
  between operations  13.7 us (6%)
  local copies, waits for them, and re-layouts  10.3 us (4%)
    ppermute x28, waiting for transfers between devices, shifted(): return lax.ppermute(x, 'tp', shift(by))  46.1 us
    pallas_call x2, Pallas kernels, body(): pl.pallas_call(functools.partial(expert_body, start=sum(parts[:h])), in_s...  35.7 us
    ppermute x28, starting transfers between devices, shifted(): return lax.ppermute(x, 'tp', shift(by))  35.1 us
    all_to_all x1, blocking collectives, body(): lax.all_to_all(jnp.concatenate(summed, axis=1), 'ep', split_axis=0, conca...  23.5 us
    pallas_call x2, Pallas kernels, body(): pl.pallas_call(functools.partial(acts_body, first=first, count=count), in...  23 us
    pallas_call x1, Pallas kernels, body(): pl.pallas_call(turn_body, grid=(TP,), in_specs=[pl.BlockSpec((width, unit...  21.5 us
    all_to_all x1, blocking collectives, body(): got = lax.all_to_all(sent, 'ep', split_axis=0, concat_axis=0, tiled=True)  17.7 us
    unnamed x26, local copies, waits for them, and re-layouts  7.99 us
  transfers between devices with their start and end apart: 29, of which 9 were waited for; matrix products, arithmetic and copies ran while one was open for 3% of the time, Pallas kernels for 28%

profile of v1, /device:TPU:1, one launch (start us, length us, event | category | flops | bytes accessed | tf_op | source)
XLA Modules:
  0.0 230.2 jit_solution(17318480749705519946)
XLA Ops:
  9.6 17.7 %all_to_all.10 = bf16[8,192,256]{2,1,0:T(8,128)(2,1)S(1)} all-to-all(bf16[8,192,256]{2,1,0:T(8,128)(2,1)S(1)} %dispatch.1), channel_id=1, replica_groups=mesh['ep'=8,'tp'=16] {'ep'}, dimensions={0} | all-to-all | bytes 1572864 | tf_op jit(solution)/shard_map/all_to_all | solution.py:290
  28.1 1.7 collective-permute-start
  29.8 2.2 collective-permute-start.1
  33.3 1.4 collective-permute-start.9
  36.3 2.7 %collective-permute-start.3 = (bf16[192,256]{1,0:T(8,128)(2,1)S(1)}, bf16[192,256]{1,0:T(8,128)(2,1)S(1)}, u32[]{:S(2)}, u32[]{:S(2)}) collective-permute-start(bf16[192,256]{1,0:T(8,128)(2,1)S(1)} %slice.84), channel_id=1, source_target_pairs={{0,12},{1,13},{2,14},{3,15},{4,0},{5,1},{6,2},{7,3},{8,4},{9,5},{1... | collective-permute-start | bytes 294920 | tf_op jit(solution)/shard_map/ppermute | solution.py:235
  40.4 1.5 collective-permute-start.11
  46.1 2.7 %collective-permute-start.6 = (bf16[1536,256]{1,0:T(8,128)(2,1)}, bf16[1536,256]{1,0:T(8,128)(2,1)S(1)}, u32[]{:S(2)}, u32[]{:S(2)}) collective-permute-start(bf16[1536,256]{1,0:T(8,128)(2,1)} %constant_dynamic-update-slice_fusion), channel_id=1, source_target_pairs={{0,3},{1,0},{2,1},{3,2},{4,7},{5,4},{6,5},{7,6},{8,11},{9,8},{10,9... | collective-permute-start | bytes 2359304 | tf_op jit(solution)/shard_map/ppermute | solution.py:235
  50.1 2.7 %collective-permute-start.14 = (bf16[1536,256]{1,0:T(8,128)(2,1)}, bf16[1536,256]{1,0:T(8,128)(2,1)S(1)}, u32[]{:S(2)}, u32[]{:S(2)}) collective-permute-start(bf16[1536,256]{1,0:T(8,128)(2,1)} %constant_dynamic-update-slice_fusion.5), channel_id=1, source_target_pairs={{0,12},{1,13},{2,14},{3,15},{4,0},{5,1},{6,2},{7,3},{8,4},{9,5},{1... | collective-permute-start | bytes 2359304 | tf_op jit(solution)/shard_map/ppermute | solution.py:235
  52.7 21.5 %turn.1 = (bf16[16,1792,256]{2,1,0:T(8,128)(2,1)}, bf16[16,256,896]{2,1,0:T(8,128)(2,1)}) custom-call(bf16[4096,896]{1,0:T(8,128)(2,1)} %bitcast.67, bf16[4096,896]{1,0:T(8,128)(2,1)} %bitcast.70, bf16[896,4096]{1,0:T(8,128)(2,1)} %bitcast.77), custom_call_target="tpu_custom_call" | custom-call | tf_op jit(solution)/shard_map/turn/pallas_call | solution.py:297
  74.5 2.7 %collective-permute-start.7 = (bf16[768,256]{1,0:T(8,128)(2,1)S(1)}, bf16[768,256]{1,0:T(8,128)(2,1)S(1)}, u32[]{:S(2)}, u32[]{:S(2)}) collective-permute-start(bf16[768,256]{1,0:T(8,128)(2,1)S(1)} %slice.86), channel_id=1, source_target_pairs={{0,3},{1,0},{2,1},{3,2},{4,7},{5,4},{6,5},{7,6},{8,11},{9,8},{10,9... | collective-permute-start | bytes 1179656 | tf_op jit(solution)/shard_map/ppermute | solution.py:235
  77.4 2.9 %collective-permute-start.15 = (bf16[768,256]{1,0:T(8,128)(2,1)S(1)}, bf16[768,256]{1,0:T(8,128)(2,1)S(1)}, u32[]{:S(2)}, u32[]{:S(2)}) collective-permute-start(bf16[768,256]{1,0:T(8,128)(2,1)S(1)} %slice.91), channel_id=1, source_target_pairs={{0,12},{1,13},{2,14},{3,15},{4,0},{5,1},{6,2},{7,3},{8,4},{9,5},{1... | collective-permute-start | bytes 1179656 | tf_op jit(solution)/shard_map/ppermute | solution.py:235
  80.3 15.1 %acts.2.refs_4_ = f32[2,384,1792]{2,1,0:T(8,128)S(1)} custom-call(s32[16]{0:T(128)S(1)} %fusion.9.order, bf16[4,384,256]{2,1,0:T(8,128)(2,1)} %bitcast.8.refs_0_, bf16[4,384,256]{2,1,0:T(8,128)(2,1)S(1)} %bitcast.56, bf16[4,384,256]{2,1,0:T(8,128)(2,1)S(1)} %bitcast.57, bf16[4,384,256]{2,1,0:T(8,128)(2,1)} %bitcast.11.refs_3_, ...), custom_call_target="tpu_custom_call" | custom-call | tf_op jit(solution)/shard_map/acts/pallas_call | solution.py:329
  96.7 8.0 %acts.3 = f32[2,384,1792]{2,1,0:T(8,128)} custom-call(s32[16]{0:T(128)S(1)} %fusion.9.order, bf16[2,384,256]{2,1,0:T(8,128)(2,1)S(1)} %bitcast.60, bf16[2,384,256]{2,1,0:T(8,128)(2,1)S(1)} %bitcast.61, bf16[2,384,256]{2,1,0:T(8,128)(2,1)S(1)} %bitcast.62, bf16[2,384,256]{2,1,0:T(8,128)(2,1)S(1)} %bitcast.63, f32[2,384,1792]{2,1,0:T(8,128)S(1)} %acts.2.refs_4_, ...), custom_call_target="tpu_custom_call" | custom-call | tf_op jit(solution)/shard_map/acts/pallas_call | solution.py:329
  105.5 15.1 %expert.3 = (bf16[4,256,256]{2,1,0:T(8,128)(2,1)S(1)}, bf16[4,256,256]{2,1,0:T(8,128)(2,1)S(1)}, bf16[4,256,256]{2,1,0:T(8,128)(2,1)S(1)}, bf16[4,256,256]{2,1,0:T(8,128)(2,1)S(1)}) custom-call(s32[16]{0:T(128)S(1)} %get-tuple-element.38.order, f32[8,96,1792]{2,1,0:T(8,128)} %bitcast.73, bf16[16,8,96,256]{3,2,1,0:T(8,128)(2,1)} %bitcast.75, ...), custom_call_target="tpu_custom_call" | custom-call | tf_op jit(solution)/shard_map/expert/pallas_call | solution.py:353
  123.0 20.6 %expert.2 = (bf16[4,512,256]{2,1,0:T(8,128)(2,1)S(1)}, bf16[4,512,256]{2,1,0:T(8,128)(2,1)S(1)}, bf16[4,512,256]{2,1,0:T(8,128)(2,1)S(1)}, bf16[4,512,256]{2,1,0:T(8,128)(2,1)S(1)}) custom-call(s32[16]{0:T(128)S(1)} %get-tuple-element.37.order, f32[8,96,1792]{2,1,0:T(8,128)} %bitcast.74, bf16[16,8,96,256]{3,2,1,0:T(8,128)(2,1)} %bitcast.76, ...), custom_call_target="tpu_custom_call" | custom-call | tf_op jit(solution)/shard_map/expert/pallas_call | solution.py:353
  143.6 1.9 collective-permute-start.18
  147.1 1.5 collective-permute-start.27
  149.2 14.7 %collective-permute-done.18 = bf16[4,512,256]{2,1,0:T(8,128)(2,1)S(1)} collective-permute-done((bf16[4,512,256]{2,1,0:T(8,128)(2,1)S(1)}, bf16[4,512,256]{2,1,0:T(8,128)(2,1)S(1)}, u32[]{:S(2)}, u32[]{:S(2)}) %collective-permute-start.18) | collective-permute-done | bytes 1048608 | tf_op jit(solution)/shard_map/ppermute | solution.py:235
  164.1 2.0 collective-permute-done.17
  166.1 20.3 %collective-permute-done.16 = bf16[4,512,256]{2,1,0:T(8,128)(2,1)S(1)} collective-permute-done((bf16[4,512,256]{2,1,0:T(8,128)(2,1)S(1)}, bf16[4,512,256]{2,1,0:T(8,128)(2,1)S(1)}, u32[]{:S(2)}, u32[]{:S(2)}) %collective-permute-start.16) | collective-permute-done | bytes 1048608 | tf_op jit(solution)/shard_map/ppermute | solution.py:235
  187.0 2.0 collective-permute-start.21
  189.2 1.6 collective-permute-start.19
  193.0 5.5 %collective-permute-done.20 = bf16[512,256]{1,0:T(8,128)(2,1)S(1)} collective-permute-done((bf16[512,256]{1,0:T(8,128)(2,1)S(1)}, bf16[512,256]{1,0:T(8,128)(2,1)S(1)}, u32[]{:S(2)}, u32[]{:S(2)}) %collective-permute-start.20) | collective-permute-done | bytes 262176 | tf_op jit(solution)/shard_map/ppermute | solution.py:235
  198.7 23.5 %all_to_all.11.refs_0_ = bf16[8,96,256]{2,1,0:T(8,128)(2,1)S(1)} all-to-all(bf16[8,96,256]{2,1,0:T(8,128)(2,1)S(1)} %pad_maximum_fusion), channel_id=1, replica_groups=mesh['ep'=8,'tp'=16] {'ep'}, dimensions={0} | all-to-all | bytes 786432 | tf_op jit(solution)/shard_map/all_to_all | solution.py:378
  (91 shorter events, 25.2 us)
Async XLA Ops:
  6.5 99.0 %all-gather.2.cloned.1.call-start = ((), (), s32[]{:S(2)}) async-start(), calls=%async_computation.2 | async-start | bytes 6684672 | tf_op jit(solution)/shard_map/all_gather | solution.py:291
  36.2 8.6 %collective-permute-start.2 = (bf16[192,256]{1,0:T(8,128)(2,1)S(1)}, bf16[192,256]{1,0:T(8,128)(2,1)S(1)}, u32[]{:S(2)}, u32[]{:S(2)}) collective-permute-start(bf16[192,256]{1,0:T(8,128)(2,1)S(1)} %slice.83), channel_id=1, source_target_pairs={{0,4},{1,5},{2,6},{3,7},{4,8},{5,9},{6,10},{7,11},{8,12},{9,13},{1... | collective-permute-start | bytes 294920 | tf_op jit(solution)/shard_map/ppermute | solution.py:235
  36.3 9.1 %collective-permute-start.3 = (bf16[192,256]{1,0:T(8,128)(2,1)S(1)}, bf16[192,256]{1,0:T(8,128)(2,1)S(1)}, u32[]{:S(2)}, u32[]{:S(2)}) collective-permute-start(bf16[192,256]{1,0:T(8,128)(2,1)S(1)} %slice.84), channel_id=1, source_target_pairs={{0,12},{1,13},{2,14},{3,15},{4,0},{5,1},{6,2},{7,3},{8,4},{9,5},{1... | collective-permute-start | bytes 294920 | tf_op jit(solution)/shard_map/ppermute | solution.py:235
  39.0 9.7 %collective-permute-start.10 = (bf16[192,256]{1,0:T(8,128)(2,1)S(1)}, bf16[192,256]{1,0:T(8,128)(2,1)S(1)}, u32[]{:S(2)}, u32[]{:S(2)}) collective-permute-start(bf16[192,256]{1,0:T(8,128)(2,1)S(1)} %slice.88), channel_id=1, source_target_pairs={{0,1},{1,2},{2,3},{3,0},{4,5},{5,6},{6,7},{7,4},{8,9},{9,10},{10,1... | collective-permute-start | bytes 294920 | tf_op jit(solution)/shard_map/ppermute | solution.py:235
  40.4 9.0 %collective-permute-start.11 = (bf16[192,256]{1,0:T(8,128)(2,1)S(1)}, bf16[192,256]{1,0:T(8,128)(2,1)S(1)}, u32[]{:S(2)}, u32[]{:S(2)}) collective-permute-start(bf16[192,256]{1,0:T(8,128)(2,1)S(1)} %slice.89), channel_id=1, source_target_pairs={{0,3},{1,0},{2,1},{3,2},{4,7},{5,4},{6,5},{7,6},{8,11},{9,8},{10,9... | collective-permute-start | bytes 294920 | tf_op jit(solution)/shard_map/ppermute | solution.py:235
  46.1 28.2 %collective-permute-start.4 = (bf16[1536,256]{1,0:T(8,128)(2,1)}, bf16[1536,256]{1,0:T(8,128)(2,1)S(1)}, u32[]{:S(2)}, u32[]{:S(2)}) collective-permute-start(bf16[1536,256]{1,0:T(8,128)(2,1)} %constant_dynamic-update-slice_fusion), channel_id=1, source_target_pairs={{0,1},{1,2},{2,3},{3,0},{4,5},{5,6},{6,7},{7,4},{8,9},{9,10},{10,1... | collective-permute-start | bytes 2359304 | tf_op jit(solution)/shard_map/ppermute | solution.py:235
  46.1 28.4 %collective-permute-start.6 = (bf16[1536,256]{1,0:T(8,128)(2,1)}, bf16[1536,256]{1,0:T(8,128)(2,1)S(1)}, u32[]{:S(2)}, u32[]{:S(2)}) collective-permute-start(bf16[1536,256]{1,0:T(8,128)(2,1)} %constant_dynamic-update-slice_fusion), channel_id=1, source_target_pairs={{0,3},{1,0},{2,1},{3,2},{4,7},{5,4},{6,5},{7,6},{8,11},{9,8},{10,9... | collective-permute-start | bytes 2359304 | tf_op jit(solution)/shard_map/ppermute | solution.py:235
  50.1 27.1 %collective-permute-start.12 = (bf16[1536,256]{1,0:T(8,128)(2,1)}, bf16[1536,256]{1,0:T(8,128)(2,1)S(1)}, u32[]{:S(2)}, u32[]{:S(2)}) collective-permute-start(bf16[1536,256]{1,0:T(8,128)(2,1)} %constant_dynamic-update-slice_fusion.5), channel_id=1, source_target_pairs={{0,4},{1,5},{2,6},{3,7},{4,8},{5,9},{6,10},{7,11},{8,12},{9,13},{1... | collective-permute-start | bytes 2359304 | tf_op jit(solution)/shard_map/ppermute | solution.py:235
  50.1 27.3 %collective-permute-start.14 = (bf16[1536,256]{1,0:T(8,128)(2,1)}, bf16[1536,256]{1,0:T(8,128)(2,1)S(1)}, u32[]{:S(2)}, u32[]{:S(2)}) collective-permute-start(bf16[1536,256]{1,0:T(8,128)(2,1)} %constant_dynamic-update-slice_fusion.5), channel_id=1, source_target_pairs={{0,12},{1,13},{2,14},{3,15},{4,0},{5,1},{6,2},{7,3},{8,4},{9,5},{1... | collective-permute-start | bytes 2359304 | tf_op jit(solution)/shard_map/ppermute | solution.py:235
  74.4 21.0 %collective-permute-start.5 = (bf16[768,256]{1,0:T(8,128)(2,1)S(1)}, bf16[768,256]{1,0:T(8,128)(2,1)S(1)}, u32[]{:S(2)}, u32[]{:S(2)}) collective-permute-start(bf16[768,256]{1,0:T(8,128)(2,1)S(1)} %slice.85), channel_id=1, source_target_pairs={{0,1},{1,2},{2,3},{3,0},{4,5},{5,6},{6,7},{7,4},{8,9},{9,10},{10,1... | collective-permute-start | bytes 1179656 | tf_op jit(solution)/shard_map/ppermute | solution.py:235
  74.5 20.9 %collective-permute-start.7 = (bf16[768,256]{1,0:T(8,128)(2,1)S(1)}, bf16[768,256]{1,0:T(8,128)(2,1)S(1)}, u32[]{:S(2)}, u32[]{:S(2)}) collective-permute-start(bf16[768,256]{1,0:T(8,128)(2,1)S(1)} %slice.86), channel_id=1, source_target_pairs={{0,3},{1,0},{2,1},{3,2},{4,7},{5,4},{6,5},{7,6},{8,11},{9,8},{10,9... | collective-permute-start | bytes 1179656 | tf_op jit(solution)/shard_map/ppermute | solution.py:235
  77.2 19.5 %collective-permute-start.13 = (bf16[768,256]{1,0:T(8,128)(2,1)S(1)}, bf16[768,256]{1,0:T(8,128)(2,1)S(1)}, u32[]{:S(2)}, u32[]{:S(2)}) collective-permute-start(bf16[768,256]{1,0:T(8,128)(2,1)S(1)} %slice.90), channel_id=1, source_target_pairs={{0,4},{1,5},{2,6},{3,7},{4,8},{5,9},{6,10},{7,11},{8,12},{9,13},{1... | collective-permute-start | bytes 1179656 | tf_op jit(solution)/shard_map/ppermute | solution.py:235
  77.4 19.3 %collective-permute-start.15 = (bf16[768,256]{1,0:T(8,128)(2,1)S(1)}, bf16[768,256]{1,0:T(8,128)(2,1)S(1)}, u32[]{:S(2)}, u32[]{:S(2)}) collective-permute-start(bf16[768,256]{1,0:T(8,128)(2,1)S(1)} %slice.91), channel_id=1, source_target_pairs={{0,12},{1,13},{2,14},{3,15},{4,0},{5,1},{6,2},{7,3},{8,4},{9,5},{1... | collective-permute-start | bytes 1179656 | tf_op jit(solution)/shard_map/ppermute | solution.py:235
  120.6 24.9 %collective-permute-start.24 = (bf16[4,256,256]{2,1,0:T(8,128)(2,1)S(1)}, bf16[4,256,256]{2,1,0:T(8,128)(2,1)S(1)}, u32[]{:S(2)}, u32[]{:S(2)}) collective-permute-start(bf16[4,256,256]{2,1,0:T(8,128)(2,1)S(1)} %get-tuple-element.24), channel_id=1, source_target_pairs={{0,3},{1,0},{2,1},{3,2},{4,7},{5,4},{6,5},{7,6},{8,11},{9,8},{10,9... | collective-permute-start | bytes 1572872 | tf_op jit(solution)/shard_map/ppermute | solution.py:235
  121.7 25.0 %collective-permute-start.23 = (bf16[4,256,256]{2,1,0:T(8,128)(2,1)S(1)}, bf16[4,256,256]{2,1,0:T(8,128)(2,1)S(1)}, u32[]{:S(2)}, u32[]{:S(2)}) collective-permute-start(bf16[4,256,256]{2,1,0:T(8,128)(2,1)S(1)} %get-tuple-element.23), channel_id=1, source_target_pairs={{0,1},{1,2},{2,3},{3,0},{4,5},{5,6},{6,7},{7,4},{8,9},{9,10},{10,1... | collective-permute-start | bytes 1572872 | tf_op jit(solution)/shard_map/ppermute | solution.py:235
  122.1 24.7 %collective-permute-start.22 = (bf16[4,256,256]{2,1,0:T(8,128)(2,1)S(1)}, bf16[4,256,256]{2,1,0:T(8,128)(2,1)S(1)}, u32[]{:S(2)}, u32[]{:S(2)}) collective-permute-start(bf16[4,256,256]{2,1,0:T(8,128)(2,1)S(1)} %get-tuple-element.22), channel_id=1, source_target_pairs={{0,2},{1,3},{2,0},{3,1},{4,6},{5,7},{6,4},{7,5},{8,10},{9,11},{10,... | collective-permute-start | bytes 1572872 | tf_op jit(solution)/shard_map/ppermute | solution.py:235
  143.6 20.3 %collective-permute-start.18 = (bf16[4,512,256]{2,1,0:T(8,128)(2,1)S(1)}, bf16[4,512,256]{2,1,0:T(8,128)(2,1)S(1)}, u32[]{:S(2)}, u32[]{:S(2)}) collective-permute-start(bf16[4,512,256]{2,1,0:T(8,128)(2,1)S(1)} %get-tuple-element.20), channel_id=1, source_target_pairs={{0,12},{1,13},{2,14},{3,15},{4,0},{5,1},{6,2},{7,3},{8,4},{9,5},{1... | collective-permute-start | bytes 3145736 | tf_op jit(solution)/shard_map/ppermute | solution.py:235
  145.5 20.6 %collective-permute-start.17 = (bf16[4,512,256]{2,1,0:T(8,128)(2,1)S(1)}, bf16[4,512,256]{2,1,0:T(8,128)(2,1)S(1)}, u32[]{:S(2)}, u32[]{:S(2)}) collective-permute-start(bf16[4,512,256]{2,1,0:T(8,128)(2,1)S(1)} %get-tuple-element.19), channel_id=1, source_target_pairs={{0,4},{1,5},{2,6},{3,7},{4,8},{5,9},{6,10},{7,11},{8,12},{9,13},{1... | collective-permute-start | bytes 3145736 | tf_op jit(solution)/shard_map/ppermute | solution.py:235
  145.5 40.9 %collective-permute-start.16 = (bf16[4,512,256]{2,1,0:T(8,128)(2,1)S(1)}, bf16[4,512,256]{2,1,0:T(8,128)(2,1)S(1)}, u32[]{:S(2)}, u32[]{:S(2)}) collective-permute-start(bf16[4,512,256]{2,1,0:T(8,128)(2,1)S(1)} %get-tuple-element.18), channel_id=1, source_target_pairs={{0,8},{1,9},{2,10},{3,11},{4,12},{5,13},{6,14},{7,15},{8,0},{9,1},... | collective-permute-start | bytes 3145736 | tf_op jit(solution)/shard_map/ppermute | solution.py:235
  147.1 42.2 %collective-permute-start.27 = (bf16[256,256]{1,0:T(8,128)(2,1)S(1)}, bf16[256,256]{1,0:T(8,128)(2,1)S(1)}, u32[]{:S(2)}, u32[]{:S(2)}) collective-permute-start(bf16[256,256]{1,0:T(8,128)(2,1)S(1)} %get-tuple-element.35), channel_id=1, source_target_pairs={{0,12},{1,13},{2,14},{3,15},{4,0},{5,1},{6,2},{7,3},{8,4},{9,5},{1... | collective-permute-start | bytes 393224 | tf_op jit(solution)/shard_map/ppermute | solution.py:235
  148.6 42.3 %collective-permute-start.26 = (bf16[256,256]{1,0:T(8,128)(2,1)S(1)}, bf16[256,256]{1,0:T(8,128)(2,1)S(1)}, u32[]{:S(2)}, u32[]{:S(2)}) collective-permute-start(bf16[256,256]{1,0:T(8,128)(2,1)S(1)} %get-tuple-element.36), channel_id=1, source_target_pairs={{0,4},{1,5},{2,6},{3,7},{4,8},{5,9},{6,10},{7,11},{8,12},{9,13},{1... | collective-permute-start | bytes 393224 | tf_op jit(solution)/shard_map/ppermute | solution.py:235
  163.9 28.1 %collective-permute-start.25 = (bf16[256,256]{1,0:T(8,128)(2,1)S(1)}, bf16[256,256]{1,0:T(8,128)(2,1)S(1)}, u32[]{:S(2)}, u32[]{:S(2)}) collective-permute-start(bf16[256,256]{1,0:T(8,128)(2,1)S(1)} %get-tuple-element.34), channel_id=1, source_target_pairs={{0,8},{1,9},{2,10},{3,11},{4,12},{5,13},{6,14},{7,15},{8,0},{9,1},... | collective-permute-start | bytes 393224 | tf_op jit(solution)/shard_map/ppermute | solution.py:235
  189.0 9.5 %collective-permute-start.20 = (bf16[512,256]{1,0:T(8,128)(2,1)S(1)}, bf16[512,256]{1,0:T(8,128)(2,1)S(1)}, u32[]{:S(2)}, u32[]{:S(2)}) collective-permute-start(bf16[512,256]{1,0:T(8,128)(2,1)S(1)} %get-tuple-element.31), channel_id=1, source_target_pairs={{0,1},{1,2},{2,3},{3,0},{4,5},{5,6},{6,7},{7,4},{8,9},{9,10},{10,1... | collective-permute-start | bytes 786440 | tf_op jit(solution)/shard_map/ppermute | solution.py:235
  189.2 9.3 %collective-permute-start.19 = (bf16[512,256]{1,0:T(8,128)(2,1)S(1)}, bf16[512,256]{1,0:T(8,128)(2,1)S(1)}, u32[]{:S(2)}, u32[]{:S(2)}) collective-permute-start(bf16[512,256]{1,0:T(8,128)(2,1)S(1)} %get-tuple-element.29), channel_id=1, source_target_pairs={{0,2},{1,3},{2,0},{3,1},{4,6},{5,7},{6,4},{7,5},{8,10},{9,11},{10,... | collective-permute-start | bytes 786440 | tf_op jit(solution)/shard_map/ppermute | solution.py:235
  (14 other events, 131.4 us)
Sparse Core Ops, SparseCore 0:
  28.2 77.2 all-gather.1

commit v2 on v1

v2 whole, which is shorter than its diff:
```python
import functools

import jax
import jax.numpy as jnp
import numpy as np
from jax import lax
from jax.experimental import pallas as pl
from jax.experimental.pallas import tpu as pltpu
from jax.sharding import PartitionSpec as P


BF = jnp.bfloat16
F32 = jnp.float32
SIDE = 4
TP = SIDE * SIDE
ROWS_BY_ROWS = (((1,), (1,)), ((), ()))
COLS_BY_COLS = (((0,), (0,)), ((), ()))


def flat_slots(routes, experts, capacity):
    tokens = routes.shape[1]
    first, second = routes[0:1, :], routes[1:2, :]
    expert = lax.broadcasted_iota(jnp.int32, (experts, tokens), 0)
    in_first, in_second = expert == first, expert == second
    named = jnp.where(in_first | in_second, 1.0, 0.0).astype(BF)
    earlier = lax.broadcasted_iota(jnp.int32, (tokens, tokens), 0)
    later = lax.broadcasted_iota(jnp.int32, (tokens, tokens), 1)
    before = jnp.dot(named, jnp.where(earlier < later, 1.0, 0.0).astype(BF), preferred_element_type=F32)
    place_first = jnp.sum(jnp.where(in_first, before, 0.0), axis=0, keepdims=True)
    place_second = jnp.sum(jnp.where(in_second, before, 0.0), axis=0, keepdims=True)
    return (
        first * capacity + place_first.astype(jnp.int32),
        second * capacity + place_second.astype(jnp.int32),
    )


def dispatch_body(routes, inputs, grads, out):
    experts, both, _ = out.shape
    capacity = both // 2
    tokens = inputs.shape[0]
    first, second = flat_slots(routes[...], experts, capacity)
    slot = lax.broadcasted_iota(jnp.int32, (experts * capacity, tokens), 0)
    pick = jnp.where((slot == first) | (slot == second), 1.0, 0.0).astype(BF)
    for at, source in ((0, inputs), (capacity, grads)):
        rows = jnp.dot(pick, source[...], preferred_element_type=F32).astype(BF)
        for e in range(experts):
            out[e, at : at + capacity] = rows[e * capacity : (e + 1) * capacity]


def combine_body(routes, shares, *refs):
    backs, out = refs[:-1], refs[-1]
    experts, part, _ = backs[0].shape
    capacity = part * len(backs)
    tokens = out.shape[0]
    first, second = flat_slots(routes[...], experts, capacity)
    slot = lax.broadcasted_iota(jnp.int32, (experts * capacity, tokens), 0)
    share = jnp.concatenate([shares[...], jnp.zeros((6, tokens), F32)], axis=0).T
    back = jnp.concatenate([ref[e] for e in range(experts) for ref in backs], axis=0)
    one = lax.dot_general(
        jnp.where(slot == first, 1.0, 0.0).astype(BF), back, COLS_BY_COLS, preferred_element_type=F32
    )
    two = lax.dot_general(
        jnp.where(slot == second, 1.0, 0.0).astype(BF), back, COLS_BY_COLS, preferred_element_type=F32
    )
    out[...] = (one * share[:, 0:1] + two * share[:, 1:2]).astype(out.dtype)


def absorb_body(x_order, g_order, *refs, first, count, last):
    per = 3 if first == 0 else 2
    pieces, refs = (refs[:per], refs[per : 2 * per]), refs[2 * per :]
    before, refs = (refs[:2], refs[2:]) if first > 0 else ((), refs)
    gate, up, down = refs[:3]
    outs, (sides, downs, rows, sides_here, downs_here) = refs[3:-5], refs[-5:]
    width, units = gate.shape[1:]
    wide = SIDE * width

    def fetch_sides(k):
        t = x_order[first * SIDE + k]
        return [
            pltpu.make_async_copy(gate.at[t], sides.at[k, :, :units], sides_here.at[0, k]),
            pltpu.make_async_copy(up.at[t], sides.at[k, :, units:], sides_here.at[1, k]),
        ]

    def fetch_downs(i, f):
        t = g_order[(first + i) * SIDE + f]
        return pltpu.make_async_copy(
            down.at[:, pl.ds(pl.multiple_of(t * width, width), width)],
            downs.at[i, :, f * width : (f + 1) * width],
            downs_here.at[i, f],
        )

    for i in range(count):
        for f in range(SIDE):
            for copy in fetch_sides(i * SIDE + f):
                copy.start()
        for f in range(SIDE):
            fetch_downs(i, f).start()
    for kind in range(2):
        blocks = [p.at[i] for p in pieces[kind] for i in range(p.shape[0])]
        for at, block in enumerate(blocks):
            s, f = at // SIDE, at % SIDE
            rows[kind, s, :, f * width : (f + 1) * width] = block[...]

    def ring(i, carry):
        for f in range(SIDE):
            for copy in fetch_sides(i * SIDE + f):
                copy.wait()
        right = sides[pl.ds(i * SIDE, SIDE)].reshape(wide, 2 * units)
        acts_part = jnp.dot(rows[0, i], right, preferred_element_type=F32)
        for f in range(SIDE):
            fetch_downs(i, f).wait()
        hidden_part = lax.dot_general(rows[1, i], downs[i], ROWS_BY_ROWS, preferred_element_type=F32)
        if last:
            form_grads(before[0][...] + acts_part, before[1][...] + hidden_part, *outs)
        else:

            @pl.when(i == 0)
            def _():
                outs[0][...] = acts_part
                outs[1][...] = hidden_part

            @pl.when(i != 0)
            def _():
                outs[0][...] += acts_part
                outs[1][...] += hidden_part

        return carry

    lax.fori_loop(0, count, ring, 0)


def form_grads(acts, hidden, *outs):
    units = hidden.shape[1]
    gate, up = acts[:, :units], acts[:, units:]
    sigma = jax.nn.sigmoid(gate)
    slope = sigma * (1.0 + gate * (1.0 - sigma))
    for_gate = (hidden * up * slope).astype(BF)
    for_up = (hidden * gate * sigma).astype(BF)
    experts = outs[0].shape[0]
    start = 0
    for out in outs:
        part = out.shape[1]
        for b in range(experts):
            here = slice(b * hidden.shape[0] // experts + start, b * hidden.shape[0] // experts + start + part)
            out[b, :, :units] = for_gate[here]
            out[b, :, units:] = for_up[here]
        start += part


def parts_body(order, grads, gate, up, *refs):
    outs, (sides, sides_here) = refs[:SIDE], refs[SIDE:]
    experts, part_rows, _ = grads.shape
    width, units = gate.shape[1:]

    def fetch(k):
        return [
            pltpu.make_async_copy(gate.at[order[k]], sides.at[k, :, :units], sides_here.at[0, k]),
            pltpu.make_async_copy(up.at[order[k]], sides.at[k, :, units:], sides_here.at[1, k]),
        ]

    for k in range(TP):
        for copy in fetch(k):
            copy.start()

    def members(j, carry):
        k = 2 * j
        for copy in fetch(k) + fetch(k + 1):
            copy.wait()
        part = lax.dot_general(
            grads[...].reshape(experts * part_rows, 2 * units),
            sides[pl.ds(k, 2)].reshape(2 * width, 2 * units),
            ROWS_BY_ROWS,
            preferred_element_type=F32,
        ).astype(BF)
        for f in range(SIDE):

            @pl.when(k // SIDE == f)
            def _():
                outs[f][k % SIDE] = part[:, :width]
                outs[f][k % SIDE + 1] = part[:, width:]

        return carry

    lax.fori_loop(0, TP // 2, members, 0)


def vmem(mebibytes):
    return pltpu.CompilerParams(vmem_limit_bytes=mebibytes << 20)


def in_hbm(*arrays):
    return [pltpu.with_memory_space_constraint(a, pltpu.HBM) for a in arrays]


def z_shift(by):
    return [(z * SIDE + y, (z + by) % SIDE * SIDE + y) for z in range(SIDE) for y in range(SIDE)]


def y_shift(by):
    return [(z * SIDE + y, z * SIDE + (y + by) % SIDE) for z in range(SIDE) for y in range(SIDE)]


def shifted(x, shift, by):
    return lax.ppermute(x, "tp", shift(by))


def ring_gather(x, shift):
    half = x.shape[0] // 2
    below = shifted(x, shift, 1)
    above = shifted(x, shift, 3)
    far_low = shifted(below[:half], shift, 1)
    far_high = shifted(above[half:], shift, 3)
    return [x, below, above, far_low, far_high]


def plane_gather(x, first, second):
    rows, width = x.shape
    line = jnp.concatenate(ring_gather(x, first), axis=0)
    return [piece.reshape(-1, rows, width) for piece in ring_gather(line, second)]


def ring_sum(far, ahead, behind, own, shift):
    total = own.astype(F32)
    for by, part in ((2, far), (1, ahead), (3, behind)):
        total = total + shifted(part.astype(BF), shift, by).astype(F32)
    return total


def body(layer_input, out_grad, route, gate_share, gate_weight, up_weight, down_weight):
    experts = lax.axis_size("ep")
    tokens, width = layer_input.shape
    choose = route.shape[1]
    capacity = tokens * choose * 3 // (2 * experts)
    slots = experts * capacity
    parts = (2 * capacity // 3, capacity // 3)
    gate_matrix, up_matrix, down_matrix = gate_weight[0], up_weight[0], down_weight[0]
    _, units = gate_matrix.shape
    routes, shares = route.T, gate_share.T

    me = lax.axis_index("tp")
    z, y = me // SIDE, me % SIDE
    away = np.array([0, SIDE - 1, 1, 2], np.int32)
    ahead = np.array([2, 1, 3, 0], np.int32)

    def plane(outer, inner, z_outer):
        outer, inner = np.repeat(outer, SIDE), np.tile(inner, SIDE)
        in_z, in_y = (outer, inner) if z_outer else (inner, outer)
        return ((z + in_z) % SIDE * SIDE + (y + in_y) % SIDE).astype(jnp.int32)

    x_order, g_order = plane(away, away, False), plane(away, away, True)
    summed_order = [plane(ahead, np.arange(SIDE), True), plane(ahead, np.arange(SIDE), False)]

    sent = pl.pallas_call(
        dispatch_body,
        out_shape=jax.ShapeDtypeStruct((experts, 2 * capacity, width), BF),
        name="dispatch",
        compiler_params=vmem(16),
    )(routes, layer_input, out_grad)
    got = lax.all_to_all(sent, "ep", split_axis=0, concat_axis=0, tiled=True)
    x = plane_gather(got[:, :capacity].reshape(slots, width), z_shift, y_shift)
    g = plane_gather(got[:, capacity:].reshape(slots, width), y_shift, z_shift)

    in_vmem = pl.BlockSpec(memory_space=pltpu.VMEM)
    in_smem = pl.BlockSpec(memory_space=pltpu.SMEM)
    stays = pl.BlockSpec(memory_space=pltpu.HBM)
    dma = pltpu.SemaphoreType.DMA
    sums = []
    for first, count in ((0, SIDE - 1), (SIDE - 1, 1)):
        last = first > 0
        which = slice(3, 5) if last else slice(0, 3)
        if last:
            outs = [jax.ShapeDtypeStruct((experts, part, 2 * units), BF) for part in parts]
        else:
            outs = [jax.ShapeDtypeStruct((slots, 2 * units), F32), jax.ShapeDtypeStruct((slots, units), F32)]
        used = [*x[which], *g[which], *sums]
        sums = pl.pallas_call(
            functools.partial(absorb_body, first=first, count=count, last=last),
            in_specs=[in_smem] * 2 + [in_vmem] * len(used) + [stays] * 3,
            out_specs=[in_vmem] * 2,
            out_shape=outs,
            scratch_shapes=[
                pltpu.VMEM((count * SIDE, width, 2 * units), BF),
                pltpu.VMEM((count, units, SIDE * width), BF),
                pltpu.VMEM((2, count, slots, SIDE * width), BF),
                dma((2, count * SIDE)),
                dma((count, SIDE)),
            ],
            name="absorb",
            compiler_params=vmem(44),
        )(
            x_order,
            g_order,
            *used,
            *in_hbm(
                gate_matrix.reshape(TP, width, units), up_matrix.reshape(TP, width, units), down_matrix
            ),
        )

    summed = []
    for h, part in enumerate(parts):
        rows = experts * part
        outs = pl.pallas_call(
            parts_body,
            in_specs=[in_smem, in_vmem] + [stays] * 2,
            out_specs=[in_vmem] * SIDE,
            out_shape=[jax.ShapeDtypeStruct((SIDE, rows, width), BF)] * SIDE,
            scratch_shapes=[pltpu.VMEM((TP, width, 2 * units), BF), dma((2, TP))],
            name="parts",
            compiler_params=vmem(32),
        )(summed_order[h], sums[h], *in_hbm(gate_matrix.reshape(TP, width, units), up_matrix.reshape(TP, width, units)))
        first, second = (z_shift, y_shift) if h == 0 else (y_shift, z_shift)
        line = ring_sum(*outs, first)
        mine = ring_sum(line[2], line[1], line[3], line[0], second)
        summed.append(mine.astype(BF).reshape(experts, part, width))
    backs = [
        lax.all_to_all(jnp.concatenate(summed, axis=1), "ep", split_axis=0, concat_axis=0, tiled=True)
    ]

    return pl.pallas_call(
        combine_body,
        out_shape=jax.ShapeDtypeStruct((tokens, width), BF),
        name="combine",
        compiler_params=vmem(16),
    )(routes, shares, *backs)


def solution(mesh):
    return jax.shard_map(
        body,
        mesh=mesh,
        in_specs=(
            P("ep", "tp"),
            P("ep", "tp"),
            P("ep", None),
            P("ep", None),
            P("ep", None, "tp"),
            P("ep", None, "tp"),
            P("ep", "tp", None),
        ),
        out_specs=P("ep", "tp"),
        check_vma=False,
    )
```

time: 231 us -> 230 us (level)
  waiting for transfers between devices: 46.9 us -> 94.2 us
  Pallas kernels: 82 us -> 56.7 us
  between operations: 13.7 us -> 0.39 us
  blocking collectives: 41.2 us -> 28.6 us
  local copies, waits for them, and re-layouts: 10.3 us -> 14.3 us
    ppermute x28, waiting for transfers between devices: 46.1 us -> 94.2 us  [shifted(): return lax.ppermute(x, 'tp', shift(by))]
    pallas_call x5 -> x4, Pallas kernels: 80.2 us -> 54.9 us  [the longest x2 34.9 us: body(): pl.pallas_call(functools.partial(absorb_body, first=first, count=count, l...]
    all_to_all x1, blocking collectives: 23.5 us -> 10.9 us  [body(): lax.all_to_all(jnp.concatenate(summed, axis=1), 'ep', split_axis=0, conca...]
    unnamed x26 -> x44, local copies, waits for them, and re-layouts: 7.99 us -> 10.1 us
  transfers between devices with their start and end apart: 29 -> 28, of which waited for: 9 -> 8; matrix products, arithmetic and copies ran while one was open for 3% -> 2% of each run, Pallas kernels for 28% -> 15%
where the time goes in v2:
time: 230 us
  waiting for transfers between devices  94.2 us (41%)
  Pallas kernels  56.7 us (25%)
  starting transfers between devices  34.6 us (15%)
  blocking collectives  28.6 us (12%)
  local copies, waits for them, and re-layouts  14.3 us (6%)
    ppermute x28, waiting for transfers between devices, shifted(): return lax.ppermute(x, 'tp', shift(by))  94.2 us
    pallas_call x2, Pallas kernels, body(): pl.pallas_call(functools.partial(absorb_body, first=first, count=count, l...  34.9 us
    ppermute x28, starting transfers between devices, shifted(): return lax.ppermute(x, 'tp', shift(by))  34.6 us
    pallas_call x2, Pallas kernels, body(): pl.pallas_call(parts_body, in_specs=[in_smem, in_vmem] + [stays] * 2, out...  20 us
    all_to_all x1, blocking collectives, body(): got = lax.all_to_all(sent, 'ep', split_axis=0, concat_axis=0, tiled=True)  17.7 us
    all_to_all x1, blocking collectives, body(): lax.all_to_all(jnp.concatenate(summed, axis=1), 'ep', split_axis=0, conca...  10.9 us
    unnamed x44, local copies, waits for them, and re-layouts  10.1 us
  transfers between devices with their start and end apart: 28, of which 8 were waited for; matrix products, arithmetic and copies ran while one was open for 2% of the time, Pallas kernels for 15%

profile of v2, /device:TPU:1, one launch (start us, length us, event | category | flops | bytes accessed | tf_op | source)
XLA Modules:
  0.0 229.8 jit_solution(5141296525644016652)
XLA Ops:
  3.0 17.7 %all_to_all.10 = bf16[8,192,256]{2,1,0:T(8,128)(2,1)S(1)} all-to-all(bf16[8,192,256]{2,1,0:T(8,128)(2,1)S(1)} %dispatch.1), channel_id=1, replica_groups=mesh['ep'=8,'tp'=16] {'ep'}, dimensions={0} | all-to-all | bytes 1572864 | tf_op jit(solution)/shard_map/all_to_all | solution.py:259
  25.3 2.1 collective-permute-start.1
  27.5 4.3 %collective-permute-done.8 = bf16[768,256]{1,0:T(8,128)(2,1)S(1)} collective-permute-done((bf16[768,256]{1,0:T(8,128)(2,1)S(1)}, bf16[768,256]{1,0:T(8,128)(2,1)S(1)}, u32[]{:S(2)}, u32[]{:S(2)}) %collective-permute-start.8) | collective-permute-done | bytes 393248 | tf_op jit(solution)/shard_map/ppermute | solution.py:204
  32.0 2.7 %collective-permute-start.11 = (bf16[384,256]{1,0:T(8,128)(2,1)S(1)}, bf16[384,256]{1,0:T(8,128)(2,1)S(1)}, u32[]{:S(2)}, u32[]{:S(2)}) collective-permute-start(bf16[384,256]{1,0:T(8,128)(2,1)S(1)} %slice.85), channel_id=1, source_target_pairs={{0,3},{1,0},{2,1},{3,2},{4,7},{5,4},{6,5},{7,6},{8,11},{9,8},{10,9... | collective-permute-start | bytes 589832 | tf_op jit(solution)/shard_map/ppermute | solution.py:204
  36.4 2.2 collective-permute-start.3
  39.4 2.2 collective-permute-start.14
  42.2 2.4 %collective-permute-start.6 = (bf16[3072,256]{1,0:T(8,128)(2,1)S(1)}, bf16[3072,256]{1,0:T(8,128)(2,1)S(1)}, u32[]{:S(2)}, u32[]{:S(2)}) collective-permute-start(bf16[3072,256]{1,0:T(8,128)(2,1)S(1)} %constant_dynamic-update-slice_fusion), channel_id=1, source_target_pairs={{0,3},{1,0},{2,1},{3,2},{4,7},{5,4},{6,5},{7,6},{8,11},{9,8},{10,9... | collective-permute-start | bytes 4718600 | tf_op jit(solution)/shard_map/ppermute | solution.py:204
  44.6 32.0 %collective-permute-done.12 = bf16[3072,256]{1,0:T(8,128)(2,1)S(1)} collective-permute-done((bf16[3072,256]{1,0:T(8,128)(2,1)S(1)}, bf16[3072,256]{1,0:T(8,128)(2,1)S(1)}, u32[]{:S(2)}, u32[]{:S(2)}) %collective-permute-start.12) | collective-permute-done | bytes 1572896 | tf_op jit(solution)/shard_map/ppermute | solution.py:204
  78.5 2.7 %collective-permute-start.15 = (bf16[1536,256]{1,0:T(8,128)(2,1)}, bf16[1536,256]{1,0:T(8,128)(2,1)}, u32[]{:S(2)}, u32[]{:S(2)}) collective-permute-start(bf16[1536,256]{1,0:T(8,128)(2,1)} %slice.87), channel_id=1, source_target_pairs={{0,12},{1,13},{2,14},{3,15},{4,0},{5,1},{6,2},{7,3},{8,4},{9,5},{1... | collective-permute-start | bytes 2359304 | tf_op jit(solution)/shard_map/ppermute | solution.py:204
  83.3 2.7 %collective-permute-start.7 = (bf16[1536,256]{1,0:T(8,128)(2,1)}, bf16[1536,256]{1,0:T(8,128)(2,1)}, u32[]{:S(2)}, u32[]{:S(2)}) collective-permute-start(bf16[1536,256]{1,0:T(8,128)(2,1)} %slice.82), channel_id=1, source_target_pairs={{0,3},{1,0},{2,1},{3,2},{4,7},{5,4},{6,5},{7,6},{8,11},{9,8},{10,9... | collective-permute-start | bytes 2359304 | tf_op jit(solution)/shard_map/ppermute | solution.py:204
  91.7 22.8 %absorb.2 = (f32[768,1792]{1,0:T(8,128)}, f32[768,896]{1,0:T(8,128)}) custom-call(s32[16]{0:T(128)S(1)} %get-tuple-element.44.x_order, s32[16]{0:T(128)S(1)} %get-tuple-element.43.g_order, bf16[4,768,256]{2,1,0:T(8,128)(2,1)S(1)} %bitcast.55, bf16[4,768,256]{2,1,0:T(8,128)(2,1)S(1)} %bitcast.53, bf16[4,768,256]{2,1,0:T(8,128)(2,1)S(1)} %bitcast.54, ...), custom_call_target="tpu_custom_call" | custom-call | tf_op jit(solution)/shard_map/absorb/pallas_call | solution.py:276
  114.5 1.8 copy-done.4
  116.3 12.1 %absorb.3 = (bf16[8,64,1792]{2,1,0:T(8,128)(2,1)S(1)}, bf16[8,32,1792]{2,1,0:T(8,128)(2,1)S(1)}) custom-call(s32[16]{0:T(128)S(1)} %get-tuple-element.44.x_order, s32[16]{0:T(128)S(1)} %get-tuple-element.43.g_order, bf16[2,768,256]{2,1,0:T(8,128)(2,1)} %bitcast.3.refs_0_, bf16[2,768,256]{2,1,0:T(8,128)(2,1)} %bitcast.4.refs_1_, ...), custom_call_target="tpu_custom_call" | custom-call | tf_op jit(solution)/shard_map/absorb/pallas_call | solution.py:276
  128.4 8.0 %parts.3 = (bf16[4,256,256]{2,1,0:T(8,128)(2,1)S(1)}, bf16[4,256,256]{2,1,0:T(8,128)(2,1)S(1)}, bf16[4,256,256]{2,1,0:T(8,128)(2,1)S(1)}, bf16[4,256,256]{2,1,0:T(8,128)(2,1)S(1)}) custom-call(s32[16]{0:T(128)S(1)} %get-tuple-element.42.order, bf16[8,32,1792]{2,1,0:T(8,128)(2,1)S(1)} %get-tuple-element.24.grads, bf16[16,256,896]{2,1,0:T(8,128)(2,1)} %bitcast.62, ...), custom_call_target="tpu_custom_call" | custom-call | tf_op jit(solution)/shard_map/parts/pallas_call | solution.py:302
  137.4 1.8 collective-permute-start.24
  139.3 12.0 %parts.2 = (bf16[4,512,256]{2,1,0:T(8,128)(2,1)S(1)}, bf16[4,512,256]{2,1,0:T(8,128)(2,1)S(1)}, bf16[4,512,256]{2,1,0:T(8,128)(2,1)S(1)}, bf16[4,512,256]{2,1,0:T(8,128)(2,1)S(1)}) custom-call(s32[16]{0:T(128)S(1)} %get-tuple-element.41.order, bf16[8,64,1792]{2,1,0:T(8,128)(2,1)S(1)} %get-tuple-element.19.grads, bf16[16,256,896]{2,1,0:T(8,128)(2,1)} %bitcast.63, ...), custom_call_target="tpu_custom_call" | custom-call | tf_op jit(solution)/shard_map/parts/pallas_call | solution.py:302
  152.1 2.0 collective-permute-start.18
  154.1 8.6 %collective-permute-done.23 = bf16[4,256,256]{2,1,0:T(8,128)(2,1)S(1)} collective-permute-done((bf16[4,256,256]{2,1,0:T(8,128)(2,1)S(1)}, bf16[4,256,256]{2,1,0:T(8,128)(2,1)S(1)}, u32[]{:S(2)}, u32[]{:S(2)}) %collective-permute-start.23) | collective-permute-done | bytes 524320 | tf_op jit(solution)/shard_map/ppermute | solution.py:204
  163.8 10.0 %collective-permute-done.16 = bf16[4,512,256]{2,1,0:T(8,128)(2,1)S(1)} collective-permute-done((bf16[4,512,256]{2,1,0:T(8,128)(2,1)S(1)}, bf16[4,512,256]{2,1,0:T(8,128)(2,1)S(1)}, u32[]{:S(2)}, u32[]{:S(2)}) %collective-permute-start.16) | collective-permute-done | bytes 1048608 | tf_op jit(solution)/shard_map/ppermute | solution.py:204
  173.8 27.6 %collective-permute-done.17 = bf16[4,512,256]{2,1,0:T(8,128)(2,1)S(1)} collective-permute-done((bf16[4,512,256]{2,1,0:T(8,128)(2,1)S(1)}, bf16[4,512,256]{2,1,0:T(8,128)(2,1)S(1)}, u32[]{:S(2)}, u32[]{:S(2)}) %collective-permute-start.17) | collective-permute-done | bytes 1048608 | tf_op jit(solution)/shard_map/ppermute | solution.py:204
  203.7 2.7 %collective-permute-start.21 = (bf16[512,256]{1,0:T(8,128)(2,1)S(1)}, bf16[512,256]{1,0:T(8,128)(2,1)S(1)}, u32[]{:S(2)}, u32[]{:S(2)}) collective-permute-start(bf16[512,256]{1,0:T(8,128)(2,1)S(1)} %get-tuple-element.34), channel_id=1, source_target_pairs={{0,3},{1,0},{2,1},{3,2},{4,7},{5,4},{6,5},{7,6},{8,11},{9,8},{10,9... | collective-permute-start | bytes 786440 | tf_op jit(solution)/shard_map/ppermute | solution.py:204
  206.5 4.0 %collective-permute-done.19 = bf16[512,256]{1,0:T(8,128)(2,1)S(1)} collective-permute-done((bf16[512,256]{1,0:T(8,128)(2,1)S(1)}, bf16[512,256]{1,0:T(8,128)(2,1)S(1)}, u32[]{:S(2)}, u32[]{:S(2)}) %collective-permute-start.19) | collective-permute-done | bytes 262176 | tf_op jit(solution)/shard_map/ppermute | solution.py:204
  210.5 7.0 %collective-permute-done.20 = bf16[512,256]{1,0:T(8,128)(2,1)S(1)} collective-permute-done((bf16[512,256]{1,0:T(8,128)(2,1)S(1)}, bf16[512,256]{1,0:T(8,128)(2,1)S(1)}, u32[]{:S(2)}, u32[]{:S(2)}) %collective-permute-start.20) | collective-permute-done | bytes 262176 | tf_op jit(solution)/shard_map/ppermute | solution.py:204
  217.6 10.9 %all_to_all.11.refs_0_ = bf16[8,96,256]{2,1,0:T(8,128)(2,1)S(1)} all-to-all(bf16[8,96,256]{2,1,0:T(8,128)(2,1)S(1)} %pad_maximum_fusion), channel_id=1, replica_groups=mesh['ep'=8,'tp'=16] {'ep'}, dimensions={0} | all-to-all | bytes 786432 | tf_op jit(solution)/shard_map/all_to_all | solution.py:316
  (104 shorter events, 27.1 us)
Async XLA Ops:
  20.8 11.0 %collective-permute-start.8 = (bf16[768,256]{1,0:T(8,128)(2,1)S(1)}, bf16[768,256]{1,0:T(8,128)(2,1)S(1)}, u32[]{:S(2)}, u32[]{:S(2)}) collective-permute-start(bf16[768,256]{1,0:T(8,128)(2,1)S(1)} %bitcast.73), channel_id=1, source_target_pairs={{0,1},{1,2},{2,3},{3,0},{4,5},{5,6},{6,7},{7,4},{8,9},{9,10},{10,1... | collective-permute-start | bytes 1179656 | tf_op jit(solution)/shard_map/ppermute | solution.py:204
  22.2 9.8 %collective-permute-start.9 = (bf16[768,256]{1,0:T(8,128)(2,1)S(1)}, bf16[768,256]{1,0:T(8,128)(2,1)S(1)}, u32[]{:S(2)}, u32[]{:S(2)}) collective-permute-start(bf16[768,256]{1,0:T(8,128)(2,1)S(1)} %bitcast.74), channel_id=1, source_target_pairs={{0,3},{1,0},{2,1},{3,2},{4,7},{5,4},{6,5},{7,6},{8,11},{9,8},{10,9... | collective-permute-start | bytes 1179656 | tf_op jit(solution)/shard_map/ppermute | solution.py:204
  23.7 11.8 %collective-permute-start = (bf16[768,256]{1,0:T(8,128)(2,1)S(1)}, bf16[768,256]{1,0:T(8,128)(2,1)S(1)}, u32[]{:S(2)}, u32[]{:S(2)}) collective-permute-start(bf16[768,256]{1,0:T(8,128)(2,1)S(1)} %bitcast.70), channel_id=1, source_target_pairs={{0,4},{1,5},{2,6},{3,7},{4,8},{5,9},{6,10},{7,11},{8,12},{9,13},{1... | collective-permute-start | bytes 1179656 | tf_op jit(solution)/shard_map/ppermute | solution.py:204
  25.3 11.1 %collective-permute-start.1 = (bf16[768,256]{1,0:T(8,128)(2,1)S(1)}, bf16[768,256]{1,0:T(8,128)(2,1)S(1)}, u32[]{:S(2)}, u32[]{:S(2)}) collective-permute-start(bf16[768,256]{1,0:T(8,128)(2,1)S(1)} %bitcast.71), channel_id=1, source_target_pairs={{0,12},{1,13},{2,14},{3,15},{4,0},{5,1},{6,2},{7,3},{8,4},{9,5},{1... | collective-permute-start | bytes 1179656 | tf_op jit(solution)/shard_map/ppermute | solution.py:204
  38.9 37.7 %collective-permute-start.12 = (bf16[3072,256]{1,0:T(8,128)(2,1)S(1)}, bf16[3072,256]{1,0:T(8,128)(2,1)S(1)}, u32[]{:S(2)}, u32[]{:S(2)}) collective-permute-start(bf16[3072,256]{1,0:T(8,128)(2,1)S(1)} %constant_dynamic-update-slice_fusion.5), channel_id=1, source_target_pairs={{0,4},{1,5},{2,6},{3,7},{4,8},{5,9},{6,10},{7,11},{8,12},{9,13},{1... | collective-permute-start | bytes 4718600 | tf_op jit(solution)/shard_map/ppermute | solution.py:204
  39.4 38.1 %collective-permute-start.14 = (bf16[3072,256]{1,0:T(8,128)(2,1)S(1)}, bf16[3072,256]{1,0:T(8,128)(2,1)S(1)}, u32[]{:S(2)}, u32[]{:S(2)}) collective-permute-start(bf16[3072,256]{1,0:T(8,128)(2,1)S(1)} %constant_dynamic-update-slice_fusion.5), channel_id=1, source_target_pairs={{0,12},{1,13},{2,14},{3,15},{4,0},{5,1},{6,2},{7,3},{8,4},{9,5},{1... | collective-permute-start | bytes 4718600 | tf_op jit(solution)/shard_map/ppermute | solution.py:204
  41.7 39.6 %collective-permute-start.4 = (bf16[3072,256]{1,0:T(8,128)(2,1)S(1)}, bf16[3072,256]{1,0:T(8,128)(2,1)S(1)}, u32[]{:S(2)}, u32[]{:S(2)}) collective-permute-start(bf16[3072,256]{1,0:T(8,128)(2,1)S(1)} %constant_dynamic-update-slice_fusion), channel_id=1, source_target_pairs={{0,1},{1,2},{2,3},{3,0},{4,5},{5,6},{6,7},{7,4},{8,9},{9,10},{10,1... | collective-permute-start | bytes 4718600 | tf_op jit(solution)/shard_map/ppermute | solution.py:204
  42.2 40.1 %collective-permute-start.6 = (bf16[3072,256]{1,0:T(8,128)(2,1)S(1)}, bf16[3072,256]{1,0:T(8,128)(2,1)S(1)}, u32[]{:S(2)}, u32[]{:S(2)}) collective-permute-start(bf16[3072,256]{1,0:T(8,128)(2,1)S(1)} %constant_dynamic-update-slice_fusion), channel_id=1, source_target_pairs={{0,3},{1,0},{2,1},{3,2},{4,7},{5,4},{6,5},{7,6},{8,11},{9,8},{10,9... | collective-permute-start | bytes 4718600 | tf_op jit(solution)/shard_map/ppermute | solution.py:204
  77.5 37.0 %collective-permute-start.13 = (bf16[1536,256]{1,0:T(8,128)(2,1)}, bf16[1536,256]{1,0:T(8,128)(2,1)}, u32[]{:S(2)}, u32[]{:S(2)}) collective-permute-start(bf16[1536,256]{1,0:T(8,128)(2,1)} %slice.86), channel_id=1, source_target_pairs={{0,4},{1,5},{2,6},{3,7},{4,8},{5,9},{6,10},{7,11},{8,12},{9,13},{1... | collective-permute-start | bytes 2359304 | tf_op jit(solution)/shard_map/ppermute | solution.py:204
  78.5 36.0 %collective-permute-start.15 = (bf16[1536,256]{1,0:T(8,128)(2,1)}, bf16[1536,256]{1,0:T(8,128)(2,1)}, u32[]{:S(2)}, u32[]{:S(2)}) collective-permute-start(bf16[1536,256]{1,0:T(8,128)(2,1)} %slice.87), channel_id=1, source_target_pairs={{0,12},{1,13},{2,14},{3,15},{4,0},{5,1},{6,2},{7,3},{8,4},{9,5},{1... | collective-permute-start | bytes 2359304 | tf_op jit(solution)/shard_map/ppermute | solution.py:204
  82.3 32.2 %collective-permute-start.5 = (bf16[1536,256]{1,0:T(8,128)(2,1)}, bf16[1536,256]{1,0:T(8,128)(2,1)}, u32[]{:S(2)}, u32[]{:S(2)}) collective-permute-start(bf16[1536,256]{1,0:T(8,128)(2,1)} %slice.81), channel_id=1, source_target_pairs={{0,1},{1,2},{2,3},{3,0},{4,5},{5,6},{6,7},{7,4},{8,9},{9,10},{10,1... | collective-permute-start | bytes 2359304 | tf_op jit(solution)/shard_map/ppermute | solution.py:204
  83.3 31.2 %collective-permute-start.7 = (bf16[1536,256]{1,0:T(8,128)(2,1)}, bf16[1536,256]{1,0:T(8,128)(2,1)}, u32[]{:S(2)}, u32[]{:S(2)}) collective-permute-start(bf16[1536,256]{1,0:T(8,128)(2,1)} %slice.82), channel_id=1, source_target_pairs={{0,3},{1,0},{2,1},{3,2},{4,7},{5,4},{6,5},{7,6},{8,11},{9,8},{10,9... | collective-permute-start | bytes 2359304 | tf_op jit(solution)/shard_map/ppermute | solution.py:204
  136.4 15.7 %collective-permute-start.22 = (bf16[4,256,256]{2,1,0:T(8,128)(2,1)S(1)}, bf16[4,256,256]{2,1,0:T(8,128)(2,1)S(1)}, u32[]{:S(2)}, u32[]{:S(2)}) collective-permute-start(bf16[4,256,256]{2,1,0:T(8,128)(2,1)S(1)} %get-tuple-element.26), channel_id=1, source_target_pairs={{0,2},{1,3},{2,0},{3,1},{4,6},{5,7},{6,4},{7,5},{8,10},{9,11},{10,... | collective-permute-start | bytes 1572872 | tf_op jit(solution)/shard_map/ppermute | solution.py:204
  136.5 26.1 %collective-permute-start.23 = (bf16[4,256,256]{2,1,0:T(8,128)(2,1)S(1)}, bf16[4,256,256]{2,1,0:T(8,128)(2,1)S(1)}, u32[]{:S(2)}, u32[]{:S(2)}) collective-permute-start(bf16[4,256,256]{2,1,0:T(8,128)(2,1)S(1)} %get-tuple-element.27), channel_id=1, source_target_pairs={{0,1},{1,2},{2,3},{3,0},{4,5},{5,6},{6,7},{7,4},{8,9},{9,10},{10,1... | collective-permute-start | bytes 1572872 | tf_op jit(solution)/shard_map/ppermute | solution.py:204
  137.4 25.2 %collective-permute-start.24 = (bf16[4,256,256]{2,1,0:T(8,128)(2,1)S(1)}, bf16[4,256,256]{2,1,0:T(8,128)(2,1)S(1)}, u32[]{:S(2)}, u32[]{:S(2)}) collective-permute-start(bf16[4,256,256]{2,1,0:T(8,128)(2,1)S(1)} %get-tuple-element.28), channel_id=1, source_target_pairs={{0,3},{1,0},{2,1},{3,2},{4,7},{5,4},{6,5},{7,6},{8,11},{9,8},{10,9... | collective-permute-start | bytes 1572872 | tf_op jit(solution)/shard_map/ppermute | solution.py:204
  151.3 22.6 %collective-permute-start.16 = (bf16[4,512,256]{2,1,0:T(8,128)(2,1)S(1)}, bf16[4,512,256]{2,1,0:T(8,128)(2,1)S(1)}, u32[]{:S(2)}, u32[]{:S(2)}) collective-permute-start(bf16[4,512,256]{2,1,0:T(8,128)(2,1)S(1)} %get-tuple-element.21), channel_id=1, source_target_pairs={{0,8},{1,9},{2,10},{3,11},{4,12},{5,13},{6,14},{7,15},{8,0},{9,1},... | collective-permute-start | bytes 3145736 | tf_op jit(solution)/shard_map/ppermute | solution.py:204
  151.4 50.0 %collective-permute-start.17 = (bf16[4,512,256]{2,1,0:T(8,128)(2,1)S(1)}, bf16[4,512,256]{2,1,0:T(8,128)(2,1)S(1)}, u32[]{:S(2)}, u32[]{:S(2)}) collective-permute-start(bf16[4,512,256]{2,1,0:T(8,128)(2,1)S(1)} %get-tuple-element.22), channel_id=1, source_target_pairs={{0,4},{1,5},{2,6},{3,7},{4,8},{5,9},{6,10},{7,11},{8,12},{9,13},{1... | collective-permute-start | bytes 3145736 | tf_op jit(solution)/shard_map/ppermute | solution.py:204
  152.1 49.3 %collective-permute-start.18 = (bf16[4,512,256]{2,1,0:T(8,128)(2,1)S(1)}, bf16[4,512,256]{2,1,0:T(8,128)(2,1)S(1)}, u32[]{:S(2)}, u32[]{:S(2)}) collective-permute-start(bf16[4,512,256]{2,1,0:T(8,128)(2,1)S(1)} %get-tuple-element.23), channel_id=1, source_target_pairs={{0,12},{1,13},{2,14},{3,15},{4,0},{5,1},{6,2},{7,3},{8,4},{9,5},{1... | collective-permute-start | bytes 3145736 | tf_op jit(solution)/shard_map/ppermute | solution.py:204
  163.0 40.8 %collective-permute-start.25 = (bf16[256,256]{1,0:T(8,128)(2,1)S(1)}, bf16[256,256]{1,0:T(8,128)(2,1)S(1)}, u32[]{:S(2)}, u32[]{:S(2)}) collective-permute-start(bf16[256,256]{1,0:T(8,128)(2,1)S(1)} %get-tuple-element.38), channel_id=1, source_target_pairs={{0,8},{1,9},{2,10},{3,11},{4,12},{5,13},{6,14},{7,15},{8,0},{9,1},... | collective-permute-start | bytes 393224 | tf_op jit(solution)/shard_map/ppermute | solution.py:204
  163.1 43.4 %collective-permute-start.26 = (bf16[256,256]{1,0:T(8,128)(2,1)S(1)}, bf16[256,256]{1,0:T(8,128)(2,1)S(1)}, u32[]{:S(2)}, u32[]{:S(2)}) collective-permute-start(bf16[256,256]{1,0:T(8,128)(2,1)S(1)} %get-tuple-element.40), channel_id=1, source_target_pairs={{0,4},{1,5},{2,6},{3,7},{4,8},{5,9},{6,10},{7,11},{8,12},{9,13},{1... | collective-permute-start | bytes 393224 | tf_op jit(solution)/shard_map/ppermute | solution.py:204
  173.8 32.6 %collective-permute-start.27 = (bf16[256,256]{1,0:T(8,128)(2,1)S(1)}, bf16[256,256]{1,0:T(8,128)(2,1)S(1)}, u32[]{:S(2)}, u32[]{:S(2)}) collective-permute-start(bf16[256,256]{1,0:T(8,128)(2,1)S(1)} %get-tuple-element.39), channel_id=1, source_target_pairs={{0,12},{1,13},{2,14},{3,15},{4,0},{5,1},{6,2},{7,3},{8,4},{9,5},{1... | collective-permute-start | bytes 393224 | tf_op jit(solution)/shard_map/ppermute | solution.py:204
  202.0 8.5 %collective-permute-start.19 = (bf16[512,256]{1,0:T(8,128)(2,1)S(1)}, bf16[512,256]{1,0:T(8,128)(2,1)S(1)}, u32[]{:S(2)}, u32[]{:S(2)}) collective-permute-start(bf16[512,256]{1,0:T(8,128)(2,1)S(1)} %get-tuple-element.33), channel_id=1, source_target_pairs={{0,2},{1,3},{2,0},{3,1},{4,6},{5,7},{6,4},{7,5},{8,10},{9,11},{10,... | collective-permute-start | bytes 786440 | tf_op jit(solution)/shard_map/ppermute | solution.py:204
  203.7 13.7 %collective-permute-start.20 = (bf16[512,256]{1,0:T(8,128)(2,1)S(1)}, bf16[512,256]{1,0:T(8,128)(2,1)S(1)}, u32[]{:S(2)}, u32[]{:S(2)}) collective-permute-start(bf16[512,256]{1,0:T(8,128)(2,1)S(1)} %get-tuple-element.35), channel_id=1, source_target_pairs={{0,1},{1,2},{2,3},{3,0},{4,5},{5,6},{6,7},{7,4},{8,9},{9,10},{10,1... | collective-permute-start | bytes 786440 | tf_op jit(solution)/shard_map/ppermute | solution.py:204
  203.7 13.7 %collective-permute-start.21 = (bf16[512,256]{1,0:T(8,128)(2,1)S(1)}, bf16[512,256]{1,0:T(8,128)(2,1)S(1)}, u32[]{:S(2)}, u32[]{:S(2)}) collective-permute-start(bf16[512,256]{1,0:T(8,128)(2,1)S(1)} %get-tuple-element.34), channel_id=1, source_target_pairs={{0,3},{1,0},{2,1},{3,2},{4,7},{5,4},{6,5},{7,6},{8,11},{9,8},{10,9... | collective-permute-start | bytes 786440 | tf_op jit(solution)/shard_map/ppermute | solution.py:204
  (22 other events, 169.5 us)

commit v3 on v2

--- a/solution.py
+++ b/solution.py
@@ -66,11 +66,11 @@
 
 
 def absorb_body(x_order, g_order, *refs, first, count, last):
-    per = 3 if first == 0 else 2
+    per = 2 if last else count
     pieces, refs = (refs[:per], refs[per : 2 * per]), refs[2 * per :]
     before, refs = (refs[:2], refs[2:]) if first > 0 else ((), refs)
     gate, up, down = refs[:3]
-    outs, (sides, downs, rows, sides_here, downs_here) = refs[3:-5], refs[-5:]
+    outs, (sides, downs, sides_here, downs_here), rows = refs[3:5], refs[5:9], refs[9:]
     width, units = gate.shape[1:]
     wide = SIDE * width
 
@@ -95,29 +95,38 @@
                 copy.start()
         for f in range(SIDE):
             fetch_downs(i, f).start()
-    for kind in range(2):
-        blocks = [p.at[i] for p in pieces[kind] for i in range(p.shape[0])]
-        for at, block in enumerate(blocks):
-            s, f = at // SIDE, at % SIDE
-            rows[kind, s, :, f * width : (f + 1) * width] = block[...]
+    blocks = [[p.at[i] for p in pieces[kind] for i in range(p.shape[0])] for kind in range(2)]
+    if count > 1:
+        for kind in range(2):
+            for at, block in enumerate(blocks[kind]):
+                s, f = at // SIDE, at % SIDE
+                rows[0][kind, s, :, f * width : (f + 1) * width] = block[...]
+
+    def left(kind, i):
+        if count > 1:
+            return rows[0][kind, i]
+        return jnp.concatenate([block[...] for block in blocks[kind]], axis=1)
 
     def ring(i, carry):
         for f in range(SIDE):
             for copy in fetch_sides(i * SIDE + f):
                 copy.wait()
         right = sides[pl.ds(i * SIDE, SIDE)].reshape(wide, 2 * units)
-        acts_part = jnp.dot(rows[0, i], right, preferred_element_type=F32)
+        acts_part = jnp.dot(left(0, i), right, preferred_element_type=F32)
         for f in range(SIDE):
             fetch_downs(i, f).wait()
-        hidden_part = lax.dot_general(rows[1, i], downs[i], ROWS_BY_ROWS, preferred_element_type=F32)
+        hidden_part = lax.dot_general(left(1, i), downs[i], ROWS_BY_ROWS, preferred_element_type=F32)
         if last:
             form_grads(before[0][...] + acts_part, before[1][...] + hidden_part, *outs)
+        elif count == 1:
+            outs[0][...] = acts_part
+            outs[1][...] = hidden_part
         else:
 
             @pl.when(i == 0)
             def _():
-                outs[0][...] = acts_part
-                outs[1][...] = hidden_part
+                outs[0][...] = before[0][...] + acts_part
+                outs[1][...] = before[1][...] + hidden_part
 
             @pl.when(i != 0)
             def _():
@@ -126,7 +135,10 @@
 
         return carry
 
-    lax.fori_loop(0, count, ring, 0)
+    if count > 1:
+        lax.fori_loop(0, count, ring, 0)
+    else:
+        ring(0, 0)
 
 
 def form_grads(acts, hidden, *outs):
@@ -134,16 +146,16 @@
     gate, up = acts[:, :units], acts[:, units:]
     sigma = jax.nn.sigmoid(gate)
     slope = sigma * (1.0 + gate * (1.0 - sigma))
-    for_gate = (hidden * up * slope).astype(BF)
-    for_up = (hidden * gate * sigma).astype(BF)
+    for_gate = hidden * up * slope
+    for_up = hidden * gate * sigma
     experts = outs[0].shape[0]
     start = 0
     for out in outs:
         part = out.shape[1]
         for b in range(experts):
             here = slice(b * hidden.shape[0] // experts + start, b * hidden.shape[0] // experts + start + part)
-            out[b, :, :units] = for_gate[here]
-            out[b, :, units:] = for_up[here]
+            out[b, :, :units] = for_gate[here].astype(BF)
+            out[b, :, units:] = for_up[here].astype(BF)
         start += part
 
 
@@ -232,7 +244,7 @@
     choose = route.shape[1]
     capacity = tokens * choose * 3 // (2 * experts)
     slots = experts * capacity
-    parts = (2 * capacity // 3, capacity // 3)
+    parts = (7 * capacity // 12, 5 * capacity // 12)
     gate_matrix, up_matrix, down_matrix = gate_weight[0], up_weight[0], down_weight[0]
     _, units = gate_matrix.shape
     routes, shares = route.T, gate_share.T
@@ -265,9 +277,8 @@
     stays = pl.BlockSpec(memory_space=pltpu.HBM)
     dma = pltpu.SemaphoreType.DMA
     sums = []
-    for first, count in ((0, SIDE - 1), (SIDE - 1, 1)):
-        last = first > 0
-        which = slice(3, 5) if last else slice(0, 3)
+    for first, count, which, limit in ((0, 1, slice(0, 1), 28), (1, 2, slice(1, 3), 34), (3, 1, slice(3, 5), 28)):
+        last = first + count == SIDE
         if last:
             outs = [jax.ShapeDtypeStruct((experts, part, 2 * units), BF) for part in parts]
         else:
@@ -281,12 +292,12 @@
             scratch_shapes=[
                 pltpu.VMEM((count * SIDE, width, 2 * units), BF),
                 pltpu.VMEM((count, units, SIDE * width), BF),
-                pltpu.VMEM((2, count, slots, SIDE * width), BF),
                 dma((2, count * SIDE)),
                 dma((count, SIDE)),
-            ],
+            ]
+            + [pltpu.VMEM((2, count, slots, SIDE * width), BF)] * (count > 1),
             name="absorb",
-            compiler_params=vmem(44),
+            compiler_params=vmem(limit),
         )(
             x_order,
             g_order,

time: 230 us -> 222 us (0.965)
  waiting for transfers between devices: 94.2 us -> 85.9 us
    ppermute x28, waiting for transfers between devices: 94.2 us -> 85.9 us  [shifted(): return lax.ppermute(x, 'tp', shift(by))]
    pallas_call x2 -> x3, Pallas kernels: 34.9 us -> 35.6 us  [body(): pl.pallas_call(functools.partial(absorb_body, first=first, count=count, l...]
  transfers between devices with their start and end apart: 28 -> 28, of which waited for: 8 -> 10; matrix products, arithmetic and copies ran while one was open for 2% -> 2% of each run, Pallas kernels for 15% -> 16%
where the time goes in v3:
time: 222 us
  waiting for transfers between devices  85.9 us (39%)
  Pallas kernels  57.3 us (26%)
  starting transfers between devices  36 us (16%)
  blocking collectives  28.6 us (13%)
  local copies, waits for them, and re-layouts  12.2 us (5%)
    ppermute x28, waiting for transfers between devices, shifted(): return lax.ppermute(x, 'tp', shift(by))  85.9 us
    ppermute x28, starting transfers between devices, shifted(): return lax.ppermute(x, 'tp', shift(by))  36 us
    pallas_call x3, Pallas kernels, body(): pl.pallas_call(functools.partial(absorb_body, first=first, count=count, l...  35.6 us
    pallas_call x2, Pallas kernels, body(): pl.pallas_call(parts_body, in_specs=[in_smem, in_vmem] + [stays] * 2, out...  19.9 us
    all_to_all x1, blocking collectives, body(): got = lax.all_to_all(sent, 'ep', split_axis=0, concat_axis=0, tiled=True)  17.7 us
    all_to_all x1, blocking collectives, body(): lax.all_to_all(jnp.concatenate(summed, axis=1), 'ep', split_axis=0, conca...  10.9 us
    unnamed x44, local copies, waits for them, and re-layouts  7.97 us
  transfers between devices with their start and end apart: 28, of which 10 were waited for; matrix products, arithmetic and copies ran while one was open for 2% of the time, Pallas kernels for 16%

profile of v3, /device:TPU:1, one launch (start us, length us, event | category | flops | bytes accessed | tf_op | source)
XLA Modules:
  0.0 221.5 jit_solution(17386918713760270286)
XLA Ops:
  3.0 17.7 %all_to_all.10 = bf16[8,192,256]{2,1,0:T(8,128)(2,1)S(1)} all-to-all(bf16[8,192,256]{2,1,0:T(8,128)(2,1)S(1)} %dispatch.1), channel_id=1, replica_groups=mesh['ep'=8,'tp'=16] {'ep'}, dimensions={0} | all-to-all | bytes 1572864 | tf_op jit(solution)/shard_map/all_to_all | solution.py:271
  25.3 2.1 collective-permute-start.1
  27.5 4.3 %collective-permute-done.8 = bf16[768,256]{1,0:T(8,128)(2,1)S(1)} collective-permute-done((bf16[768,256]{1,0:T(8,128)(2,1)S(1)}, bf16[768,256]{1,0:T(8,128)(2,1)S(1)}, u32[]{:S(2)}, u32[]{:S(2)}) %collective-permute-start.8) | collective-permute-done | bytes 393248 | tf_op jit(solution)/shard_map/ppermute | solution.py:216
  32.0 2.7 %collective-permute-start.11 = (bf16[384,256]{1,0:T(8,128)(2,1)S(1)}, bf16[384,256]{1,0:T(8,128)(2,1)S(1)}, u32[]{:S(2)}, u32[]{:S(2)}) collective-permute-start(bf16[384,256]{1,0:T(8,128)(2,1)S(1)} %slice.85), channel_id=1, source_target_pairs={{0,3},{1,0},{2,1},{3,2},{4,7},{5,4},{6,5},{7,6},{8,11},{9,8},{10,9... | collective-permute-start | bytes 589832 | tf_op jit(solution)/shard_map/ppermute | solution.py:216
  36.4 2.2 collective-permute-start.3
  39.4 2.2 collective-permute-start.14
  42.2 2.4 %collective-permute-start.6 = (bf16[3072,256]{1,0:T(8,128)(2,1)S(1)}, bf16[3072,256]{1,0:T(8,128)(2,1)S(1)}, u32[]{:S(2)}, u32[]{:S(2)}) collective-permute-start(bf16[3072,256]{1,0:T(8,128)(2,1)S(1)} %constant_dynamic-update-slice_fusion), channel_id=1, source_target_pairs={{0,3},{1,0},{2,1},{3,2},{4,7},{5,4},{6,5},{7,6},{8,11},{9,8},{10,9... | collective-permute-start | bytes 4718600 | tf_op jit(solution)/shard_map/ppermute | solution.py:216
  44.6 32.0 %collective-permute-done.12 = bf16[3072,256]{1,0:T(8,128)(2,1)S(1)} collective-permute-done((bf16[3072,256]{1,0:T(8,128)(2,1)S(1)}, bf16[3072,256]{1,0:T(8,128)(2,1)S(1)}, u32[]{:S(2)}, u32[]{:S(2)}) %collective-permute-start.12) | collective-permute-done | bytes 1572896 | tf_op jit(solution)/shard_map/ppermute | solution.py:216
  78.6 2.7 %collective-permute-start.15 = (bf16[1536,256]{1,0:T(8,128)(2,1)}, bf16[1536,256]{1,0:T(8,128)(2,1)}, u32[]{:S(2)}, u32[]{:S(2)}) collective-permute-start(bf16[1536,256]{1,0:T(8,128)(2,1)} %slice.87), channel_id=1, source_target_pairs={{0,12},{1,13},{2,14},{3,15},{4,0},{5,1},{6,2},{7,3},{8,4},{9,5},{1... | collective-permute-start | bytes 2359304 | tf_op jit(solution)/shard_map/ppermute | solution.py:216
  83.4 2.7 %collective-permute-start.7 = (bf16[1536,256]{1,0:T(8,128)(2,1)}, bf16[1536,256]{1,0:T(8,128)(2,1)}, u32[]{:S(2)}, u32[]{:S(2)}) collective-permute-start(bf16[1536,256]{1,0:T(8,128)(2,1)} %slice.82), channel_id=1, source_target_pairs={{0,3},{1,0},{2,1},{3,2},{4,7},{5,4},{6,5},{7,6},{8,11},{9,8},{10,9... | collective-permute-start | bytes 2359304 | tf_op jit(solution)/shard_map/ppermute | solution.py:216
  88.9 8.5 %absorb.3 = (f32[768,1792]{1,0:T(8,128)S(1)}, f32[768,896]{1,0:T(8,128)S(1)}) custom-call(s32[16]{0:T(128)S(1)} %get-tuple-element.48.x_order, s32[16]{0:T(128)S(1)} %get-tuple-element.47.g_order, bf16[4,768,256]{2,1,0:T(8,128)(2,1)S(1)} %bitcast.55, bf16[4,768,256]{2,1,0:T(8,128)(2,1)S(1)} %bitcast.56, bf16[16,256,896]{2,1,0:T(8,128)(2,1)} %bitcast.60, ...), custom_call_target="tpu_custom_call" | custom-call | tf_op jit(solution)/shard_map/absorb/pallas_call | solution.py:287
  97.5 2.4 %copy-done = f32[768,1792]{1,0:T(8,128)} copy-done((f32[768,1792]{1,0:T(8,128)}, f32[768,1792]{1,0:T(8,128)S(1)}, u32[]{:S(2)}) %copy-start) | copy-done | bytes 5505048
  99.9 16.4 %absorb.4 = (f32[768,1792]{1,0:T(8,128)S(1)}, f32[768,896]{1,0:T(8,128)S(1)}) custom-call(s32[16]{0:T(128)S(1)} %get-tuple-element.48.x_order, s32[16]{0:T(128)S(1)} %get-tuple-element.47.g_order, bf16[4,768,256]{2,1,0:T(8,128)(2,1)S(1)} %bitcast.53, bf16[4,768,256]{2,1,0:T(8,128)(2,1)S(1)} %bitcast.54, bf16[4,768,256]{2,1,0:T(8,128)(2,1)S(1)} %bitcast.51, ...), custom_call_target="tpu_custom_call" | custom-call | tf_op jit(solution)/shard_map/absorb/pallas_call | solution.py:287
  116.3 10.6 %absorb.5 = (bf16[8,56,1792]{2,1,0:T(8,128)(2,1)S(1)}, bf16[8,40,1792]{2,1,0:T(8,128)(2,1)S(1)}) custom-call(s32[16]{0:T(128)S(1)} %get-tuple-element.48.x_order, s32[16]{0:T(128)S(1)} %get-tuple-element.47.g_order, bf16[2,768,256]{2,1,0:T(8,128)(2,1)} %bitcast.3.refs_0_, bf16[2,768,256]{2,1,0:T(8,128)(2,1)} %bitcast.4.refs_1_, ...), custom_call_target="tpu_custom_call" | custom-call | tf_op jit(solution)/shard_map/absorb/pallas_call | solution.py:287
  127.0 9.0 %parts.3 = (bf16[4,320,256]{2,1,0:T(8,128)(2,1)S(1)}, bf16[4,320,256]{2,1,0:T(8,128)(2,1)S(1)}, bf16[4,320,256]{2,1,0:T(8,128)(2,1)S(1)}, bf16[4,320,256]{2,1,0:T(8,128)(2,1)S(1)}) custom-call(s32[16]{0:T(128)S(1)} %get-tuple-element.46.order, bf16[8,40,1792]{2,1,0:T(8,128)(2,1)S(1)} %get-tuple-element.28.grads, bf16[16,256,896]{2,1,0:T(8,128)(2,1)} %bitcast.63, ...), custom_call_target="tpu_custom_call" | custom-call | tf_op jit(solution)/shard_map/parts/pallas_call | solution.py:313
  138.8 11.0 %parts.2 = (bf16[4,448,256]{2,1,0:T(8,128)(2,1)S(1)}, bf16[4,448,256]{2,1,0:T(8,128)(2,1)S(1)}, bf16[4,448,256]{2,1,0:T(8,128)(2,1)S(1)}, bf16[4,448,256]{2,1,0:T(8,128)(2,1)S(1)}) custom-call(s32[16]{0:T(128)S(1)} %get-tuple-element.45.order, bf16[8,56,1792]{2,1,0:T(8,128)(2,1)S(1)} %get-tuple-element.23.grads, bf16[16,256,896]{2,1,0:T(8,128)(2,1)} %bitcast.64, ...), custom_call_target="tpu_custom_call" | custom-call | tf_op jit(solution)/shard_map/parts/pallas_call | solution.py:313
  150.8 1.8 collective-permute-start.18
  152.6 15.2 %collective-permute-done.23 = bf16[4,320,256]{2,1,0:T(8,128)(2,1)S(1)} collective-permute-done((bf16[4,320,256]{2,1,0:T(8,128)(2,1)S(1)}, bf16[4,320,256]{2,1,0:T(8,128)(2,1)S(1)}, u32[]{:S(2)}, u32[]{:S(2)}) %collective-permute-start.23) | collective-permute-done | bytes 655392 | tf_op jit(solution)/shard_map/ppermute | solution.py:216
  171.1 23.5 %collective-permute-done.17 = bf16[4,448,256]{2,1,0:T(8,128)(2,1)S(1)} collective-permute-done((bf16[4,448,256]{2,1,0:T(8,128)(2,1)S(1)}, bf16[4,448,256]{2,1,0:T(8,128)(2,1)S(1)}, u32[]{:S(2)}, u32[]{:S(2)}) %collective-permute-start.17) | collective-permute-done | bytes 917536 | tf_op jit(solution)/shard_map/ppermute | solution.py:216
  195.1 1.8 collective-permute-start.19
  196.9 2.7 %collective-permute-start.21 = (bf16[448,256]{1,0:T(8,128)(2,1)S(1)}, bf16[448,256]{1,0:T(8,128)(2,1)S(1)}, u32[]{:S(2)}, u32[]{:S(2)}) collective-permute-start(bf16[448,256]{1,0:T(8,128)(2,1)S(1)} %get-tuple-element.38), channel_id=1, source_target_pairs={{0,3},{1,0},{2,1},{3,2},{4,7},{5,4},{6,5},{7,6},{8,11},{9,8},{10,9... | collective-permute-start | bytes 688136 | tf_op jit(solution)/shard_map/ppermute | solution.py:216
  200.0 2.9 %collective-permute-done.19 = bf16[448,256]{1,0:T(8,128)(2,1)S(1)} collective-permute-done((bf16[448,256]{1,0:T(8,128)(2,1)S(1)}, bf16[448,256]{1,0:T(8,128)(2,1)S(1)}, u32[]{:S(2)}, u32[]{:S(2)}) %collective-permute-start.19) | collective-permute-done | bytes 229408 | tf_op jit(solution)/shard_map/ppermute | solution.py:216
  202.9 6.2 %collective-permute-done.20 = bf16[448,256]{1,0:T(8,128)(2,1)S(1)} collective-permute-done((bf16[448,256]{1,0:T(8,128)(2,1)S(1)}, bf16[448,256]{1,0:T(8,128)(2,1)S(1)}, u32[]{:S(2)}, u32[]{:S(2)}) %collective-permute-start.20) | collective-permute-done | bytes 229408 | tf_op jit(solution)/shard_map/ppermute | solution.py:216
  209.3 10.9 %all_to_all.11.refs_0_ = bf16[8,96,256]{2,1,0:T(8,128)(2,1)S(1)} all-to-all(bf16[8,96,256]{2,1,0:T(8,128)(2,1)S(1)} %pad_maximum_fusion), channel_id=1, replica_groups=mesh['ep'=8,'tp'=16] {'ep'}, dimensions={0} | all-to-all | bytes 786432 | tf_op jit(solution)/shard_map/all_to_all | solution.py:327
  (105 shorter events, 27.0 us)
Async XLA Ops:
  20.8 11.0 %collective-permute-start.8 = (bf16[768,256]{1,0:T(8,128)(2,1)S(1)}, bf16[768,256]{1,0:T(8,128)(2,1)S(1)}, u32[]{:S(2)}, u32[]{:S(2)}) collective-permute-start(bf16[768,256]{1,0:T(8,128)(2,1)S(1)} %bitcast.76), channel_id=1, source_target_pairs={{0,1},{1,2},{2,3},{3,0},{4,5},{5,6},{6,7},{7,4},{8,9},{9,10},{10,1... | collective-permute-start | bytes 1179656 | tf_op jit(solution)/shard_map/ppermute | solution.py:216
  22.2 9.8 %collective-permute-start.9 = (bf16[768,256]{1,0:T(8,128)(2,1)S(1)}, bf16[768,256]{1,0:T(8,128)(2,1)S(1)}, u32[]{:S(2)}, u32[]{:S(2)}) collective-permute-start(bf16[768,256]{1,0:T(8,128)(2,1)S(1)} %bitcast.77), channel_id=1, source_target_pairs={{0,3},{1,0},{2,1},{3,2},{4,7},{5,4},{6,5},{7,6},{8,11},{9,8},{10,9... | collective-permute-start | bytes 1179656 | tf_op jit(solution)/shard_map/ppermute | solution.py:216
  23.7 11.8 %collective-permute-start = (bf16[768,256]{1,0:T(8,128)(2,1)S(1)}, bf16[768,256]{1,0:T(8,128)(2,1)S(1)}, u32[]{:S(2)}, u32[]{:S(2)}) collective-permute-start(bf16[768,256]{1,0:T(8,128)(2,1)S(1)} %bitcast.73), channel_id=1, source_target_pairs={{0,4},{1,5},{2,6},{3,7},{4,8},{5,9},{6,10},{7,11},{8,12},{9,13},{1... | collective-permute-start | bytes 1179656 | tf_op jit(solution)/shard_map/ppermute | solution.py:216
  25.3 11.1 %collective-permute-start.1 = (bf16[768,256]{1,0:T(8,128)(2,1)S(1)}, bf16[768,256]{1,0:T(8,128)(2,1)S(1)}, u32[]{:S(2)}, u32[]{:S(2)}) collective-permute-start(bf16[768,256]{1,0:T(8,128)(2,1)S(1)} %bitcast.74), channel_id=1, source_target_pairs={{0,12},{1,13},{2,14},{3,15},{4,0},{5,1},{6,2},{7,3},{8,4},{9,5},{1... | collective-permute-start | bytes 1179656 | tf_op jit(solution)/shard_map/ppermute | solution.py:216
  38.9 37.7 %collective-permute-start.12 = (bf16[3072,256]{1,0:T(8,128)(2,1)S(1)}, bf16[3072,256]{1,0:T(8,128)(2,1)S(1)}, u32[]{:S(2)}, u32[]{:S(2)}) collective-permute-start(bf16[3072,256]{1,0:T(8,128)(2,1)S(1)} %constant_dynamic-update-slice_fusion.5), channel_id=1, source_target_pairs={{0,4},{1,5},{2,6},{3,7},{4,8},{5,9},{6,10},{7,11},{8,12},{9,13},{1... | collective-permute-start | bytes 4718600 | tf_op jit(solution)/shard_map/ppermute | solution.py:216
  39.4 38.1 %collective-permute-start.14 = (bf16[3072,256]{1,0:T(8,128)(2,1)S(1)}, bf16[3072,256]{1,0:T(8,128)(2,1)S(1)}, u32[]{:S(2)}, u32[]{:S(2)}) collective-permute-start(bf16[3072,256]{1,0:T(8,128)(2,1)S(1)} %constant_dynamic-update-slice_fusion.5), channel_id=1, source_target_pairs={{0,12},{1,13},{2,14},{3,15},{4,0},{5,1},{6,2},{7,3},{8,4},{9,5},{1... | collective-permute-start | bytes 4718600 | tf_op jit(solution)/shard_map/ppermute | solution.py:216
  41.7 39.6 %collective-permute-start.4 = (bf16[3072,256]{1,0:T(8,128)(2,1)S(1)}, bf16[3072,256]{1,0:T(8,128)(2,1)S(1)}, u32[]{:S(2)}, u32[]{:S(2)}) collective-permute-start(bf16[3072,256]{1,0:T(8,128)(2,1)S(1)} %constant_dynamic-update-slice_fusion), channel_id=1, source_target_pairs={{0,1},{1,2},{2,3},{3,0},{4,5},{5,6},{6,7},{7,4},{8,9},{9,10},{10,1... | collective-permute-start | bytes 4718600 | tf_op jit(solution)/shard_map/ppermute | solution.py:216
  42.2 40.2 %collective-permute-start.6 = (bf16[3072,256]{1,0:T(8,128)(2,1)S(1)}, bf16[3072,256]{1,0:T(8,128)(2,1)S(1)}, u32[]{:S(2)}, u32[]{:S(2)}) collective-permute-start(bf16[3072,256]{1,0:T(8,128)(2,1)S(1)} %constant_dynamic-update-slice_fusion), channel_id=1, source_target_pairs={{0,3},{1,0},{2,1},{3,2},{4,7},{5,4},{6,5},{7,6},{8,11},{9,8},{10,9... | collective-permute-start | bytes 4718600 | tf_op jit(solution)/shard_map/ppermute | solution.py:216
  77.5 38.8 %collective-permute-start.13 = (bf16[1536,256]{1,0:T(8,128)(2,1)}, bf16[1536,256]{1,0:T(8,128)(2,1)}, u32[]{:S(2)}, u32[]{:S(2)}) collective-permute-start(bf16[1536,256]{1,0:T(8,128)(2,1)} %slice.86), channel_id=1, source_target_pairs={{0,4},{1,5},{2,6},{3,7},{4,8},{5,9},{6,10},{7,11},{8,12},{9,13},{1... | collective-permute-start | bytes 2359304 | tf_op jit(solution)/shard_map/ppermute | solution.py:216
  78.6 37.7 %collective-permute-start.15 = (bf16[1536,256]{1,0:T(8,128)(2,1)}, bf16[1536,256]{1,0:T(8,128)(2,1)}, u32[]{:S(2)}, u32[]{:S(2)}) collective-permute-start(bf16[1536,256]{1,0:T(8,128)(2,1)} %slice.87), channel_id=1, source_target_pairs={{0,12},{1,13},{2,14},{3,15},{4,0},{5,1},{6,2},{7,3},{8,4},{9,5},{1... | collective-permute-start | bytes 2359304 | tf_op jit(solution)/shard_map/ppermute | solution.py:216
  82.3 34.0 %collective-permute-start.5 = (bf16[1536,256]{1,0:T(8,128)(2,1)}, bf16[1536,256]{1,0:T(8,128)(2,1)}, u32[]{:S(2)}, u32[]{:S(2)}) collective-permute-start(bf16[1536,256]{1,0:T(8,128)(2,1)} %slice.81), channel_id=1, source_target_pairs={{0,1},{1,2},{2,3},{3,0},{4,5},{5,6},{6,7},{7,4},{8,9},{9,10},{10,1... | collective-permute-start | bytes 2359304 | tf_op jit(solution)/shard_map/ppermute | solution.py:216
  83.4 33.0 %collective-permute-start.7 = (bf16[1536,256]{1,0:T(8,128)(2,1)}, bf16[1536,256]{1,0:T(8,128)(2,1)}, u32[]{:S(2)}, u32[]{:S(2)}) collective-permute-start(bf16[1536,256]{1,0:T(8,128)(2,1)} %slice.82), channel_id=1, source_target_pairs={{0,3},{1,0},{2,1},{3,2},{4,7},{5,4},{6,5},{7,6},{8,11},{9,8},{10,9... | collective-permute-start | bytes 2359304 | tf_op jit(solution)/shard_map/ppermute | solution.py:216
  135.9 14.8 %collective-permute-start.22 = (bf16[4,320,256]{2,1,0:T(8,128)(2,1)S(1)}, bf16[4,320,256]{2,1,0:T(8,128)(2,1)S(1)}, u32[]{:S(2)}, u32[]{:S(2)}) collective-permute-start(bf16[4,320,256]{2,1,0:T(8,128)(2,1)S(1)} %get-tuple-element.30), channel_id=1, source_target_pairs={{0,2},{1,3},{2,0},{3,1},{4,6},{5,7},{6,4},{7,5},{8,10},{9,11},{10,... | collective-permute-start | bytes 1966088 | tf_op jit(solution)/shard_map/ppermute | solution.py:216
  136.0 31.8 %collective-permute-start.23 = (bf16[4,320,256]{2,1,0:T(8,128)(2,1)S(1)}, bf16[4,320,256]{2,1,0:T(8,128)(2,1)S(1)}, u32[]{:S(2)}, u32[]{:S(2)}) collective-permute-start(bf16[4,320,256]{2,1,0:T(8,128)(2,1)S(1)} %get-tuple-element.31), channel_id=1, source_target_pairs={{0,1},{1,2},{2,3},{3,0},{4,5},{5,6},{6,7},{7,4},{8,9},{9,10},{10,1... | collective-permute-start | bytes 1966088 | tf_op jit(solution)/shard_map/ppermute | solution.py:216
  137.1 30.7 %collective-permute-start.24 = (bf16[4,320,256]{2,1,0:T(8,128)(2,1)S(1)}, bf16[4,320,256]{2,1,0:T(8,128)(2,1)S(1)}, u32[]{:S(2)}, u32[]{:S(2)}) collective-permute-start(bf16[4,320,256]{2,1,0:T(8,128)(2,1)S(1)} %get-tuple-element.32), channel_id=1, source_target_pairs={{0,3},{1,0},{2,1},{3,2},{4,7},{5,4},{6,5},{7,6},{8,11},{9,8},{10,9... | collective-permute-start | bytes 1966088 | tf_op jit(solution)/shard_map/ppermute | solution.py:216
  149.8 19.7 %collective-permute-start.16 = (bf16[4,448,256]{2,1,0:T(8,128)(2,1)S(1)}, bf16[4,448,256]{2,1,0:T(8,128)(2,1)S(1)}, u32[]{:S(2)}, u32[]{:S(2)}) collective-permute-start(bf16[4,448,256]{2,1,0:T(8,128)(2,1)S(1)} %get-tuple-element.25), channel_id=1, source_target_pairs={{0,8},{1,9},{2,10},{3,11},{4,12},{5,13},{6,14},{7,15},{8,0},{9,1},... | collective-permute-start | bytes 2752520 | tf_op jit(solution)/shard_map/ppermute | solution.py:216
  149.9 44.7 %collective-permute-start.17 = (bf16[4,448,256]{2,1,0:T(8,128)(2,1)S(1)}, bf16[4,448,256]{2,1,0:T(8,128)(2,1)S(1)}, u32[]{:S(2)}, u32[]{:S(2)}) collective-permute-start(bf16[4,448,256]{2,1,0:T(8,128)(2,1)S(1)} %get-tuple-element.26), channel_id=1, source_target_pairs={{0,4},{1,5},{2,6},{3,7},{4,8},{5,9},{6,10},{7,11},{8,12},{9,13},{1... | collective-permute-start | bytes 2752520 | tf_op jit(solution)/shard_map/ppermute | solution.py:216
  150.8 43.8 %collective-permute-start.18 = (bf16[4,448,256]{2,1,0:T(8,128)(2,1)S(1)}, bf16[4,448,256]{2,1,0:T(8,128)(2,1)S(1)}, u32[]{:S(2)}, u32[]{:S(2)}) collective-permute-start(bf16[4,448,256]{2,1,0:T(8,128)(2,1)S(1)} %get-tuple-element.27), channel_id=1, source_target_pairs={{0,12},{1,13},{2,14},{3,15},{4,0},{5,1},{6,2},{7,3},{8,4},{9,5},{1... | collective-permute-start | bytes 2752520 | tf_op jit(solution)/shard_map/ppermute | solution.py:216
  168.2 28.7 %collective-permute-start.25 = (bf16[320,256]{1,0:T(8,128)(2,1)S(1)}, bf16[320,256]{1,0:T(8,128)(2,1)S(1)}, u32[]{:S(2)}, u32[]{:S(2)}) collective-permute-start(bf16[320,256]{1,0:T(8,128)(2,1)S(1)} %get-tuple-element.42), channel_id=1, source_target_pairs={{0,8},{1,9},{2,10},{3,11},{4,12},{5,13},{6,14},{7,15},{8,0},{9,1},... | collective-permute-start | bytes 491528 | tf_op jit(solution)/shard_map/ppermute | solution.py:216
  168.3 31.5 %collective-permute-start.26 = (bf16[320,256]{1,0:T(8,128)(2,1)S(1)}, bf16[320,256]{1,0:T(8,128)(2,1)S(1)}, u32[]{:S(2)}, u32[]{:S(2)}) collective-permute-start(bf16[320,256]{1,0:T(8,128)(2,1)S(1)} %get-tuple-element.44), channel_id=1, source_target_pairs={{0,4},{1,5},{2,6},{3,7},{4,8},{5,9},{6,10},{7,11},{8,12},{9,13},{1... | collective-permute-start | bytes 491528 | tf_op jit(solution)/shard_map/ppermute | solution.py:216
  169.5 30.4 %collective-permute-start.27 = (bf16[320,256]{1,0:T(8,128)(2,1)S(1)}, bf16[320,256]{1,0:T(8,128)(2,1)S(1)}, u32[]{:S(2)}, u32[]{:S(2)}) collective-permute-start(bf16[320,256]{1,0:T(8,128)(2,1)S(1)} %get-tuple-element.43), channel_id=1, source_target_pairs={{0,12},{1,13},{2,14},{3,15},{4,0},{5,1},{6,2},{7,3},{8,4},{9,5},{1... | collective-permute-start | bytes 491528 | tf_op jit(solution)/shard_map/ppermute | solution.py:216
  195.1 7.8 %collective-permute-start.19 = (bf16[448,256]{1,0:T(8,128)(2,1)S(1)}, bf16[448,256]{1,0:T(8,128)(2,1)S(1)}, u32[]{:S(2)}, u32[]{:S(2)}) collective-permute-start(bf16[448,256]{1,0:T(8,128)(2,1)S(1)} %get-tuple-element.37), channel_id=1, source_target_pairs={{0,2},{1,3},{2,0},{3,1},{4,6},{5,7},{6,4},{7,5},{8,10},{9,11},{10,... | collective-permute-start | bytes 688136 | tf_op jit(solution)/shard_map/ppermute | solution.py:216
  196.9 12.3 %collective-permute-start.20 = (bf16[448,256]{1,0:T(8,128)(2,1)S(1)}, bf16[448,256]{1,0:T(8,128)(2,1)S(1)}, u32[]{:S(2)}, u32[]{:S(2)}) collective-permute-start(bf16[448,256]{1,0:T(8,128)(2,1)S(1)} %get-tuple-element.39), channel_id=1, source_target_pairs={{0,1},{1,2},{2,3},{3,0},{4,5},{5,6},{6,7},{7,4},{8,9},{9,10},{10,1... | collective-permute-start | bytes 688136 | tf_op jit(solution)/shard_map/ppermute | solution.py:216
  196.9 12.3 %collective-permute-start.21 = (bf16[448,256]{1,0:T(8,128)(2,1)S(1)}, bf16[448,256]{1,0:T(8,128)(2,1)S(1)}, u32[]{:S(2)}, u32[]{:S(2)}) collective-permute-start(bf16[448,256]{1,0:T(8,128)(2,1)S(1)} %get-tuple-element.38), channel_id=1, source_target_pairs={{0,3},{1,0},{2,1},{3,2},{4,7},{5,4},{6,5},{7,6},{8,11},{9,8},{10,9... | collective-permute-start | bytes 688136 | tf_op jit(solution)/shard_map/ppermute | solution.py:216
  (22 other events, 207.6 us)

commit v4 on v3

--- a/solution.py
+++ b/solution.py
@@ -65,23 +65,18 @@
     out[...] = (one * share[:, 0:1] + two * share[:, 1:2]).astype(out.dtype)
 
 
-def absorb_body(x_order, g_order, *refs, first, count, last):
-    per = 2 if last else count
-    pieces, refs = (refs[:per], refs[per : 2 * per]), refs[2 * per :]
-    before, refs = (refs[:2], refs[2:]) if first > 0 else ((), refs)
-    gate, up, down = refs[:3]
-    outs, (sides, downs, sides_here, downs_here), rows = refs[3:5], refs[5:9], refs[9:]
+def weight_copies(x_order, g_order, hbm, vmem, here, first, count):
+    (gate, up, down), (sides, downs), (sides_here, downs_here) = hbm, vmem, here
     width, units = gate.shape[1:]
-    wide = SIDE * width
-
-    def fetch_sides(k):
+
+    def for_acts(k):
         t = x_order[first * SIDE + k]
         return [
             pltpu.make_async_copy(gate.at[t], sides.at[k, :, :units], sides_here.at[0, k]),
             pltpu.make_async_copy(up.at[t], sides.at[k, :, units:], sides_here.at[1, k]),
         ]
 
-    def fetch_downs(i, f):
+    def for_hidden(i, f):
         t = g_order[(first + i) * SIDE + f]
         return pltpu.make_async_copy(
             down.at[:, pl.ds(pl.multiple_of(t * width, width), width)],
@@ -89,56 +84,61 @@
             downs_here.at[i, f],
         )
 
-    for i in range(count):
+    def every():
+        for i in range(count):
+            for f in range(SIDE):
+                yield from for_acts(i * SIDE + f)
+            for f in range(SIDE):
+                yield for_hidden(i, f)
+
+    return for_acts, for_hidden, every
+
+
+def absorb_body(x_order, g_order, *refs, first, count, ahead):
+    pieces, refs = (refs[:count], refs[count : 2 * count]), refs[2 * count :]
+    given = first > 0
+    before, refs = (refs[:4], refs[4:]) if given else ((), refs)
+    hbm, outs, refs = refs[:3], refs[3:7], refs[7:]
+    following = weight_copies(x_order, g_order, hbm, outs[2:], refs[:2], first + count, ahead)[2]
+    if given:
+        sides, downs = before[2:]
+    else:
+        sides, downs = refs[2:4]
+        for_acts, for_hidden, every = weight_copies(x_order, g_order, hbm, refs[2:4], refs[4:6], first, count)
+        for copy in every():
+            copy.start()
+    for copy in following():
+        copy.start()
+    wide = SIDE * hbm[0].shape[1]
+    left = [jnp.concatenate([pieces[kind][0][f] for f in range(SIDE)], axis=1) for kind in range(2)]
+    if not given:
         for f in range(SIDE):
-            for copy in fetch_sides(i * SIDE + f):
-                copy.start()
+            for copy in for_acts(f):
+                copy.wait()
+    part = jnp.dot(left[0], sides[...].reshape(wide, sides.shape[2]), preferred_element_type=F32)
+    outs[0][...] = before[0][...] + part if given else part
+    if not given:
         for f in range(SIDE):
-            fetch_downs(i, f).start()
-    blocks = [[p.at[i] for p in pieces[kind] for i in range(p.shape[0])] for kind in range(2)]
-    if count > 1:
-        for kind in range(2):
-            for at, block in enumerate(blocks[kind]):
-                s, f = at // SIDE, at % SIDE
-                rows[0][kind, s, :, f * width : (f + 1) * width] = block[...]
-
-    def left(kind, i):
-        if count > 1:
-            return rows[0][kind, i]
-        return jnp.concatenate([block[...] for block in blocks[kind]], axis=1)
-
-    def ring(i, carry):
-        for f in range(SIDE):
-            for copy in fetch_sides(i * SIDE + f):
-                copy.wait()
-        right = sides[pl.ds(i * SIDE, SIDE)].reshape(wide, 2 * units)
-        acts_part = jnp.dot(left(0, i), right, preferred_element_type=F32)
-        for f in range(SIDE):
-            fetch_downs(i, f).wait()
-        hidden_part = lax.dot_general(left(1, i), downs[i], ROWS_BY_ROWS, preferred_element_type=F32)
-        if last:
-            form_grads(before[0][...] + acts_part, before[1][...] + hidden_part, *outs)
-        elif count == 1:
-            outs[0][...] = acts_part
-            outs[1][...] = hidden_part
-        else:
-
-            @pl.when(i == 0)
-            def _():
-                outs[0][...] = before[0][...] + acts_part
-                outs[1][...] = before[1][...] + hidden_part
-
-            @pl.when(i != 0)
-            def _():
-                outs[0][...] += acts_part
-                outs[1][...] += hidden_part
-
-        return carry
-
-    if count > 1:
-        lax.fori_loop(0, count, ring, 0)
-    else:
-        ring(0, 0)
+            for_hidden(0, f).wait()
+    part = lax.dot_general(left[1], downs[0], ROWS_BY_ROWS, preferred_element_type=F32)
+    outs[1][...] = before[1][...] + part if given else part
+    for copy in following():
+        copy.wait()
+
+
+def finish_body(order, *refs):
+    pieces, (acts, hidden, sides, downs, gate, up) = (refs[:2], refs[2:4]), refs[4:10]
+    outs, later, (grads, wide, wide_here) = refs[10 : 10 + SIDE], refs[10 + SIDE], refs[11 + SIDE :]
+    start_parts(order, gate, up, wide, wide_here)
+    left = [jnp.concatenate([p[i] for p in pieces[kind] for i in range(p.shape[0])], axis=1) for kind in range(2)]
+    right = sides[...].reshape(left[0].shape[1], sides.shape[2])
+    form_grads(
+        acts[...] + jnp.dot(left[0], right, preferred_element_type=F32),
+        hidden[...] + lax.dot_general(left[1], downs[0], ROWS_BY_ROWS, preferred_element_type=F32),
+        grads,
+        later,
+    )
+    form_parts(order, grads, gate, up, wide, wide_here, outs)
 
 
 def form_grads(acts, hidden, *outs):
@@ -159,28 +159,31 @@
         start += part
 
 
-def parts_body(order, grads, gate, up, *refs):
-    outs, (sides, sides_here) = refs[:SIDE], refs[SIDE:]
-    experts, part_rows, _ = grads.shape
-    width, units = gate.shape[1:]
-
-    def fetch(k):
-        return [
-            pltpu.make_async_copy(gate.at[order[k]], sides.at[k, :, :units], sides_here.at[0, k]),
-            pltpu.make_async_copy(up.at[order[k]], sides.at[k, :, units:], sides_here.at[1, k]),
-        ]
-
+def part_copies(order, gate, up, sides, here, k):
+    units = gate.shape[2]
+    return [
+        pltpu.make_async_copy(gate.at[order[k]], sides.at[k, :, :units], here.at[0, k]),
+        pltpu.make_async_copy(up.at[order[k]], sides.at[k, :, units:], here.at[1, k]),
+    ]
+
+
+def start_parts(order, gate, up, sides, here):
     for k in range(TP):
-        for copy in fetch(k):
+        for copy in part_copies(order, gate, up, sides, here, k):
             copy.start()
+
+
+def form_parts(order, grads, gate, up, sides, here, outs):
+    experts, part_rows, both = grads.shape
+    width = gate.shape[1]
 
     def members(j, carry):
         k = 2 * j
-        for copy in fetch(k) + fetch(k + 1):
+        for copy in part_copies(order, gate, up, sides, here, k) + part_copies(order, gate, up, sides, here, k + 1):
             copy.wait()
         part = lax.dot_general(
-            grads[...].reshape(experts * part_rows, 2 * units),
-            sides[pl.ds(k, 2)].reshape(2 * width, 2 * units),
+            grads[...].reshape(experts * part_rows, both),
+            sides[pl.ds(k, 2)].reshape(2 * width, both),
             ROWS_BY_ROWS,
             preferred_element_type=F32,
         ).astype(BF)
@@ -194,6 +197,12 @@
         return carry
 
     lax.fori_loop(0, TP // 2, members, 0)
+
+
+def parts_body(order, grads, gate, up, *refs):
+    outs, (sides, here) = refs[:SIDE], refs[SIDE:]
+    start_parts(order, gate, up, sides, here)
+    form_parts(order, grads, gate, up, sides, here, outs)
 
 
 def vmem(mebibytes):
@@ -227,7 +236,8 @@
 
 def plane_gather(x, first, second):
     rows, width = x.shape
-    line = jnp.concatenate(ring_gather(x, first), axis=0)
+    far, below, above = [shifted(x, first, by) for by in (2, 1, 3)]
+    line = jnp.concatenate([x, below, above, far], axis=0)
     return [piece.reshape(-1, rows, width) for piece in ring_gather(line, second)]
 
 
@@ -267,7 +277,7 @@
         out_shape=jax.ShapeDtypeStruct((experts, 2 * capacity, width), BF),
         name="dispatch",
         compiler_params=vmem(16),
-    )(routes, layer_input, out_grad)
+    )(routes, *in_hbm(layer_input, out_grad))
     got = lax.all_to_all(sent, "ep", split_axis=0, concat_axis=0, tiled=True)
     x = plane_gather(got[:, :capacity].reshape(slots, width), z_shift, y_shift)
     g = plane_gather(got[:, capacity:].reshape(slots, width), y_shift, z_shift)
@@ -276,49 +286,56 @@
     in_smem = pl.BlockSpec(memory_space=pltpu.SMEM)
     stays = pl.BlockSpec(memory_space=pltpu.HBM)
     dma = pltpu.SemaphoreType.DMA
-    sums = []
-    for first, count, which, limit in ((0, 1, slice(0, 1), 28), (1, 2, slice(1, 3), 34), (3, 1, slice(3, 5), 28)):
-        last = first + count == SIDE
-        if last:
-            outs = [jax.ShapeDtypeStruct((experts, part, 2 * units), BF) for part in parts]
-        else:
-            outs = [jax.ShapeDtypeStruct((slots, 2 * units), F32), jax.ShapeDtypeStruct((slots, units), F32)]
-        used = [*x[which], *g[which], *sums]
-        sums = pl.pallas_call(
-            functools.partial(absorb_body, first=first, count=count, last=last),
+    sides_of = lambda count: pltpu.VMEM((count * SIDE, width, 2 * units), BF)
+    downs_of = lambda count: pltpu.VMEM((count, units, SIDE * width), BF)
+    blocks = in_hbm(gate_matrix.reshape(TP, width, units), up_matrix.reshape(TP, width, units), down_matrix)
+    state = []
+    for first, count, ahead, limit in ((0, 1, 1, 14), (1, 1, 1, 18), (2, 1, 1, 18)):
+        used = [*x[first : first + count], *g[first : first + count], *state]
+        own = []
+        if first == 0:
+            own = [sides_of(count), downs_of(count), dma((2, count * SIDE)), dma((count, SIDE))]
+        state = pl.pallas_call(
+            functools.partial(absorb_body, first=first, count=count, ahead=ahead),
             in_specs=[in_smem] * 2 + [in_vmem] * len(used) + [stays] * 3,
-            out_specs=[in_vmem] * 2,
-            out_shape=outs,
-            scratch_shapes=[
-                pltpu.VMEM((count * SIDE, width, 2 * units), BF),
-                pltpu.VMEM((count, units, SIDE * width), BF),
-                dma((2, count * SIDE)),
-                dma((count, SIDE)),
-            ]
-            + [pltpu.VMEM((2, count, slots, SIDE * width), BF)] * (count > 1),
+            out_specs=[in_vmem] * 4,
+            out_shape=[
+                jax.ShapeDtypeStruct((slots, 2 * units), F32),
+                jax.ShapeDtypeStruct((slots, units), F32),
+                jax.ShapeDtypeStruct((ahead * SIDE, width, 2 * units), BF),
+                jax.ShapeDtypeStruct((ahead, units, SIDE * width), BF),
+            ],
+            scratch_shapes=[dma((2, ahead * SIDE)), dma((ahead, SIDE))] + own,
             name="absorb",
             compiler_params=vmem(limit),
-        )(
-            x_order,
-            g_order,
-            *used,
-            *in_hbm(
-                gate_matrix.reshape(TP, width, units), up_matrix.reshape(TP, width, units), down_matrix
-            ),
-        )
+        )(x_order, g_order, *used, *blocks)
+
+    def parts_shape(part):
+        return [jax.ShapeDtypeStruct((SIDE, experts * part, width), BF)] * SIDE
 
     summed = []
     for h, part in enumerate(parts):
-        rows = experts * part
-        outs = pl.pallas_call(
-            parts_body,
-            in_specs=[in_smem, in_vmem] + [stays] * 2,
-            out_specs=[in_vmem] * SIDE,
-            out_shape=[jax.ShapeDtypeStruct((SIDE, rows, width), BF)] * SIDE,
-            scratch_shapes=[pltpu.VMEM((TP, width, 2 * units), BF), dma((2, TP))],
-            name="parts",
-            compiler_params=vmem(32),
-        )(summed_order[h], sums[h], *in_hbm(gate_matrix.reshape(TP, width, units), up_matrix.reshape(TP, width, units)))
+        if h == 0:
+            later_shape = jax.ShapeDtypeStruct((experts, parts[1], 2 * units), BF)
+            *outs, later = pl.pallas_call(
+                finish_body,
+                in_specs=[in_smem] + [in_vmem] * 8 + [stays] * 2,
+                out_specs=[in_vmem] * (SIDE + 1),
+                out_shape=parts_shape(part) + [later_shape],
+                scratch_shapes=[pltpu.VMEM((experts, part, 2 * units), BF), sides_of(SIDE), dma((2, TP))],
+                name="finish",
+                compiler_params=vmem(29),
+            )(summed_order[h], *x[3:], *g[3:], *state, *blocks[:2])
+        else:
+            outs = pl.pallas_call(
+                parts_body,
+                in_specs=[in_smem, in_vmem] + [stays] * 2,
+                out_specs=[in_vmem] * SIDE,
+                out_shape=parts_shape(part),
+                scratch_shapes=[sides_of(SIDE), dma((2, TP))],
+                name="parts",
+                compiler_params=vmem(28),
+            )(summed_order[h], later, *blocks[:2])
         first, second = (z_shift, y_shift) if h == 0 else (y_shift, z_shift)
         line = ring_sum(*outs, first)
         mine = ring_sum(line[2], line[1], line[3], line[0], second)

time: 222 us -> 216 us (0.973)
  local copies, waits for them, and re-layouts: 12.2 us -> 4.98 us
  waiting for transfers between devices: 85.9 us -> 92 us
  Pallas kernels: 57.3 us -> 53.7 us
    pallas_call x2 -> x1, Pallas kernels: 19.9 us -> 8.97 us  [body(): pl.pallas_call(parts_body, in_specs=[in_smem, in_vmem] + [stays] * 2, out...]
    unnamed x44 -> x30, local copies, waits for them, and re-layouts: 7.97 us -> 0.73 us
    pallas_call x3 -> x4, Pallas kernels: 35.6 us -> 42 us  [the longest x3 24.3 us: body(): pl.pallas_call(functools.partial(absorb_body, first=first, count=count, a...]
    ppermute x28 -> x26, waiting for transfers between devices: 85.9 us -> 92 us  [shifted(): return lax.ppermute(x, 'tp', shift(by))]
    ppermute x28 -> x26, starting transfers between devices: 36 us -> 34.9 us  [shifted(): return lax.ppermute(x, 'tp', shift(by))]
  transfers between devices with their start and end apart: 28 -> 26, of which waited for: 10 -> 10; matrix products, arithmetic and copies ran while one was open for 2% -> 2% of each run, Pallas kernels for 16% -> 11%
where the time goes in v4:
time: 216 us
  waiting for transfers between devices  92 us (43%)
  Pallas kernels  53.7 us (25%)
  starting transfers between devices  34.9 us (16%)
  blocking collectives  28.6 us (13%)
  local copies, waits for them, and re-layouts  4.98 us (2%)
    ppermute x26, waiting for transfers between devices, shifted(): return lax.ppermute(x, 'tp', shift(by))  92 us
    ppermute x26, starting transfers between devices, shifted(): return lax.ppermute(x, 'tp', shift(by))  34.9 us
    pallas_call x3, Pallas kernels, body(): pl.pallas_call(functools.partial(absorb_body, first=first, count=count, a...  24.3 us
    all_to_all x1, blocking collectives, body(): got = lax.all_to_all(sent, 'ep', split_axis=0, concat_axis=0, tiled=True)  17.7 us
    pallas_call x1, Pallas kernels, body(): pl.pallas_call(finish_body, in_specs=[in_smem] + [in_vmem] * 8 + [stays]...  17.7 us
    all_to_all x1, blocking collectives, body(): lax.all_to_all(jnp.concatenate(summed, axis=1), 'ep', split_axis=0, conca...  10.9 us
    pallas_call x1, Pallas kernels, body(): pl.pallas_call(parts_body, in_specs=[in_smem, in_vmem] + [stays] * 2, out...  8.97 us
  transfers between devices with their start and end apart: 26, of which 10 were waited for; matrix products, arithmetic and copies ran while one was open for 2% of the time, Pallas kernels for 11%

profile of v4, /device:TPU:1, one launch (start us, length us, event | category | flops | bytes accessed | tf_op | source)
XLA Modules:
  0.0 215.8 jit_solution(927812792432465768)
XLA Ops:
  2.2 17.7 %all_to_all.10 = bf16[8,192,256]{2,1,0:T(8,128)(2,1)S(1)} all-to-all(bf16[8,192,256]{2,1,0:T(8,128)(2,1)S(1)} %dispatch.1), channel_id=1, replica_groups=mesh['ep'=8,'tp'=16] {'ep'}, dimensions={0} | all-to-all | bytes 1572864 | tf_op jit(solution)/shard_map/all_to_all | solution.py:281
  26.0 2.1 collective-permute-start.1
  28.2 2.8 %collective-permute-done.7 = bf16[768,256]{1,0:T(8,128)(2,1)S(1)} collective-permute-done((bf16[768,256]{1,0:T(8,128)(2,1)S(1)}, bf16[768,256]{1,0:T(8,128)(2,1)S(1)}, u32[]{:S(2)}, u32[]{:S(2)}) %collective-permute-start.7) | collective-permute-done | bytes 393248 | tf_op jit(solution)/shard_map/ppermute | solution.py:225
  31.0 3.6 %collective-permute-start.2 = (bf16[768,256]{1,0:T(8,128)(2,1)S(1)}, bf16[768,256]{1,0:T(8,128)(2,1)S(1)}, u32[]{:S(2)}, u32[]{:S(2)}) collective-permute-start(bf16[768,256]{1,0:T(8,128)(2,1)S(1)} %bitcast.75), channel_id=1, source_target_pairs={{0,8},{1,9},{2,10},{3,11},{4,12},{5,13},{6,14},{7,15},{8,0},{9,1},... | collective-permute-start | bytes 1179656 | tf_op jit(solution)/shard_map/ppermute | solution.py:225
  34.6 5.9 %collective-permute-done.9 = bf16[768,256]{1,0:T(8,128)(2,1)S(1)} collective-permute-done((bf16[768,256]{1,0:T(8,128)(2,1)S(1)}, bf16[768,256]{1,0:T(8,128)(2,1)S(1)}, u32[]{:S(2)}, u32[]{:S(2)}) %collective-permute-start.9) | collective-permute-done | bytes 393248 | tf_op jit(solution)/shard_map/ppermute | solution.py:225
  42.3 2.2 %collective-permute-start.12 = (bf16[3072,256]{1,0:T(8,128)(2,1)S(1)}, bf16[3072,256]{1,0:T(8,128)(2,1)S(1)}, u32[]{:S(2)}, u32[]{:S(2)}) collective-permute-start(bf16[3072,256]{1,0:T(8,128)(2,1)S(1)} %pad_maximum_fusion.1), channel_id=1, source_target_pairs={{0,12},{1,13},{2,14},{3,15},{4,0},{5,1},{6,2},{7,3},{8,4},{9,5},{1... | collective-permute-start | bytes 4718600 | tf_op jit(solution)/shard_map/ppermute | solution.py:225
  45.7 2.3 %collective-permute-start.5 = (bf16[3072,256]{1,0:T(8,128)(2,1)S(1)}, bf16[3072,256]{1,0:T(8,128)(2,1)S(1)}, u32[]{:S(2)}, u32[]{:S(2)}) collective-permute-start(bf16[3072,256]{1,0:T(8,128)(2,1)S(1)} %pad_maximum_fusion), channel_id=1, source_target_pairs={{0,3},{1,0},{2,1},{3,2},{4,7},{5,4},{6,5},{7,6},{8,11},{9,8},{10,9... | collective-permute-start | bytes 4718600 | tf_op jit(solution)/shard_map/ppermute | solution.py:225
  48.0 32.7 %collective-permute-done.10 = bf16[3072,256]{1,0:T(8,128)(2,1)S(1)} collective-permute-done((bf16[3072,256]{1,0:T(8,128)(2,1)S(1)}, bf16[3072,256]{1,0:T(8,128)(2,1)S(1)}, u32[]{:S(2)}, u32[]{:S(2)}) %collective-permute-start.10) | collective-permute-done | bytes 1572896 | tf_op jit(solution)/shard_map/ppermute | solution.py:225
  82.8 2.7 %collective-permute-start.13 = (bf16[1536,256]{1,0:T(8,128)(2,1)}, bf16[1536,256]{1,0:T(8,128)(2,1)}, u32[]{:S(2)}, u32[]{:S(2)}) collective-permute-start(bf16[1536,256]{1,0:T(8,128)(2,1)} %slice.67), channel_id=1, source_target_pairs={{0,12},{1,13},{2,14},{3,15},{4,0},{5,1},{6,2},{7,3},{8,4},{9,5},{1... | collective-permute-start | bytes 2359304 | tf_op jit(solution)/shard_map/ppermute | solution.py:225
  87.6 2.6 %collective-permute-start.6 = (bf16[1536,256]{1,0:T(8,128)(2,1)}, bf16[1536,256]{1,0:T(8,128)(2,1)}, u32[]{:S(2)}, u32[]{:S(2)}) collective-permute-start(bf16[1536,256]{1,0:T(8,128)(2,1)} %slice.64), channel_id=1, source_target_pairs={{0,3},{1,0},{2,1},{3,2},{4,7},{5,4},{6,5},{7,6},{8,11},{9,8},{10,9... | collective-permute-start | bytes 2359304 | tf_op jit(solution)/shard_map/ppermute | solution.py:225
  90.4 9.7 %absorb.3 = (f32[768,1792]{1,0:T(8,128)S(1)}, f32[768,896]{1,0:T(8,128)S(1)}, bf16[4,256,1792]{2,1,0:T(8,128)(2,1)S(1)}, bf16[1,896,1024]{2,1,0:T(8,128)(2,1)S(1)}) custom-call(s32[16]{0:T(128)S(1)} %get-tuple-element.60.x_order, s32[16]{0:T(128)S(1)} %get-tuple-element.59.g_order, bf16[4,768,256]{2,1,0:T(8,128)(2,1)S(1)} %bitcast.52, ...), custom_call_target="tpu_custom_call" | custom-call | tf_op jit(solution)/shard_map/absorb/pallas_call | solution.py:298
  100.1 7.3 %absorb.4 = (f32[768,1792]{1,0:T(8,128)S(1)}, f32[768,896]{1,0:T(8,128)S(1)}, bf16[4,256,1792]{2,1,0:T(8,128)(2,1)S(1)}, bf16[1,896,1024]{2,1,0:T(8,128)(2,1)S(1)}) custom-call(s32[16]{0:T(128)S(1)} %get-tuple-element.60.x_order, s32[16]{0:T(128)S(1)} %get-tuple-element.59.g_order, bf16[4,768,256]{2,1,0:T(8,128)(2,1)S(1)} %bitcast.56, ...), custom_call_target="tpu_custom_call" | custom-call | tf_op jit(solution)/shard_map/absorb/pallas_call | solution.py:298
  107.4 7.3 %absorb.5 = (f32[768,1792]{1,0:T(8,128)S(1)}, f32[768,896]{1,0:T(8,128)S(1)}, bf16[4,256,1792]{2,1,0:T(8,128)(2,1)S(1)}, bf16[1,896,1024]{2,1,0:T(8,128)(2,1)S(1)}) custom-call(s32[16]{0:T(128)S(1)} %get-tuple-element.60.x_order, s32[16]{0:T(128)S(1)} %get-tuple-element.59.g_order, bf16[4,768,256]{2,1,0:T(8,128)(2,1)S(1)} %bitcast.55, ...), custom_call_target="tpu_custom_call" | custom-call | tf_op jit(solution)/shard_map/absorb/pallas_call | solution.py:298
  114.8 17.7 %finish.1 = (bf16[4,448,256]{2,1,0:T(8,128)(2,1)S(1)}, bf16[4,448,256]{2,1,0:T(8,128)(2,1)S(1)}, bf16[4,448,256]{2,1,0:T(8,128)(2,1)S(1)}, bf16[4,448,256]{2,1,0:T(8,128)(2,1)S(1)}, bf16[8,40,1792]{2,1,0:T(8,128)(2,1)S(1)}) custom-call(s32[16]{0:T(128)S(1)} %get-tuple-element.61.order, bf16[2,768,256]{2,1,0:T(8,128)(2,1)} %bitcast.3.refs_0_, ...), custom_call_target="tpu_custom_call" | custom-call | tf_op jit(solution)/shard_map/finish/pallas_call | solution.py:320
  132.5 9.0 %parts.1 = (bf16[4,320,256]{2,1,0:T(8,128)(2,1)S(1)}, bf16[4,320,256]{2,1,0:T(8,128)(2,1)S(1)}, bf16[4,320,256]{2,1,0:T(8,128)(2,1)S(1)}, bf16[4,320,256]{2,1,0:T(8,128)(2,1)S(1)}) custom-call(s32[16]{0:T(128)S(1)} %get-tuple-element.62.order, bf16[8,40,1792]{2,1,0:T(8,128)(2,1)S(1)} %get-tuple-element.42.grads, bf16[16,256,896]{2,1,0:T(8,128)(2,1)} %bitcast.64, ...), custom_call_target="tpu_custom_call" | custom-call | tf_op jit(solution)/shard_map/parts/pallas_call | solution.py:330
  142.5 1.8 collective-permute-start.22
  144.9 12.5 %collective-permute-done.20 = bf16[4,320,256]{2,1,0:T(8,128)(2,1)S(1)} collective-permute-done((bf16[4,320,256]{2,1,0:T(8,128)(2,1)S(1)}, bf16[4,320,256]{2,1,0:T(8,128)(2,1)S(1)}, u32[]{:S(2)}, u32[]{:S(2)}) %collective-permute-start.20) | collective-permute-done | bytes 655392 | tf_op jit(solution)/shard_map/ppermute | solution.py:225
  157.8 15.5 %collective-permute-done.21 = bf16[4,320,256]{2,1,0:T(8,128)(2,1)S(1)} collective-permute-done((bf16[4,320,256]{2,1,0:T(8,128)(2,1)S(1)}, bf16[4,320,256]{2,1,0:T(8,128)(2,1)S(1)}, u32[]{:S(2)}, u32[]{:S(2)}) %collective-permute-start.21) | collective-permute-done | bytes 655392 | tf_op jit(solution)/shard_map/ppermute | solution.py:225
  174.4 2.1 collective-permute-start.25
  176.6 12.3 %collective-permute-done.15 = bf16[4,448,256]{2,1,0:T(8,128)(2,1)S(1)} collective-permute-done((bf16[4,448,256]{2,1,0:T(8,128)(2,1)S(1)}, bf16[4,448,256]{2,1,0:T(8,128)(2,1)S(1)}, u32[]{:S(2)}, u32[]{:S(2)}) %collective-permute-start.15) | collective-permute-done | bytes 917536 | tf_op jit(solution)/shard_map/ppermute | solution.py:225
  191.2 2.7 %collective-permute-start.19 = (bf16[448,256]{1,0:T(8,128)(2,1)S(1)}, bf16[448,256]{1,0:T(8,128)(2,1)S(1)}, u32[]{:S(2)}, u32[]{:S(2)}) collective-permute-start(bf16[448,256]{1,0:T(8,128)(2,1)S(1)} %get-tuple-element.52), channel_id=1, source_target_pairs={{0,3},{1,0},{2,1},{3,2},{4,7},{5,4},{6,5},{7,6},{8,11},{9,8},{10,9... | collective-permute-start | bytes 688136 | tf_op jit(solution)/shard_map/ppermute | solution.py:225
  194.3 2.8 %collective-permute-done.17 = bf16[448,256]{1,0:T(8,128)(2,1)S(1)} collective-permute-done((bf16[448,256]{1,0:T(8,128)(2,1)S(1)}, bf16[448,256]{1,0:T(8,128)(2,1)S(1)}, u32[]{:S(2)}, u32[]{:S(2)}) %collective-permute-start.17) | collective-permute-done | bytes 229408 | tf_op jit(solution)/shard_map/ppermute | solution.py:225
  197.1 6.4 %collective-permute-done.18 = bf16[448,256]{1,0:T(8,128)(2,1)S(1)} collective-permute-done((bf16[448,256]{1,0:T(8,128)(2,1)S(1)}, bf16[448,256]{1,0:T(8,128)(2,1)S(1)}, u32[]{:S(2)}, u32[]{:S(2)}) %collective-permute-start.18) | collective-permute-done | bytes 229408 | tf_op jit(solution)/shard_map/ppermute | solution.py:225
  203.6 10.9 %all_to_all.11.refs_0_ = bf16[8,96,256]{2,1,0:T(8,128)(2,1)S(1)} all-to-all(bf16[8,96,256]{2,1,0:T(8,128)(2,1)S(1)} %pad_maximum_fusion.2), channel_id=1, replica_groups=mesh['ep'=8,'tp'=16] {'ep'}, dimensions={0} | all-to-all | bytes 786432 | tf_op jit(solution)/shard_map/all_to_all | solution.py:344
  (83 shorter events, 22.6 us)
Async XLA Ops:
  21.3 13.3 %collective-permute-start.8 = (bf16[768,256]{1,0:T(8,128)(2,1)S(1)}, bf16[768,256]{1,0:T(8,128)(2,1)S(1)}, u32[]{:S(2)}, u32[]{:S(2)}) collective-permute-start(bf16[768,256]{1,0:T(8,128)(2,1)S(1)} %bitcast.78), channel_id=1, source_target_pairs={{0,3},{1,0},{2,1},{3,2},{4,7},{5,4},{6,5},{7,6},{8,11},{9,8},{10,9... | collective-permute-start | bytes 1179656 | tf_op jit(solution)/shard_map/ppermute | solution.py:225
  22.8 17.7 %collective-permute-start.9 = (bf16[768,256]{1,0:T(8,128)(2,1)S(1)}, bf16[768,256]{1,0:T(8,128)(2,1)S(1)}, u32[]{:S(2)}, u32[]{:S(2)}) collective-permute-start(bf16[768,256]{1,0:T(8,128)(2,1)S(1)} %bitcast.79), channel_id=1, source_target_pairs={{0,2},{1,3},{2,0},{3,1},{4,6},{5,7},{6,4},{7,5},{8,10},{9,11},{10,... | collective-permute-start | bytes 1179656 | tf_op jit(solution)/shard_map/ppermute | solution.py:225
  24.4 20.1 %collective-permute-start = (bf16[768,256]{1,0:T(8,128)(2,1)S(1)}, bf16[768,256]{1,0:T(8,128)(2,1)S(1)}, u32[]{:S(2)}, u32[]{:S(2)}) collective-permute-start(bf16[768,256]{1,0:T(8,128)(2,1)S(1)} %bitcast.73), channel_id=1, source_target_pairs={{0,4},{1,5},{2,6},{3,7},{4,8},{5,9},{6,10},{7,11},{8,12},{9,13},{1... | collective-permute-start | bytes 1179656 | tf_op jit(solution)/shard_map/ppermute | solution.py:225
  26.0 18.5 %collective-permute-start.1 = (bf16[768,256]{1,0:T(8,128)(2,1)S(1)}, bf16[768,256]{1,0:T(8,128)(2,1)S(1)}, u32[]{:S(2)}, u32[]{:S(2)}) collective-permute-start(bf16[768,256]{1,0:T(8,128)(2,1)S(1)} %bitcast.74), channel_id=1, source_target_pairs={{0,12},{1,13},{2,14},{3,15},{4,0},{5,1},{6,2},{7,3},{8,4},{9,5},{1... | collective-permute-start | bytes 1179656 | tf_op jit(solution)/shard_map/ppermute | solution.py:225
  31.0 14.1 %collective-permute-start.2 = (bf16[768,256]{1,0:T(8,128)(2,1)S(1)}, bf16[768,256]{1,0:T(8,128)(2,1)S(1)}, u32[]{:S(2)}, u32[]{:S(2)}) collective-permute-start(bf16[768,256]{1,0:T(8,128)(2,1)S(1)} %bitcast.75), channel_id=1, source_target_pairs={{0,8},{1,9},{2,10},{3,11},{4,12},{5,13},{6,14},{7,15},{8,0},{9,1},... | collective-permute-start | bytes 1179656 | tf_op jit(solution)/shard_map/ppermute | solution.py:225
  40.6 40.1 %collective-permute-start.10 = (bf16[3072,256]{1,0:T(8,128)(2,1)S(1)}, bf16[3072,256]{1,0:T(8,128)(2,1)S(1)}, u32[]{:S(2)}, u32[]{:S(2)}) collective-permute-start(bf16[3072,256]{1,0:T(8,128)(2,1)S(1)} %pad_maximum_fusion.1), channel_id=1, source_target_pairs={{0,4},{1,5},{2,6},{3,7},{4,8},{5,9},{6,10},{7,11},{8,12},{9,13},{1... | collective-permute-start | bytes 4718600 | tf_op jit(solution)/shard_map/ppermute | solution.py:225
  42.3 39.4 %collective-permute-start.12 = (bf16[3072,256]{1,0:T(8,128)(2,1)S(1)}, bf16[3072,256]{1,0:T(8,128)(2,1)S(1)}, u32[]{:S(2)}, u32[]{:S(2)}) collective-permute-start(bf16[3072,256]{1,0:T(8,128)(2,1)S(1)} %pad_maximum_fusion.1), channel_id=1, source_target_pairs={{0,12},{1,13},{2,14},{3,15},{4,0},{5,1},{6,2},{7,3},{8,4},{9,5},{1... | collective-permute-start | bytes 4718600 | tf_op jit(solution)/shard_map/ppermute | solution.py:225
  45.2 40.3 %collective-permute-start.3 = (bf16[3072,256]{1,0:T(8,128)(2,1)S(1)}, bf16[3072,256]{1,0:T(8,128)(2,1)S(1)}, u32[]{:S(2)}, u32[]{:S(2)}) collective-permute-start(bf16[3072,256]{1,0:T(8,128)(2,1)S(1)} %pad_maximum_fusion), channel_id=1, source_target_pairs={{0,1},{1,2},{2,3},{3,0},{4,5},{5,6},{6,7},{7,4},{8,9},{9,10},{10,1... | collective-permute-start | bytes 4718600 | tf_op jit(solution)/shard_map/ppermute | solution.py:225
  45.7 40.9 %collective-permute-start.5 = (bf16[3072,256]{1,0:T(8,128)(2,1)S(1)}, bf16[3072,256]{1,0:T(8,128)(2,1)S(1)}, u32[]{:S(2)}, u32[]{:S(2)}) collective-permute-start(bf16[3072,256]{1,0:T(8,128)(2,1)S(1)} %pad_maximum_fusion), channel_id=1, source_target_pairs={{0,3},{1,0},{2,1},{3,2},{4,7},{5,4},{6,5},{7,6},{8,11},{9,8},{10,9... | collective-permute-start | bytes 4718600 | tf_op jit(solution)/shard_map/ppermute | solution.py:225
  81.8 33.0 %collective-permute-start.11 = (bf16[1536,256]{1,0:T(8,128)(2,1)}, bf16[1536,256]{1,0:T(8,128)(2,1)}, u32[]{:S(2)}, u32[]{:S(2)}) collective-permute-start(bf16[1536,256]{1,0:T(8,128)(2,1)} %slice.66), channel_id=1, source_target_pairs={{0,4},{1,5},{2,6},{3,7},{4,8},{5,9},{6,10},{7,11},{8,12},{9,13},{1... | collective-permute-start | bytes 2359304 | tf_op jit(solution)/shard_map/ppermute | solution.py:225
  82.8 32.0 %collective-permute-start.13 = (bf16[1536,256]{1,0:T(8,128)(2,1)}, bf16[1536,256]{1,0:T(8,128)(2,1)}, u32[]{:S(2)}, u32[]{:S(2)}) collective-permute-start(bf16[1536,256]{1,0:T(8,128)(2,1)} %slice.67), channel_id=1, source_target_pairs={{0,12},{1,13},{2,14},{3,15},{4,0},{5,1},{6,2},{7,3},{8,4},{9,5},{1... | collective-permute-start | bytes 2359304 | tf_op jit(solution)/shard_map/ppermute | solution.py:225
  86.5 28.2 %collective-permute-start.4 = (bf16[1536,256]{1,0:T(8,128)(2,1)}, bf16[1536,256]{1,0:T(8,128)(2,1)}, u32[]{:S(2)}, u32[]{:S(2)}) collective-permute-start(bf16[1536,256]{1,0:T(8,128)(2,1)} %slice.63), channel_id=1, source_target_pairs={{0,1},{1,2},{2,3},{3,0},{4,5},{5,6},{6,7},{7,4},{8,9},{9,10},{10,1... | collective-permute-start | bytes 2359304 | tf_op jit(solution)/shard_map/ppermute | solution.py:225
  87.6 27.1 %collective-permute-start.6 = (bf16[1536,256]{1,0:T(8,128)(2,1)}, bf16[1536,256]{1,0:T(8,128)(2,1)}, u32[]{:S(2)}, u32[]{:S(2)}) collective-permute-start(bf16[1536,256]{1,0:T(8,128)(2,1)} %slice.64), channel_id=1, source_target_pairs={{0,3},{1,0},{2,1},{3,2},{4,7},{5,4},{6,5},{7,6},{8,11},{9,8},{10,9... | collective-permute-start | bytes 2359304 | tf_op jit(solution)/shard_map/ppermute | solution.py:225
  141.5 16.0 %collective-permute-start.20 = (bf16[4,320,256]{2,1,0:T(8,128)(2,1)S(1)}, bf16[4,320,256]{2,1,0:T(8,128)(2,1)S(1)}, u32[]{:S(2)}, u32[]{:S(2)}) collective-permute-start(bf16[4,320,256]{2,1,0:T(8,128)(2,1)S(1)} %get-tuple-element.44), channel_id=1, source_target_pairs={{0,2},{1,3},{2,0},{3,1},{4,6},{5,7},{6,4},{7,5},{8,10},{9,11},{10,... | collective-permute-start | bytes 1966088 | tf_op jit(solution)/shard_map/ppermute | solution.py:225
  141.5 31.8 %collective-permute-start.21 = (bf16[4,320,256]{2,1,0:T(8,128)(2,1)S(1)}, bf16[4,320,256]{2,1,0:T(8,128)(2,1)S(1)}, u32[]{:S(2)}, u32[]{:S(2)}) collective-permute-start(bf16[4,320,256]{2,1,0:T(8,128)(2,1)S(1)} %get-tuple-element.45), channel_id=1, source_target_pairs={{0,1},{1,2},{2,3},{3,0},{4,5},{5,6},{6,7},{7,4},{8,9},{9,10},{10,1... | collective-permute-start | bytes 1966088 | tf_op jit(solution)/shard_map/ppermute | solution.py:225
  142.5 30.8 %collective-permute-start.22 = (bf16[4,320,256]{2,1,0:T(8,128)(2,1)S(1)}, bf16[4,320,256]{2,1,0:T(8,128)(2,1)S(1)}, u32[]{:S(2)}, u32[]{:S(2)}) collective-permute-start(bf16[4,320,256]{2,1,0:T(8,128)(2,1)S(1)} %get-tuple-element.46), channel_id=1, source_target_pairs={{0,3},{1,0},{2,1},{3,2},{4,7},{5,4},{6,5},{7,6},{8,11},{9,8},{10,9... | collective-permute-start | bytes 1966088 | tf_op jit(solution)/shard_map/ppermute | solution.py:225
  144.3 30.2 %collective-permute-start.14 = (bf16[4,448,256]{2,1,0:T(8,128)(2,1)S(1)}, bf16[4,448,256]{2,1,0:T(8,128)(2,1)S(1)}, u32[]{:S(2)}, u32[]{:S(2)}) collective-permute-start(bf16[4,448,256]{2,1,0:T(8,128)(2,1)S(1)} %get-tuple-element.39), channel_id=1, source_target_pairs={{0,8},{1,9},{2,10},{3,11},{4,12},{5,13},{6,14},{7,15},{8,0},{9,1},... | collective-permute-start | bytes 2752520 | tf_op jit(solution)/shard_map/ppermute | solution.py:225
  144.3 44.6 %collective-permute-start.15 = (bf16[4,448,256]{2,1,0:T(8,128)(2,1)S(1)}, bf16[4,448,256]{2,1,0:T(8,128)(2,1)S(1)}, u32[]{:S(2)}, u32[]{:S(2)}) collective-permute-start(bf16[4,448,256]{2,1,0:T(8,128)(2,1)S(1)} %get-tuple-element.40), channel_id=1, source_target_pairs={{0,4},{1,5},{2,6},{3,7},{4,8},{5,9},{6,10},{7,11},{8,12},{9,13},{1... | collective-permute-start | bytes 2752520 | tf_op jit(solution)/shard_map/ppermute | solution.py:225
  157.4 31.5 %collective-permute-start.16 = (bf16[4,448,256]{2,1,0:T(8,128)(2,1)S(1)}, bf16[4,448,256]{2,1,0:T(8,128)(2,1)S(1)}, u32[]{:S(2)}, u32[]{:S(2)}) collective-permute-start(bf16[4,448,256]{2,1,0:T(8,128)(2,1)S(1)} %get-tuple-element.41), channel_id=1, source_target_pairs={{0,12},{1,13},{2,14},{3,15},{4,0},{5,1},{6,2},{7,3},{8,4},{9,5},{1... | collective-permute-start | bytes 2752520 | tf_op jit(solution)/shard_map/ppermute | solution.py:225
  173.7 17.5 %collective-permute-start.23 = (bf16[320,256]{1,0:T(8,128)(2,1)S(1)}, bf16[320,256]{1,0:T(8,128)(2,1)S(1)}, u32[]{:S(2)}, u32[]{:S(2)}) collective-permute-start(bf16[320,256]{1,0:T(8,128)(2,1)S(1)} %get-tuple-element.56), channel_id=1, source_target_pairs={{0,8},{1,9},{2,10},{3,11},{4,12},{5,13},{6,14},{7,15},{8,0},{9,1},... | collective-permute-start | bytes 491528 | tf_op jit(solution)/shard_map/ppermute | solution.py:225
  173.8 20.3 %collective-permute-start.24 = (bf16[320,256]{1,0:T(8,128)(2,1)S(1)}, bf16[320,256]{1,0:T(8,128)(2,1)S(1)}, u32[]{:S(2)}, u32[]{:S(2)}) collective-permute-start(bf16[320,256]{1,0:T(8,128)(2,1)S(1)} %get-tuple-element.58), channel_id=1, source_target_pairs={{0,4},{1,5},{2,6},{3,7},{4,8},{5,9},{6,10},{7,11},{8,12},{9,13},{1... | collective-permute-start | bytes 491528 | tf_op jit(solution)/shard_map/ppermute | solution.py:225
  174.4 19.7 %collective-permute-start.25 = (bf16[320,256]{1,0:T(8,128)(2,1)S(1)}, bf16[320,256]{1,0:T(8,128)(2,1)S(1)}, u32[]{:S(2)}, u32[]{:S(2)}) collective-permute-start(bf16[320,256]{1,0:T(8,128)(2,1)S(1)} %get-tuple-element.57), channel_id=1, source_target_pairs={{0,12},{1,13},{2,14},{3,15},{4,0},{5,1},{6,2},{7,3},{8,4},{9,5},{1... | collective-permute-start | bytes 491528 | tf_op jit(solution)/shard_map/ppermute | solution.py:225
  191.2 12.3 %collective-permute-start.18 = (bf16[448,256]{1,0:T(8,128)(2,1)S(1)}, bf16[448,256]{1,0:T(8,128)(2,1)S(1)}, u32[]{:S(2)}, u32[]{:S(2)}) collective-permute-start(bf16[448,256]{1,0:T(8,128)(2,1)S(1)} %get-tuple-element.53), channel_id=1, source_target_pairs={{0,1},{1,2},{2,3},{3,0},{4,5},{5,6},{6,7},{7,4},{8,9},{9,10},{10,1... | collective-permute-start | bytes 688136 | tf_op jit(solution)/shard_map/ppermute | solution.py:225
  191.2 12.3 %collective-permute-start.19 = (bf16[448,256]{1,0:T(8,128)(2,1)S(1)}, bf16[448,256]{1,0:T(8,128)(2,1)S(1)}, u32[]{:S(2)}, u32[]{:S(2)}) collective-permute-start(bf16[448,256]{1,0:T(8,128)(2,1)S(1)} %get-tuple-element.52), channel_id=1, source_target_pairs={{0,3},{1,0},{2,1},{3,2},{4,7},{5,4},{6,5},{7,6},{8,11},{9,8},{10,9... | collective-permute-start | bytes 688136 | tf_op jit(solution)/shard_map/ppermute | solution.py:225
  (17 other events, 144.3 us)

commit v5 on v4

--- a/solution.py
+++ b/solution.py
@@ -95,7 +95,7 @@
 
 
 def absorb_body(x_order, g_order, *refs, first, count, ahead):
-    pieces, refs = (refs[:count], refs[count : 2 * count]), refs[2 * count :]
+    pieces, refs = (refs[:2], refs[2:4]), refs[4:]
     given = first > 0
     before, refs = (refs[:4], refs[4:]) if given else ((), refs)
     hbm, outs, refs = refs[:3], refs[3:7], refs[7:]
@@ -110,7 +110,7 @@
     for copy in following():
         copy.start()
     wide = SIDE * hbm[0].shape[1]
-    left = [jnp.concatenate([pieces[kind][0][f] for f in range(SIDE)], axis=1) for kind in range(2)]
+    left = [jnp.concatenate([p[i] for p in pieces[kind] for i in range(p.shape[0])], axis=1) for kind in range(2)]
     if not given:
         for f in range(SIDE):
             for copy in for_acts(f):
@@ -225,20 +225,14 @@
     return lax.ppermute(x, "tp", shift(by))
 
 
-def ring_gather(x, shift):
-    half = x.shape[0] // 2
-    below = shifted(x, shift, 1)
-    above = shifted(x, shift, 3)
-    far_low = shifted(below[:half], shift, 1)
-    far_high = shifted(above[half:], shift, 3)
-    return [x, below, above, far_low, far_high]
-
-
 def plane_gather(x, first, second):
     rows, width = x.shape
-    far, below, above = [shifted(x, first, by) for by in (2, 1, 3)]
-    line = jnp.concatenate([x, below, above, far], axis=0)
-    return [piece.reshape(-1, rows, width) for piece in ring_gather(line, second)]
+    below, above, far = [shifted(x, first, by) for by in (1, 3, 2)]
+    halves = [jnp.concatenate([x, below], axis=0), jnp.concatenate([above, far], axis=0)]
+    behind = [shifted(half, second, 1) for half in halves]
+    ahead = [shifted(half, second, 3) for half in halves]
+    away = [shifted(behind[0], second, 1), shifted(ahead[1], second, 3)]
+    return [[half.reshape(2, rows, width) for half in ring] for ring in (halves, behind, ahead, away)]
 
 
 def ring_sum(far, ahead, behind, own, shift):
@@ -290,8 +284,8 @@
     downs_of = lambda count: pltpu.VMEM((count, units, SIDE * width), BF)
     blocks = in_hbm(gate_matrix.reshape(TP, width, units), up_matrix.reshape(TP, width, units), down_matrix)
     state = []
-    for first, count, ahead, limit in ((0, 1, 1, 14), (1, 1, 1, 18), (2, 1, 1, 18)):
-        used = [*x[first : first + count], *g[first : first + count], *state]
+    for first, count, ahead, limit in ((0, 1, 1, 14), (1, 1, 1, 16), (2, 1, 1, 16)):
+        used = [*x[first], *g[first], *state]
         own = []
         if first == 0:
             own = [sides_of(count), downs_of(count), dma((2, count * SIDE)), dma((count, SIDE))]
@@ -325,7 +319,7 @@
                 scratch_shapes=[pltpu.VMEM((experts, part, 2 * units), BF), sides_of(SIDE), dma((2, TP))],
                 name="finish",
                 compiler_params=vmem(29),
-            )(summed_order[h], *x[3:], *g[3:], *state, *blocks[:2])
+            )(summed_order[h], *x[3], *g[3], *state, *blocks[:2])
         else:
             outs = pl.pallas_call(
                 parts_body,

time: 216 us -> 227 us (1.051)
  waiting for transfers between devices: 92 us -> 101 us
  Pallas kernels: 53.7 us -> 56 us
    ppermute x26 -> x30, waiting for transfers between devices: 92 us -> 101 us  [shifted(): return lax.ppermute(x, 'tp', shift(by))]
    slice x4 -> x0, local copies, waits for them, and re-layouts: 4.11 us -> none  [the longest x2 2.06 us: ring_gather(): far_low = shifted(below[:half], shift, 1)]
    unnamed x30 -> x28, local copies, waits for them, and re-layouts: 0.73 us -> 3.59 us
    ppermute x26 -> x30, starting transfers between devices: 34.9 us -> 34.6 us  [shifted(): return lax.ppermute(x, 'tp', shift(by))]
  transfers between devices with their start and end apart: 26 -> 30, of which waited for: 10 -> 11; matrix products, arithmetic and copies ran while one was open for 2% -> 1% of each run, Pallas kernels for 11% -> 12%
where the time goes in v5:
time: 227 us
  waiting for transfers between devices  101 us (44%)
  Pallas kernels  56 us (25%)
  starting transfers between devices  34.6 us (15%)
  blocking collectives  29.6 us (13%)
  local copies, waits for them, and re-layouts  3.77 us (2%)
    ppermute x30, waiting for transfers between devices, shifted(): return lax.ppermute(x, 'tp', shift(by))  101 us
    ppermute x30, starting transfers between devices, shifted(): return lax.ppermute(x, 'tp', shift(by))  34.6 us
    pallas_call x3, Pallas kernels, body(): pl.pallas_call(functools.partial(absorb_body, first=first, count=count, a...  26.5 us
    all_to_all x1, blocking collectives, body(): got = lax.all_to_all(sent, 'ep', split_axis=0, concat_axis=0, tiled=True)  17.7 us
    pallas_call x1, Pallas kernels, body(): pl.pallas_call(finish_body, in_specs=[in_smem] + [in_vmem] * 8 + [stays]...  17.7 us
    all_to_all x1, blocking collectives, body(): lax.all_to_all(jnp.concatenate(summed, axis=1), 'ep', split_axis=0, conca...  11.9 us
    pallas_call x1, Pallas kernels, body(): pl.pallas_call(parts_body, in_specs=[in_smem, in_vmem] + [stays] * 2, out...  8.97 us
  transfers between devices with their start and end apart: 30, of which 11 were waited for; matrix products, arithmetic and copies ran while one was open for 1% of the time, Pallas kernels for 12%

profile of v5, /device:TPU:1, one launch (start us, length us, event | category | flops | bytes accessed | tf_op | source)
XLA Modules:
  0.0 226.8 jit_solution(6604411360172332953)
XLA Ops:
  2.2 17.7 %all_to_all.10 = bf16[8,192,256]{2,1,0:T(8,128)(2,1)S(1)} all-to-all(bf16[8,192,256]{2,1,0:T(8,128)(2,1)S(1)} %dispatch.1), channel_id=1, replica_groups=mesh['ep'=8,'tp'=16] {'ep'}, dimensions={0} | all-to-all | bytes 1572864 | tf_op jit(solution)/shard_map/all_to_all | solution.py:275
  23.0 2.1 collective-permute-start.3
  25.1 5.9 %collective-permute-done.7 = bf16[768,256]{1,0:T(8,128)(2,1)S(1)} collective-permute-done((bf16[768,256]{1,0:T(8,128)(2,1)S(1)}, bf16[768,256]{1,0:T(8,128)(2,1)S(1)}, u32[]{:S(2)}, u32[]{:S(2)}) %collective-permute-start.7) | collective-permute-done | bytes 393248 | tf_op jit(solution)/shard_map/ppermute | solution.py:225
  31.0 1.7 collective-permute-start.8
  36.3 2.6 %collective-permute-start.10 = (bf16[768,256]{1,0:T(8,128)(2,1)S(1)}, bf16[768,256]{1,0:T(8,128)(2,1)S(1)}, u32[]{:S(2)}, u32[]{:S(2)}) collective-permute-start(bf16[768,256]{1,0:T(8,128)(2,1)S(1)} %bitcast.82), channel_id=1, source_target_pairs={{0,3},{1,0},{2,1},{3,2},{4,7},{5,4},{6,5},{7,6},{8,11},{9,8},{10,9... | collective-permute-start | bytes 1179656 | tf_op jit(solution)/shard_map/ppermute | solution.py:225
  39.3 21.0 %collective-permute-done.4 = bf16[768,256]{1,0:T(8,128)(2,1)S(1)} collective-permute-done((bf16[768,256]{1,0:T(8,128)(2,1)S(1)}, bf16[768,256]{1,0:T(8,128)(2,1)S(1)}, u32[]{:S(2)}, u32[]{:S(2)}) %collective-permute-start.4) | collective-permute-done | bytes 393248 | tf_op jit(solution)/shard_map/ppermute | solution.py:225
  60.4 2.7 %collective-permute-start.5 = (bf16[1536,256]{1,0:T(8,128)(2,1)S(1)}, bf16[1536,256]{1,0:T(8,128)(2,1)}, u32[]{:S(2)}, u32[]{:S(2)}) collective-permute-start(bf16[1536,256]{1,0:T(8,128)(2,1)S(1)} %constant_dynamic-update-slice_fusion), channel_id=1, source_target_pairs={{0,3},{1,0},{2,1},{3,2},{4,7},{5,4},{6,5},{7,6},{8,11},{9,8},{10,9... | collective-permute-start | bytes 2359304 | tf_op jit(solution)/shard_map/ppermute | solution.py:225
  66.0 12.0 %collective-permute-done.16 = bf16[1536,256]{1,0:T(8,128)(2,1)S(1)} collective-permute-done((bf16[1536,256]{1,0:T(8,128)(2,1)S(1)}, bf16[1536,256]{1,0:T(8,128)(2,1)S(1)}, u32[]{:S(2)}, u32[]{:S(2)}) %collective-permute-start.16) | collective-permute-done | bytes 786464 | tf_op jit(solution)/shard_map/ppermute | solution.py:225
  82.9 13.1 %collective-permute-done.15 = bf16[1536,256]{1,0:T(8,128)(2,1)S(1)} collective-permute-done((bf16[1536,256]{1,0:T(8,128)(2,1)S(1)}, bf16[1536,256]{1,0:T(8,128)(2,1)S(1)}, u32[]{:S(2)}, u32[]{:S(2)}) %collective-permute-start.15) | collective-permute-done | bytes 786464 | tf_op jit(solution)/shard_map/ppermute | solution.py:225
  97.0 9.4 %absorb.3 = (f32[768,1792]{1,0:T(8,128)S(1)}, f32[768,896]{1,0:T(8,128)S(1)}, bf16[4,256,1792]{2,1,0:T(8,128)(2,1)S(1)}, bf16[1,896,1024]{2,1,0:T(8,128)(2,1)S(1)}) custom-call(s32[16]{0:T(128)S(1)} %get-tuple-element.60.x_order, s32[16]{0:T(128)S(1)} %get-tuple-element.59.g_order, bf16[2,768,256]{2,1,0:T(8,128)(2,1)S(1)} %bitcast.57, ...), custom_call_target="tpu_custom_call" | custom-call | tf_op jit(solution)/shard_map/absorb/pallas_call | solution.py:292
  106.4 8.5 %absorb.4 = (f32[768,1792]{1,0:T(8,128)S(1)}, f32[768,896]{1,0:T(8,128)S(1)}, bf16[4,256,1792]{2,1,0:T(8,128)(2,1)S(1)}, bf16[1,896,1024]{2,1,0:T(8,128)(2,1)S(1)}) custom-call(s32[16]{0:T(128)S(1)} %get-tuple-element.60.x_order, s32[16]{0:T(128)S(1)} %get-tuple-element.59.g_order, bf16[2,768,256]{2,1,0:T(8,128)(2,1)} %bitcast.12.refs_0_, ...), custom_call_target="tpu_custom_call" | custom-call | tf_op jit(solution)/shard_map/absorb/pallas_call | solution.py:292
  115.0 8.6 %absorb.5 = (f32[768,1792]{1,0:T(8,128)S(1)}, f32[768,896]{1,0:T(8,128)S(1)}, bf16[4,256,1792]{2,1,0:T(8,128)(2,1)S(1)}, bf16[1,896,1024]{2,1,0:T(8,128)(2,1)S(1)}) custom-call(s32[16]{0:T(128)S(1)} %get-tuple-element.60.x_order, s32[16]{0:T(128)S(1)} %get-tuple-element.59.g_order, bf16[2,768,256]{2,1,0:T(8,128)(2,1)} %bitcast.8.refs_0_, ...), custom_call_target="tpu_custom_call" | custom-call | tf_op jit(solution)/shard_map/absorb/pallas_call | solution.py:292
  123.6 17.7 %finish.1 = (bf16[4,448,256]{2,1,0:T(8,128)(2,1)S(1)}, bf16[4,448,256]{2,1,0:T(8,128)(2,1)S(1)}, bf16[4,448,256]{2,1,0:T(8,128)(2,1)S(1)}, bf16[4,448,256]{2,1,0:T(8,128)(2,1)S(1)}, bf16[8,40,1792]{2,1,0:T(8,128)(2,1)S(1)}) custom-call(s32[16]{0:T(128)S(1)} %get-tuple-element.61.order, bf16[2,768,256]{2,1,0:T(8,128)(2,1)} %bitcast.3.refs_0_, ...), custom_call_target="tpu_custom_call" | custom-call | tf_op jit(solution)/shard_map/finish/pallas_call | solution.py:314
  141.3 9.0 %parts.1 = (bf16[4,320,256]{2,1,0:T(8,128)(2,1)S(1)}, bf16[4,320,256]{2,1,0:T(8,128)(2,1)S(1)}, bf16[4,320,256]{2,1,0:T(8,128)(2,1)S(1)}, bf16[4,320,256]{2,1,0:T(8,128)(2,1)S(1)}) custom-call(s32[16]{0:T(128)S(1)} %get-tuple-element.62.order, bf16[8,40,1792]{2,1,0:T(8,128)(2,1)S(1)} %get-tuple-element.42.grads, bf16[16,256,896]{2,1,0:T(8,128)(2,1)} %bitcast.71, ...), custom_call_target="tpu_custom_call" | custom-call | tf_op jit(solution)/shard_map/parts/pallas_call | solution.py:324
  151.6 2.0 collective-permute-start.25
  154.3 2.1 collective-permute-start.19
  156.4 5.1 %collective-permute-done.24 = bf16[4,320,256]{2,1,0:T(8,128)(2,1)S(1)} collective-permute-done((bf16[4,320,256]{2,1,0:T(8,128)(2,1)S(1)}, bf16[4,320,256]{2,1,0:T(8,128)(2,1)S(1)}, u32[]{:S(2)}, u32[]{:S(2)}) %collective-permute-start.24) | collective-permute-done | bytes 655392 | tf_op jit(solution)/shard_map/ppermute | solution.py:225
  161.9 18.8 %collective-permute-done.25 = bf16[4,320,256]{2,1,0:T(8,128)(2,1)S(1)} collective-permute-done((bf16[4,320,256]{2,1,0:T(8,128)(2,1)S(1)}, bf16[4,320,256]{2,1,0:T(8,128)(2,1)S(1)}, u32[]{:S(2)}, u32[]{:S(2)}) %collective-permute-start.25) | collective-permute-done | bytes 655392 | tf_op jit(solution)/shard_map/ppermute | solution.py:225
  181.4 2.7 %collective-permute-start.29 = (bf16[320,256]{1,0:T(8,128)(2,1)S(1)}, bf16[320,256]{1,0:T(8,128)(2,1)S(1)}, u32[]{:S(2)}, u32[]{:S(2)}) collective-permute-start(bf16[320,256]{1,0:T(8,128)(2,1)S(1)} %get-tuple-element.57), channel_id=1, source_target_pairs={{0,12},{1,13},{2,14},{3,15},{4,0},{5,1},{6,2},{7,3},{8,4},{9,5},{1... | collective-permute-start | bytes 491528 | tf_op jit(solution)/shard_map/ppermute | solution.py:225
  184.0 14.9 %collective-permute-done.19 = bf16[4,448,256]{2,1,0:T(8,128)(2,1)S(1)} collective-permute-done((bf16[4,448,256]{2,1,0:T(8,128)(2,1)S(1)}, bf16[4,448,256]{2,1,0:T(8,128)(2,1)S(1)}, u32[]{:S(2)}, u32[]{:S(2)}) %collective-permute-start.19) | collective-permute-done | bytes 917536 | tf_op jit(solution)/shard_map/ppermute | solution.py:225
  200.7 2.7 %collective-permute-start.23 = (bf16[448,256]{1,0:T(8,128)(2,1)S(1)}, bf16[448,256]{1,0:T(8,128)(2,1)S(1)}, u32[]{:S(2)}, u32[]{:S(2)}) collective-permute-start(bf16[448,256]{1,0:T(8,128)(2,1)S(1)} %get-tuple-element.52), channel_id=1, source_target_pairs={{0,3},{1,0},{2,1},{3,2},{4,7},{5,4},{6,5},{7,6},{8,11},{9,8},{10,9... | collective-permute-start | bytes 688136 | tf_op jit(solution)/shard_map/ppermute | solution.py:225
  204.3 2.0 collective-permute-done.21
  206.3 7.2 %collective-permute-done.22 = bf16[448,256]{1,0:T(8,128)(2,1)S(1)} collective-permute-done((bf16[448,256]{1,0:T(8,128)(2,1)S(1)}, bf16[448,256]{1,0:T(8,128)(2,1)S(1)}, u32[]{:S(2)}, u32[]{:S(2)}) %collective-permute-start.22) | collective-permute-done | bytes 229408 | tf_op jit(solution)/shard_map/ppermute | solution.py:225
  213.6 11.9 %all_to_all.11.refs_0_ = bf16[8,96,256]{2,1,0:T(8,128)(2,1)S(1)} all-to-all(bf16[8,96,256]{2,1,0:T(8,128)(2,1)S(1)} %pad_maximum_fusion.2), channel_id=1, replica_groups=mesh['ep'=8,'tp'=16] {'ep'}, dimensions={0} | all-to-all | bytes 786432 | tf_op jit(solution)/shard_map/all_to_all | solution.py:338
  (87 shorter events, 25.2 us)
Async XLA Ops:
  23.0 16.0 %collective-permute-start.3 = (bf16[768,256]{1,0:T(8,128)(2,1)S(1)}, bf16[768,256]{1,0:T(8,128)(2,1)S(1)}, u32[]{:S(2)}, u32[]{:S(2)}) collective-permute-start(bf16[768,256]{1,0:T(8,128)(2,1)S(1)} %bitcast.85), channel_id=1, source_target_pairs={{0,12},{1,13},{2,14},{3,15},{4,0},{5,1},{6,2},{7,3},{8,4},{9,5},{1... | collective-permute-start | bytes 1179656 | tf_op jit(solution)/shard_map/ppermute | solution.py:225
  31.0 32.2 %collective-permute-start.8 = (bf16[1536,256]{1,0:T(8,128)(2,1)S(1)}, bf16[1536,256]{1,0:T(8,128)(2,1)}, u32[]{:S(2)}, u32[]{:S(2)}) collective-permute-start(bf16[1536,256]{1,0:T(8,128)(2,1)S(1)} %pad_maximum_fusion.1), channel_id=1, source_target_pairs={{0,4},{1,5},{2,6},{3,7},{4,8},{5,9},{6,10},{7,11},{8,12},{9,13},{1... | collective-permute-start | bytes 2359304 | tf_op jit(solution)/shard_map/ppermute | solution.py:225
  33.4 31.3 %collective-permute-start.1 = (bf16[1536,256]{1,0:T(8,128)(2,1)S(1)}, bf16[1536,256]{1,0:T(8,128)(2,1)}, u32[]{:S(2)}, u32[]{:S(2)}) collective-permute-start(bf16[1536,256]{1,0:T(8,128)(2,1)S(1)} %pad_maximum_fusion), channel_id=1, source_target_pairs={{0,1},{1,2},{2,3},{3,0},{4,5},{5,6},{6,7},{7,4},{8,9},{9,10},{10,1... | collective-permute-start | bytes 2359304 | tf_op jit(solution)/shard_map/ppermute | solution.py:225
  34.7 25.6 %collective-permute-start.4 = (bf16[768,256]{1,0:T(8,128)(2,1)S(1)}, bf16[768,256]{1,0:T(8,128)(2,1)S(1)}, u32[]{:S(2)}, u32[]{:S(2)}) collective-permute-start(bf16[768,256]{1,0:T(8,128)(2,1)S(1)} %bitcast.87), channel_id=1, source_target_pairs={{0,8},{1,9},{2,10},{3,11},{4,12},{5,13},{6,14},{7,15},{8,0},{9,1},... | collective-permute-start | bytes 1179656 | tf_op jit(solution)/shard_map/ppermute | solution.py:225
  36.3 24.1 %collective-permute-start.10 = (bf16[768,256]{1,0:T(8,128)(2,1)S(1)}, bf16[768,256]{1,0:T(8,128)(2,1)S(1)}, u32[]{:S(2)}, u32[]{:S(2)}) collective-permute-start(bf16[768,256]{1,0:T(8,128)(2,1)S(1)} %bitcast.82), channel_id=1, source_target_pairs={{0,3},{1,0},{2,1},{3,2},{4,7},{5,4},{6,5},{7,6},{8,11},{9,8},{10,9... | collective-permute-start | bytes 1179656 | tf_op jit(solution)/shard_map/ppermute | solution.py:225
  38.9 24.2 %collective-permute-start.11 = (bf16[768,256]{1,0:T(8,128)(2,1)S(1)}, bf16[768,256]{1,0:T(8,128)(2,1)S(1)}, u32[]{:S(2)}, u32[]{:S(2)}) collective-permute-start(bf16[768,256]{1,0:T(8,128)(2,1)S(1)} %bitcast.83), channel_id=1, source_target_pairs={{0,2},{1,3},{2,0},{3,1},{4,6},{5,7},{6,4},{7,5},{8,10},{9,11},{10,... | collective-permute-start | bytes 1179656 | tf_op jit(solution)/shard_map/ppermute | solution.py:225
  60.3 17.7 %collective-permute-start.16 = (bf16[1536,256]{1,0:T(8,128)(2,1)S(1)}, bf16[1536,256]{1,0:T(8,128)(2,1)S(1)}, u32[]{:S(2)}, u32[]{:S(2)}) collective-permute-start(bf16[1536,256]{1,0:T(8,128)(2,1)S(1)} %constant_dynamic-update-slice_fusion), channel_id=1, source_target_pairs={{0,1},{1,2},{2,3},{3,0},{4,5},{5,6},{6,7},{7,4},{8,9},{9,10},{10,1... | collective-permute-start | bytes 2359304 | tf_op jit(solution)/shard_map/ppermute | solution.py:225
  60.4 18.7 %collective-permute-start.5 = (bf16[1536,256]{1,0:T(8,128)(2,1)S(1)}, bf16[1536,256]{1,0:T(8,128)(2,1)}, u32[]{:S(2)}, u32[]{:S(2)}) collective-permute-start(bf16[1536,256]{1,0:T(8,128)(2,1)S(1)} %constant_dynamic-update-slice_fusion), channel_id=1, source_target_pairs={{0,3},{1,0},{2,1},{3,2},{4,7},{5,4},{6,5},{7,6},{8,11},{9,8},{10,9... | collective-permute-start | bytes 2359304 | tf_op jit(solution)/shard_map/ppermute | solution.py:225
  63.1 17.4 %collective-permute-start.12 = (bf16[1536,256]{1,0:T(8,128)(2,1)S(1)}, bf16[1536,256]{1,0:T(8,128)(2,1)}, u32[]{:S(2)}, u32[]{:S(2)}) collective-permute-start(bf16[1536,256]{1,0:T(8,128)(2,1)S(1)} %constant_dynamic-update-slice_fusion.2), channel_id=1, source_target_pairs={{0,12},{1,13},{2,14},{3,15},{4,0},{5,1},{6,2},{7,3},{8,4},{9,5},{1... | collective-permute-start | bytes 2359304 | tf_op jit(solution)/shard_map/ppermute | solution.py:225
  63.2 17.6 %collective-permute-start.17 = (bf16[1536,256]{1,0:T(8,128)(2,1)S(1)}, bf16[1536,256]{1,0:T(8,128)(2,1)S(1)}, u32[]{:S(2)}, u32[]{:S(2)}) collective-permute-start(bf16[1536,256]{1,0:T(8,128)(2,1)S(1)} %constant_dynamic-update-slice_fusion.2), channel_id=1, source_target_pairs={{0,4},{1,5},{2,6},{3,7},{4,8},{5,9},{6,10},{7,11},{8,12},{9,13},{1... | collective-permute-start | bytes 2359304 | tf_op jit(solution)/shard_map/ppermute | solution.py:225
  64.7 31.3 %collective-permute-start.15 = (bf16[1536,256]{1,0:T(8,128)(2,1)S(1)}, bf16[1536,256]{1,0:T(8,128)(2,1)S(1)}, u32[]{:S(2)}, u32[]{:S(2)}) collective-permute-start(bf16[1536,256]{1,0:T(8,128)(2,1)S(1)} %pad_maximum_fusion.1), channel_id=1, source_target_pairs={{0,12},{1,13},{2,14},{3,15},{4,0},{5,1},{6,2},{7,3},{8,4},{9,5},{1... | collective-permute-start | bytes 2359304 | tf_op jit(solution)/shard_map/ppermute | solution.py:225
  79.0 36.0 %collective-permute-start.14 = (bf16[1536,256]{1,0:T(8,128)(2,1)S(1)}, bf16[1536,256]{1,0:T(8,128)(2,1)}, u32[]{:S(2)}, u32[]{:S(2)}) collective-permute-start(bf16[1536,256]{1,0:T(8,128)(2,1)S(1)} %pad_maximum_fusion), channel_id=1, source_target_pairs={{0,3},{1,0},{2,1},{3,2},{4,7},{5,4},{6,5},{7,6},{8,11},{9,8},{10,9... | collective-permute-start | bytes 2359304 | tf_op jit(solution)/shard_map/ppermute | solution.py:225
  79.1 44.5 %collective-permute-start.6 = (bf16[1536,256]{1,0:T(8,128)(2,1)}, bf16[1536,256]{1,0:T(8,128)(2,1)}, u32[]{:S(2)}, u32[]{:S(2)}) collective-permute-start(bf16[1536,256]{1,0:T(8,128)(2,1)} %collective-permute-done.5), channel_id=1, source_target_pairs={{0,3},{1,0},{2,1},{3,2},{4,7},{5,4},{6,5},{7,6},{8,11},{9,8},{10,9... | collective-permute-start | bytes 2359304 | tf_op jit(solution)/shard_map/ppermute | solution.py:225
  80.5 43.1 %collective-permute-start.13 = (bf16[1536,256]{1,0:T(8,128)(2,1)}, bf16[1536,256]{1,0:T(8,128)(2,1)}, u32[]{:S(2)}, u32[]{:S(2)}) collective-permute-start(bf16[1536,256]{1,0:T(8,128)(2,1)} %collective-permute-done.12), channel_id=1, source_target_pairs={{0,12},{1,13},{2,14},{3,15},{4,0},{5,1},{6,2},{7,3},{8,4},{9,5},{1... | collective-permute-start | bytes 2359304 | tf_op jit(solution)/shard_map/ppermute | solution.py:225
  81.8 41.9 %collective-permute-start.9 = (bf16[1536,256]{1,0:T(8,128)(2,1)}, bf16[1536,256]{1,0:T(8,128)(2,1)}, u32[]{:S(2)}, u32[]{:S(2)}) collective-permute-start(bf16[1536,256]{1,0:T(8,128)(2,1)} %collective-permute-done.8), channel_id=1, source_target_pairs={{0,4},{1,5},{2,6},{3,7},{4,8},{5,9},{6,10},{7,11},{8,12},{9,13},{1... | collective-permute-start | bytes 2359304 | tf_op jit(solution)/shard_map/ppermute | solution.py:225
  96.9 26.7 %collective-permute-start.2 = (bf16[1536,256]{1,0:T(8,128)(2,1)}, bf16[1536,256]{1,0:T(8,128)(2,1)}, u32[]{:S(2)}, u32[]{:S(2)}) collective-permute-start(bf16[1536,256]{1,0:T(8,128)(2,1)} %collective-permute-done.1), channel_id=1, source_target_pairs={{0,1},{1,2},{2,3},{3,0},{4,5},{5,6},{6,7},{7,4},{8,9},{9,10},{10,1... | collective-permute-start | bytes 2359304 | tf_op jit(solution)/shard_map/ppermute | solution.py:225
  151.6 29.1 %collective-permute-start.25 = (bf16[4,320,256]{2,1,0:T(8,128)(2,1)S(1)}, bf16[4,320,256]{2,1,0:T(8,128)(2,1)S(1)}, u32[]{:S(2)}, u32[]{:S(2)}) collective-permute-start(bf16[4,320,256]{2,1,0:T(8,128)(2,1)S(1)} %get-tuple-element.45), channel_id=1, source_target_pairs={{0,1},{1,2},{2,3},{3,0},{4,5},{5,6},{6,7},{7,4},{8,9},{9,10},{10,1... | collective-permute-start | bytes 1966088 | tf_op jit(solution)/shard_map/ppermute | solution.py:225
  153.6 27.1 %collective-permute-start.26 = (bf16[4,320,256]{2,1,0:T(8,128)(2,1)S(1)}, bf16[4,320,256]{2,1,0:T(8,128)(2,1)S(1)}, u32[]{:S(2)}, u32[]{:S(2)}) collective-permute-start(bf16[4,320,256]{2,1,0:T(8,128)(2,1)S(1)} %get-tuple-element.46), channel_id=1, source_target_pairs={{0,3},{1,0},{2,1},{3,2},{4,7},{5,4},{6,5},{7,6},{8,11},{9,8},{10,9... | collective-permute-start | bytes 1966088 | tf_op jit(solution)/shard_map/ppermute | solution.py:225
  154.3 27.0 %collective-permute-start.18 = (bf16[4,448,256]{2,1,0:T(8,128)(2,1)S(1)}, bf16[4,448,256]{2,1,0:T(8,128)(2,1)S(1)}, u32[]{:S(2)}, u32[]{:S(2)}) collective-permute-start(bf16[4,448,256]{2,1,0:T(8,128)(2,1)S(1)} %get-tuple-element.39), channel_id=1, source_target_pairs={{0,8},{1,9},{2,10},{3,11},{4,12},{5,13},{6,14},{7,15},{8,0},{9,1},... | collective-permute-start | bytes 2752520 | tf_op jit(solution)/shard_map/ppermute | solution.py:225
  154.3 44.6 %collective-permute-start.19 = (bf16[4,448,256]{2,1,0:T(8,128)(2,1)S(1)}, bf16[4,448,256]{2,1,0:T(8,128)(2,1)S(1)}, u32[]{:S(2)}, u32[]{:S(2)}) collective-permute-start(bf16[4,448,256]{2,1,0:T(8,128)(2,1)S(1)} %get-tuple-element.40), channel_id=1, source_target_pairs={{0,4},{1,5},{2,6},{3,7},{4,8},{5,9},{6,10},{7,11},{8,12},{9,13},{1... | collective-permute-start | bytes 2752520 | tf_op jit(solution)/shard_map/ppermute | solution.py:225
  161.4 37.5 %collective-permute-start.20 = (bf16[4,448,256]{2,1,0:T(8,128)(2,1)S(1)}, bf16[4,448,256]{2,1,0:T(8,128)(2,1)S(1)}, u32[]{:S(2)}, u32[]{:S(2)}) collective-permute-start(bf16[4,448,256]{2,1,0:T(8,128)(2,1)S(1)} %get-tuple-element.41), channel_id=1, source_target_pairs={{0,12},{1,13},{2,14},{3,15},{4,0},{5,1},{6,2},{7,3},{8,4},{9,5},{1... | collective-permute-start | bytes 2752520 | tf_op jit(solution)/shard_map/ppermute | solution.py:225
  181.2 19.5 %collective-permute-start.27 = (bf16[320,256]{1,0:T(8,128)(2,1)S(1)}, bf16[320,256]{1,0:T(8,128)(2,1)S(1)}, u32[]{:S(2)}, u32[]{:S(2)}) collective-permute-start(bf16[320,256]{1,0:T(8,128)(2,1)S(1)} %get-tuple-element.56), channel_id=1, source_target_pairs={{0,8},{1,9},{2,10},{3,11},{4,12},{5,13},{6,14},{7,15},{8,0},{9,1},... | collective-permute-start | bytes 491528 | tf_op jit(solution)/shard_map/ppermute | solution.py:225
  181.3 22.9 %collective-permute-start.28 = (bf16[320,256]{1,0:T(8,128)(2,1)S(1)}, bf16[320,256]{1,0:T(8,128)(2,1)S(1)}, u32[]{:S(2)}, u32[]{:S(2)}) collective-permute-start(bf16[320,256]{1,0:T(8,128)(2,1)S(1)} %get-tuple-element.58), channel_id=1, source_target_pairs={{0,4},{1,5},{2,6},{3,7},{4,8},{5,9},{6,10},{7,11},{8,12},{9,13},{1... | collective-permute-start | bytes 491528 | tf_op jit(solution)/shard_map/ppermute | solution.py:225
  181.4 22.8 %collective-permute-start.29 = (bf16[320,256]{1,0:T(8,128)(2,1)S(1)}, bf16[320,256]{1,0:T(8,128)(2,1)S(1)}, u32[]{:S(2)}, u32[]{:S(2)}) collective-permute-start(bf16[320,256]{1,0:T(8,128)(2,1)S(1)} %get-tuple-element.57), channel_id=1, source_target_pairs={{0,12},{1,13},{2,14},{3,15},{4,0},{5,1},{6,2},{7,3},{8,4},{9,5},{1... | collective-permute-start | bytes 491528 | tf_op jit(solution)/shard_map/ppermute | solution.py:225
  (19 other events, 394.4 us)
